TPU v7x, 256 devices: a whole 4x4x8 slice. The times are simulated.
256 devices in a mesh: grp: 32 (over y, z_lo, core), dev: 8 (over x, z_hi).
Axes of the slice: x: 4, y: 4, z: 8 (z_hi: 2, z_lo: 4; z = z_hi * 4 + z_lo), core: 2. Of those that a mesh axis runs over, the one named last changes fastest.
Arguments:
- stack: bfloat16 [608, 256, 2048], P('grp', None, 'dev'), may hold values from -12 to 12
- network: int32 [608, 2], replicated, may hold values from 0 to 149, as said below
- bands: int32 [149], replicated, may hold values from 1 to 8
Outputs:
- deramped: bfloat16 [149, 256, 2048], P(None, 'grp', 'dev')
- misfit: float32 [256, 2048], P('grp', 'dev')
- spectrum: float32 [2, 149, 15, 15], replicated
Inputs may be any that keep to these rules, and one draw needn't show every extreme that they name: `network`: each row holds a reference date and a later secondary date, both below 150; every pair of consecutive dates is some row.
All inputs are finite; a program needn't handle non-finite values.
Results may differ from a plain program's by a relative error of at most 0.005.
Values may be sent and summed in bfloat16 or wider, within the bound.
No kernel may reach another device: no remote copies, remote signals or barrier semaphores. Data moves between devices by JAX's collectives and lax.ppermute only.
A program may use at most 128 MiB of HBM per device.

v0:
```python
import math

import jax
import jax.numpy as jnp
from jax import lax
from jax.sharding import PartitionSpec as P

BAND = 8


def from_everyone(shard, axis):
    peers = lax.axis_size(axis)
    return lax.all_to_all(
        jnp.broadcast_to(shard[None], (peers, *shard.shape)), axis, 0, 0, tiled=True
    )


def taken_together(shard, axis):
    everything = from_everyone(shard, axis)
    return jnp.sum(everything.astype(jnp.float32), axis=0)


def side_by_side(arrays, axis, dim, along):
    widths = [a.shape[along] for a in arrays]
    both = jnp.concatenate(arrays, axis=along)
    filled = lax.all_gather(both, axis, axis=dim, tiled=True)
    return tuple(jnp.split(filled, [sum(widths[:k]) for k in range(1, len(widths))], axis=along))


def build_inverse(network, solved):
    dates = jnp.arange(1, solved + 1, dtype=jnp.int32)
    design = (network[:, 1:2] == dates[None, :]).astype(jnp.float32) - (
        network[:, 0:1] == dates[None, :]
    ).astype(jnp.float32)
    normal = jnp.dot(design.T, design, precision=lax.Precision.HIGHEST)
    factor = jnp.linalg.cholesky(normal)
    pinv = jax.scipy.linalg.cho_solve((factor, True), design.T)
    return (pinv.astype(jnp.bfloat16), design.astype(jnp.bfloat16))


def tables(positions, length, count):
    half = (count + 1) // 2
    steps = jnp.arange(count, dtype=jnp.int32) - (half - 1)
    turns = positions[:, None] * steps[None, :] % length
    angle = turns.astype(jnp.float32) * (2.0 * math.pi / length)
    return (jnp.cos(angle), jnp.sin(angle))


def on_device(stack, network, bands):
    high = lax.Precision.HIGHEST
    solved = bands.shape[0]
    freqs = 2 * BAND - 1
    pinv, design = build_inverse(network, solved)
    block = lax.all_to_all(stack, "grp", split_axis=1, concat_axis=0, tiled=True)
    ifgs, strip, items = block.shape
    flat = block.reshape(ifgs, strip * items)
    series = jnp.dot(pinv, flat, preferred_element_type=jnp.float32)
    model = jnp.dot(design, series.astype(jnp.bfloat16), preferred_element_type=jnp.float32)
    resid = flat.astype(jnp.float32) - model
    fitted = jnp.sqrt(jnp.mean(resid * resid, axis=0) + 1e-06)
    series, fitted = (series.reshape(solved, strip, items), fitted.reshape(1, strip, items))
    row_dev = series.shape[1]
    col_dev = series.shape[2]
    rows_all = row_dev * lax.axis_size("grp")
    cols_all = col_dev * lax.axis_size("dev")
    row_pos = lax.axis_index("grp") * row_dev + jnp.arange(row_dev, dtype=jnp.int32)
    col_pos = lax.axis_index("dev") * col_dev + jnp.arange(col_dev, dtype=jnp.int32)
    row_cos, row_sin = tables(row_pos, rows_all, freqs)
    col_cos, col_sin = tables(col_pos, cols_all, freqs)
    part_cos = jnp.einsum("thw,wl->thl", series, col_cos, precision=high)
    part_sin = jnp.einsum("thw,wl->thl", series, col_sin, precision=high)
    part_cos, part_sin = (
        taken_together(part_cos.astype(jnp.bfloat16), "dev").astype(jnp.float32),
        taken_together(part_sin.astype(jnp.bfloat16), "dev").astype(jnp.float32),
    )
    zeros = jnp.zeros((solved, freqs, freqs), jnp.float32)
    pieces = tuple(
        (
            part.astype(jnp.float32)
            for part in side_by_side(
                (part_cos.astype(jnp.bfloat16), part_sin.astype(jnp.bfloat16)), "grp", 1, 0
            )
        )
    )
    count = pieces[0].shape[1]
    positions = jnp.arange(count, dtype=jnp.int32)
    piece_cos, piece_sin = tables(positions, rows_all, freqs)
    real_sum = zeros
    imag_sum = zeros
    real_sum = (
        real_sum
        + jnp.einsum("hk,thl->tkl", piece_cos, pieces[0], precision=high)
        - jnp.einsum("hk,thl->tkl", piece_sin, pieces[1], precision=high)
    )
    imag_sum = (
        imag_sum
        - jnp.einsum("hk,thl->tkl", piece_sin, pieces[0], precision=high)
        - jnp.einsum("hk,thl->tkl", piece_cos, pieces[1], precision=high)
    )
    real = real_sum
    imag = imag_sum
    scale = 1.0 / (rows_all * cols_all)
    steps = jnp.abs(jnp.arange(freqs, dtype=jnp.int32) - (BAND - 1))
    keep = (steps[None, :] < bands[:, None]).astype(jnp.float32)
    mask = keep[:, :, None] * keep[:, None, :]
    real = real * scale * mask
    imag = imag * scale * mask
    spectrum = jnp.stack([real, imag])
    rising = jnp.einsum("hk,tkl->thl", row_cos, real, precision=high) - jnp.einsum(
        "hk,tkl->thl", row_sin, imag, precision=high
    )
    falling = -(
        jnp.einsum("hk,tkl->thl", row_sin, real, precision=high)
        + jnp.einsum("hk,tkl->thl", row_cos, imag, precision=high)
    )
    ramp = jnp.einsum("thl,wl->thw", rising, col_cos, precision=high) + jnp.einsum(
        "thl,wl->thw", falling, col_sin, precision=high
    )
    deramped = (series - ramp).astype(jnp.bfloat16)
    return (deramped, fitted[0], spectrum)


def solution(mesh):
    return jax.shard_map(
        on_device,
        mesh=mesh,
        in_specs=(P("grp", None, "dev"), P(), P()),
        out_specs=(P(None, "grp", "dev"), P("grp", "dev"), P()),
        check_vma=False,
    )
```

profile of v0, /device:TPU:1, one launch (start us, length us, event | category | flops | bytes accessed | tf_op | source)
XLA Modules:
  0.0 228.0 jit_solution(1234289894343990187)
XLA Ops:
  7.2 4.8 %copy.10 = bf16[19,256,256]{2,0,1:T(8,128)(2,1)} copy(bf16[19,256,256]{2,1,0:T(8,128)(2,1)} %param.3) | data formatting | bytes 4980736 | tf_op args[0]
  12.0 10.3 %all-to-all-start = ((bf16[19,256,256]{2,0,1:T(8,128)(2,1)}), bf16[19,256,256]{2,0,1:T(8,128)(2,1)S(1)}, u32[]{:S(2)}, u32[]{:S(2)}) async-start(bf16[19,256,256]{2,0,1:T(8,128)(2,1)} %copy.10), calls=%async_computation | async-start | bytes 6291456 | tf_op jit(solution)/shard_map/all_to_all | solution.py:54
  22.4 1.5 fusion.41
  24.0 0.7 copy-done.3
  24.7 11.7 %cholesky.51 = f32[128,128]{1,0:T(8,128)S(1)} custom-call(f32[128,128]{1,0:T(8,128)S(1)} %cholesky.124), custom_call_target="Cholesky" | custom-call | tf_op jit(solution)/shard_map/jit(cholesky)/cholesky | solution.py:36
  36.5 9.8 %custom-call.18 = f32[1,128,128]{1,2,0:T(8,128)S(1)} custom-call(f32[1,128,128]{2,1,0:T(8,128)S(1)} %get-tuple-element.32), custom_call_target="InvertDiagBlocksLowerTriangular" | custom-call | tf_op jit(solution)/shard_map/jit(cholesky)/cholesky | solution.py:36
  46.3 0.9 constant_dynamic-update-slice_fusion.1
  47.2 0.9 convolution_subtract_fusion.2
  48.0 1.9 cholesky.110
  50.0 0.6 compare_reduce_fusion.1
  50.6 0.6 compare_reduce_fusion
  52.7 0.7 pad_maximum_fusion.1
  53.4 20.7 %custom-call.19 = f32[2,128,128]{1,2,0:T(8,128)S(1)} custom-call(f32[2,128,128]{2,1,0:T(8,128)} %pad_maximum_fusion.1), custom_call_target="InvertDiagBlocksLowerTriangular" | custom-call | tf_op jit(solution)/shard_map/jit(_cho_solve)/triangular_solve | solution.py:37
  74.2 0.5 copy-done.4
  74.7 0.7 fusion.50
  75.8 1.0 fusion.86
  76.8 0.9 fusion.168
  77.7 0.7 convolution_subtract_fusion
  78.4 1.3 convolution_convert_fusion.2
  79.7 14.5 %all-to-all-done = bf16[19,256,256]{2,0,1:T(8,128)(2,1)S(1)} async-done(((bf16[19,256,256]{2,0,1:T(8,128)(2,1)}), bf16[19,256,256]{2,0,1:T(8,128)(2,1)S(1)}, u32[]{:S(2)}, u32[]{:S(2)}) %all-to-all-start) | async-done | bytes 2490400 | tf_op jit(solution)/shard_map/all_to_all | solution.py:54
  94.3 0.7 copy.11
  95.0 0.8 copy.23
  95.8 0.7 fusion.59
  96.5 0.8 copy-done.1
  97.3 0.4 copy.24
  97.7 1.2 convolution_convert_fusion.1
  99.2 0.8 broadcast_in_dim.8
  100.1 8.0 %all-to-all-start.1 = ((bf16[8,149,8,15]{1,2,3,0:T(8,128)(2,1)}), bf16[8,149,8,15]{1,2,3,0:T(8,128)(2,1)S(1)}, u32[]{:S(2)}, u32[]{:S(2)}) async-start(bf16[8,149,8,15]{1,2,3,0:T(8,128)(2,1)} %broadcast_in_dim.8), calls=%async_computation.1 | async-start | bytes 983040 | tf_op jit(solution)/shard_map/all_to_all | solution.py:13
  108.0 1.2 convolution_convert_fusion
  109.5 13.0 %all-to-all-done.1 = bf16[8,149,8,15]{1,2,3,0:T(8,128)(2,1)S(1)} async-done(((bf16[8,149,8,15]{1,2,3,0:T(8,128)(2,1)}), bf16[8,149,8,15]{1,2,3,0:T(8,128)(2,1)S(1)}, u32[]{:S(2)}, u32[]{:S(2)}) %all-to-all-start.1) | async-done | bytes 286112 | tf_op jit(solution)/shard_map/all_to_all | solution.py:13
  122.6 0.8 broadcast_in_dim.9
  123.4 5.0 %all-to-all-start.2 = ((bf16[8,149,8,15]{1,2,3,0:T(8,128)(2,1)}), bf16[8,149,8,15]{1,2,3,0:T(8,128)(2,1)S(1)}, u32[]{:S(2)}, u32[]{:S(2)}) async-start(bf16[8,149,8,15]{1,2,3,0:T(8,128)(2,1)} %broadcast_in_dim.9), calls=%async_computation.2 | async-start | bytes 983040 | tf_op jit(solution)/shard_map/all_to_all | solution.py:13
  128.8 12.5 %all-to-all-done.2 = bf16[8,149,8,15]{1,2,3,0:T(8,128)(2,1)S(1)} async-done(((bf16[8,149,8,15]{1,2,3,0:T(8,128)(2,1)}), bf16[8,149,8,15]{1,2,3,0:T(8,128)(2,1)S(1)}, u32[]{:S(2)}, u32[]{:S(2)}) %all-to-all-start.2) | async-done | bytes 286112 | tf_op jit(solution)/shard_map/all_to_all | solution.py:13
  141.4 0.7 pad_maximum_fusion.2
  142.1 0.8 compare_convert_fusion
  142.9 2.6 %multiply_reduce_fusion = f32[2048]{0:T(1024)S(1)} fusion(bf16[608,2048]{1,0:T(8,128)(2,1)} %bitcast.96, f32[149,2048]{1,0:T(8,128)S(1)} %fusion.59, s32[149]{0:T(256)S(1)} %iota_add_fusion.1, s32[608]{0:T(1024)S(1)} %get-tuple-element.30, s32[608]{0:T(1024)S(1)} %get-tuple-element.29), kind=kOutput, calls=%fused_computation | convolution fusion | flops 376892224 | bytes 3724628 | tf_op jit(solution)/shard_map/dot_general | solution.py:58
  145.6 0.6 sqrt.8
  146.2 58.7 %all-gather.2.cloned.1.call-done = bf16[298,256,15]{0,1,2:T(8,128)(2,1)} async-done(((bf16[298,8,15]{0,1,2:T(8,128)(2,1)}), bf16[298,256,15]{0,1,2:T(8,128)(2,1)}) %all-gather.2.cloned.1.call-update) | async-done | bytes 2288656 | tf_op jit(solution)/shard_map/all_gather | solution.py:26
  204.8 2.9 %fusion = f32[149,15,15]{0,2,1:T(8,128)S(1)} fusion(bf16[298,256,15]{0,1,2:T(8,128)(2,1)} %all-gather.2.cloned.1.call-done, s32[15]{0:T(128)S(1)} %iota_add_fusion.3), kind=kOutput, calls=%fused_computation.1 | convolution fusion | flops 103042560 | bytes 2100240 | tf_op jit(solution)/shard_map/hk,thl->tkl/dot_general | solution.py:93
  207.7 2.7 %fusion.34 = f32[149,15,15]{0,1,2:T(8,128)S(1)} fusion(f32[149,15,15]{0,2,1:T(8,128)S(1)} %fusion, bf16[298,256,15]{0,1,2:T(8,128)(2,1)} %all-gather.2.cloned.1.call-done, f32[149,15]{0,1:T(8,128)S(1)} %compare_convert_fusion, s32[15]{0:T(128)S(1)} %iota_add_fusion.3), kind=kOutput, calls=%fused_computation.24 | convolution fusion | flops 103176656 | bytes 2379220 | tf_op jit(solution)/shard_map/hk,thl->tkl/dot_general | solution.py:92
  211.1 1.3 fusion.2
  212.5 1.0 fusion.22
  214.3 1.1 copy.16
  215.8 0.4 copy.20
  216.2 0.4 copy.17
  216.6 1.2 copy.19
  217.9 1.2 fusion.45
  219.1 2.1 fusion.9
  (41 shorter events, 3.9 us)
Async XLA Ops:
  12.0 10.3 %copy-start.5 = (s32[608,2]{0,1:T(2,128)S(1)}, s32[608,2]{0,1:T(2,128)}, u32[]{:S(2)}) copy-start(s32[608,2]{0,1:T(2,128)} %param.4) | copy-start | bytes 14596
  12.0 82.3 %all-to-all-start = ((bf16[19,256,256]{2,0,1:T(8,128)(2,1)}), bf16[19,256,256]{2,0,1:T(8,128)(2,1)S(1)}, u32[]{:S(2)}, u32[]{:S(2)}) async-start(bf16[19,256,256]{2,0,1:T(8,128)(2,1)} %copy.10), calls=%async_computation | async-start | bytes 6291456 | tf_op jit(solution)/shard_map/all_to_all | solution.py:54
  24.0 0.7 copy-start.3
  74.1 0.7 copy-start.4
  95.8 1.5 copy-start.1
  100.1 22.5 %all-to-all-start.1 = ((bf16[8,149,8,15]{1,2,3,0:T(8,128)(2,1)}), bf16[8,149,8,15]{1,2,3,0:T(8,128)(2,1)S(1)}, u32[]{:S(2)}, u32[]{:S(2)}) async-start(bf16[8,149,8,15]{1,2,3,0:T(8,128)(2,1)} %broadcast_in_dim.8), calls=%async_computation.1 | async-start | bytes 983040 | tf_op jit(solution)/shard_map/all_to_all | solution.py:13
  123.4 17.9 %all-to-all-start.2 = ((bf16[8,149,8,15]{1,2,3,0:T(8,128)(2,1)}), bf16[8,149,8,15]{1,2,3,0:T(8,128)(2,1)S(1)}, u32[]{:S(2)}, u32[]{:S(2)}) async-start(bf16[8,149,8,15]{1,2,3,0:T(8,128)(2,1)} %broadcast_in_dim.9), calls=%async_computation.2 | async-start | bytes 983040 | tf_op jit(solution)/shard_map/all_to_all | solution.py:13
  128.4 76.4 %all-gather.2.cloned.1.call-start = ((), (), s32[]{:S(2)}) async-start(), calls=%async_computation.3 | async-start | bytes 3041280 | tf_op jit(solution)/shard_map/all_gather | solution.py:26
  207.7 3.5 %copy-start = (bf16[298,256,15]{0,1,2:T(8,128)(2,1)S(1)}, bf16[298,256,15]{0,1,2:T(8,128)(2,1)}, u32[]{:S(2)}) copy-start(bf16[298,256,15]{0,1,2:T(8,128)(2,1)} %all-gather.2.cloned.1.call-done) | copy-start | bytes 6865924
  217.8 1.3 copy-start.2
Sparse Core Ops, SparseCore 0:
  142.2 62.5 all-gather.1
where the time goes:
time: 229 us; the launch traced here: 228 us
  waiting for transfers between devices  98.7 us (43%)
  other arithmetic  48.1 us (21%)
  matrix products  26.7 us (12%)
  starting transfers between devices  23.5 us (10%)
  between operations  15.7 us (7%)
  local copies, waits for them, and re-layouts  15.2 us (7%)
    all_gather x1, waiting for transfers between devices, side_by_side(): filled = lax.all_gather(both, axis, axis=dim, tiled=True)  58.7 us
    all_to_all x2, waiting for transfers between devices, from_everyone(): lax.all_to_all(jnp.broadcast_to(shard[None], (peers, *shard.shape)), axis...  25.5 us
    another operation x7, other arithmetic, build_inverse(): factor = jnp.linalg.cholesky(normal)  24.8 us
    another operation x6, other arithmetic, build_inverse(): pinv = jax.scipy.linalg.cho_solve((factor, True), design.T)  21.5 us
    all_to_all x1, waiting for transfers between devices, on_device(): lax.all_to_all(stack, 'grp', split_axis=1, concat_axis=0, tiled=True)  14.5 us
    all_to_all x2, starting transfers between devices, from_everyone(): lax.all_to_all(jnp.broadcast_to(shard[None], (peers, *shard.shape)), axis...  13 us
    all_to_all x1, starting transfers between devices, on_device(): lax.all_to_all(stack, 'grp', split_axis=1, concat_axis=0, tiled=True)  10.3 us
    unnamed x16, local copies, waits for them, and re-layouts  9.14 us
  transfers between devices with their start and end apart: 4, of which 4 were waited for; matrix products, arithmetic and copies ran while one was open for 26% of the time, Pallas kernels for 0%

commit v1 on v0

v1 whole, which is shorter than its diff:
```python
import math

import jax
import jax.numpy as jnp
import numpy as np
from jax import lax
from jax.sharding import PartitionSpec as P

BAND = 8
FREQS = 2 * BAND - 1
HIGH = lax.Precision.HIGHEST


def design_of(network, solved):
    dates = jnp.arange(1, solved + 1, dtype=jnp.int32)
    return (network[:, 1:2] == dates[None, :]).astype(jnp.float32) - (
        network[:, 0:1] == dates[None, :]
    ).astype(jnp.float32)


def build_inverse(network, solved):
    design = design_of(network, solved)
    normal = jnp.dot(design.T, design, precision=HIGH)
    factor = jnp.linalg.cholesky(normal)
    pinv = jax.scipy.linalg.cho_solve((factor, True), design.T)
    return (pinv.astype(jnp.bfloat16), design.astype(jnp.bfloat16))


def basis(positions, length):
    index = jnp.arange(FREQS, dtype=jnp.int32)
    step = jnp.where(index < BAND, index, index - (BAND - 1))
    turns = positions[:, None] * step[None, :] % length
    angle = turns.astype(jnp.float32) * (2.0 * math.pi / length)
    return jnp.where(index[None, :] < BAND, jnp.cos(angle), jnp.sin(angle))


def mirror():
    out = np.zeros((FREQS, FREQS, 2, FREQS, FREQS), np.float32)
    for k in range(FREQS):
        for l in range(FREQS):
            fk, fl = k - (BAND - 1), l - (BAND - 1)
            ck, cl = abs(fk), abs(fl)
            sk, sl = abs(fk) + BAND - 1, abs(fl) + BAND - 1
            gk, gl = np.sign(fk), np.sign(fl)
            out[k, l, 0, ck, cl] += 1
            if gk * gl:
                out[k, l, 0, sk, sl] -= gk * gl
            if gk:
                out[k, l, 1, sk, cl] -= gk
            if gl:
                out[k, l, 1, ck, sl] -= gl
    return out.reshape(FREQS * FREQS * 2, FREQS * FREQS)


def on_device(stack, network, bands):
    solved = bands.shape[0]
    groups = lax.axis_size("grp")
    held, rows_all, col_dev = stack.shape
    row_dev = rows_all // groups
    cols_all = col_dev * lax.axis_size("dev")
    pixels = row_dev * col_dev

    packed = stack.reshape(held, groups, row_dev, col_dev).transpose(1, 0, 2, 3)
    block = lax.all_to_all(packed, "grp", 0, 0, tiled=True)

    rows = basis(jnp.arange(rows_all, dtype=jnp.int32), rows_all)
    cols = basis(
        lax.axis_index("dev") * col_dev + jnp.arange(col_dev, dtype=jnp.int32), cols_all
    )
    wide = stack.astype(jnp.float32)
    half = jnp.einsum("ihw,ha->iaw", wide, rows, precision=HIGH)
    local = jnp.einsum("iaw,wb->iab", half, cols, precision=HIGH)
    local = local.reshape(held, FREQS * FREQS)
    summed = lax.psum(local, "dev")
    every = lax.all_gather(summed, "grp", axis=0, tiled=True)

    pinv, design = build_inverse(network, solved)
    scale = 1.0 / (rows_all * cols_all)
    coef = scale * lax.dot_general(
        every, pinv.astype(jnp.float32), (((0,), (1,)), ((), ())), precision=HIGH
    )
    index = np.arange(FREQS)
    step = np.where(index < BAND, index, index - (BAND - 1))
    weight = np.where(step == 0, 1.0, 2.0)
    kmax = np.maximum(step[:, None], step[None, :]).reshape(-1)
    both = (weight[:, None] * weight[None, :]).reshape(-1).astype(np.float32)
    masked = jnp.where(jnp.asarray(kmax)[:, None] < bands[None, :], coef, 0.0)
    signed = jnp.dot(jnp.asarray(mirror()), masked, precision=HIGH)
    spectrum = signed.reshape(FREQS, FREQS, 2, solved).transpose(2, 3, 0, 1)

    row_here = basis(
        lax.axis_index("grp") * row_dev + jnp.arange(row_dev, dtype=jnp.int32), rows_all
    )
    waves = (row_here.T[:, None, :, None] * cols.T[None, :, None, :]).reshape(
        FREQS * FREQS, pixels
    )
    ramp = lax.dot_general(
        masked * jnp.asarray(both)[:, None], waves, (((0,), (0,)), ((), ())), precision=HIGH
    )

    flat = block.reshape(held * groups, pixels)
    series = jnp.dot(pinv, flat, preferred_element_type=jnp.float32)
    deramped = (series - ramp).astype(jnp.bfloat16).reshape(solved, row_dev, col_dev)
    model = jnp.dot(design, series.astype(jnp.bfloat16), preferred_element_type=jnp.float32)
    resid = flat.astype(jnp.float32) - model
    misfit = jnp.sqrt(jnp.mean(resid * resid, axis=0) + 1e-06).reshape(row_dev, col_dev)
    return (deramped, misfit, spectrum)


def solution(mesh):
    return jax.shard_map(
        on_device,
        mesh=mesh,
        in_specs=(P("grp", None, "dev"), P(), P()),
        out_specs=(P(None, "grp", "dev"), P("grp", "dev"), P()),
        check_vma=False,
    )
```

time: 229 us -> 183 us (0.80)
  blocking collectives: 0 us -> 99.7 us
  waiting for transfers between devices: 98.7 us -> 0.01 us
  matrix products: 26.7 us -> 11 us
  between operations: 15.7 us -> 2.38 us
  starting transfers between devices: 23.5 us -> 10.4 us
  other arithmetic: 48.1 us -> 45.4 us
    all_gather x1 -> x0, waiting for transfers between devices: 58.7 us -> none  [side_by_side(): filled = lax.all_gather(both, axis, axis=dim, tiled=True)]
    all_gather x0 -> x1, blocking collectives: none -> 53.9 us  [on_device(): every = lax.all_gather(summed, 'grp', axis=0, tiled=True)]
    psum x0 -> x1, blocking collectives: none -> 45.8 us  [on_device(): summed = lax.psum(local, 'dev')]
    all_to_all x3 -> x1, waiting for transfers between devices: 40.1 us -> 0.01 us  [on_device(): block = lax.all_to_all(packed, 'grp', 0, 0, tiled=True)]
    all_to_all x3 -> x1, starting transfers between devices: 23.3 us -> 10.4 us  [on_device(): block = lax.all_to_all(packed, 'grp', 0, 0, tiled=True)]
    dot_general x13 -> x6, matrix products: 16.7 us -> 5.66 us  [the longest x1 1.54 us: build_inverse(): normal = jnp.dot(design.T, design, precision=HIGH)]
    dot_general x5 -> x1, local copies, waits for them, and re-layouts: 2.54 us -> 0.1 us  [build_inverse(): normal = jnp.dot(design.T, design, precision=HIGH)]
    unnamed x16 -> x31, local copies, waits for them, and re-layouts: 9.14 us -> 8.8 us
  transfers between devices with their start and end apart: 4 -> 1, of which waited for: 4 -> 0; matrix products, arithmetic and copies ran while one was open for 26% -> 32% of each run, Pallas kernels for 0% -> 0%
where the time goes in v1:
time: 183 us; the launch traced here: 182 us
  blocking collectives  99.7 us (54%)
  other arithmetic  45.4 us (25%)
  local copies, waits for them, and re-layouts  13.4 us (7%)
  matrix products  11 us (6%)
  starting transfers between devices  10.4 us (6%)
  between operations  2.38 us (1%)
    all_gather x1, blocking collectives, on_device(): every = lax.all_gather(summed, 'grp', axis=0, tiled=True)  53.9 us
    psum x1, blocking collectives, on_device(): summed = lax.psum(local, 'dev')  45.8 us
    another operation x7, other arithmetic, build_inverse(): factor = jnp.linalg.cholesky(normal)  24.8 us
    another operation x6, other arithmetic, build_inverse(): pinv = jax.scipy.linalg.cho_solve((factor, True), design.T)  20 us
    all_to_all x1, starting transfers between devices, on_device(): block = lax.all_to_all(packed, 'grp', 0, 0, tiled=True)  10.4 us
    unnamed x31, local copies, waits for them, and re-layouts  8.8 us
  transfers between devices with their start and end apart: 1, of which 0 were waited for; matrix products, arithmetic and copies ran while one was open for 32% of the time, Pallas kernels for 0%

profile of v1, /device:TPU:1, one launch (start us, length us, event | category | flops | bytes accessed | tf_op | source)
XLA Modules:
  0.0 182.2 jit_solution(6894326143020125078)
XLA Ops:
  0.6 0.0 copy-start
  0.6 1.7 copy-done
  2.3 1.6 copy_bitcast_fusion
  4.0 10.4 %all-to-all-start = ((bf16[32,19,8,256]{3,2,1,0:T(8,128)(2,1)}), bf16[32,19,8,256]{3,2,1,0:T(8,128)(2,1)}, u32[]{:S(2)}, u32[]{:S(2)}) async-start(bf16[32,19,8,256]{3,2,1,0:T(8,128)(2,1)} %copy_bitcast_fusion), calls=%async_computation | async-start | bytes 4980736 | tf_op jit(solution)/shard_map/all_to_all | solution.py:64
  14.4 1.5 fusion.4
  15.9 0.1 copy.17
  16.1 11.7 %cholesky.51 = f32[128,128]{1,0:T(8,128)S(1)} custom-call(f32[128,128]{1,0:T(8,128)S(1)} %cholesky.124), custom_call_target="Cholesky" | custom-call | tf_op jit(solution)/shard_map/jit(cholesky)/cholesky | solution.py:24
  27.8 9.8 %custom-call.18 = f32[1,128,128]{1,2,0:T(8,128)S(1)} custom-call(f32[1,128,128]{2,1,0:T(8,128)S(1)} %get-tuple-element.26), custom_call_target="InvertDiagBlocksLowerTriangular" | custom-call | tf_op jit(solution)/shard_map/jit(cholesky)/cholesky | solution.py:24
  37.7 0.2 constant_dynamic-update-slice_fusion.1
  37.8 0.2 convolution_subtract_fusion.3
  38.0 1.9 %cholesky.110 = f32[21,21]{1,0:T(8,128)S(1)} custom-call(f32[21,21]{1,0:T(8,128)S(1)} %convolution_subtract_fusion.3), custom_call_target="Cholesky" | custom-call | tf_op jit(solution)/shard_map/jit(cholesky)/cholesky | solution.py:24
  39.9 0.6 compare_reduce_fusion
  40.6 0.6 compare_reduce_fusion.1
  42.6 0.1 fusion.20
  42.7 19.9 %custom-call.19 = f32[2,128,128]{1,2,0:T(8,128)S(1)} custom-call(f32[2,128,128]{2,1,0:T(8,128)S(1)} %pad_maximum_fusion.3), custom_call_target="InvertDiagBlocksLowerTriangular" | custom-call | tf_op jit(solution)/shard_map/jit(_cho_solve)/triangular_solve | solution.py:25
  62.6 0.1 convert_subtract_fusion.2
  62.7 0.7 fusion.7
  63.4 0.7 copy-done.2
  64.2 0.4 convolution_subtract_fusion.2
  64.6 0.3 fusion.53
  64.8 0.2 fusion.82
  65.0 0.2 copy.18
  65.3 1.2 convolution_bitcast_fusion
  66.5 0.5 fusion.32
  67.0 0.1 reshape.205
  67.1 45.8 %psum.7 = f32[19,225]{1,0:T(8,128)S(1)} all-reduce(f32[19,225]{1,0:T(8,128)S(1)} %reshape.205), channel_id=1, replica_groups=mesh['grp'=32,'dev'=8] {'dev'}, use_global_device_ids=true, to_apply=%region_4.5 | all-reduce | flops 4275 | bytes 34200 | tf_op jit(solution)/shard_map/psum | solution.py:74
  112.9 53.9 %all-gather = f32[32,19,225]{2,1,0:T(8,128)S(1)} all-gather(f32[1,19,225]{2,1,0:T(8,128)S(1)} %bitcast.72), channel_id=1, replica_groups=mesh['grp'=32,'dev'=8] {'grp'}, dimensions={0}, use_global_device_ids=true | all-gather | bytes 564300 | tf_op jit(solution)/shard_map/all_gather | solution.py:75
  166.8 0.9 reshape.238
  167.7 0.1 sine_select_fusion.1
  167.8 0.2 sine_select_fusion
  168.0 0.2 broadcast_multiply_fusion
  168.2 0.1 pad.23
  168.4 0.0 copy-start.12
  168.4 2.1 %copy.23 = f32[29,8,8,256]{3,1,2,0:T(8,128)} copy(f32[29,8,8,256]{3,2,1,0:T(8,128)S(1)} %bitcast.67) | data formatting | bytes 3801088
  170.5 1.4 convolution_subtract_fusion.1
  171.9 0.4 convolution_convert_fusion
  172.3 0.5 fusion.1
  172.9 0.5 fusion.83
  173.4 1.0 reshape.207
  174.5 2.5 %copy.22 = bf16[76,8,8,256]{3,1,2,0:T(8,128)(2,1)S(1)} copy(bf16[76,8,8,256]{3,2,1,0:T(8,128)(2,1)} %bitcast.15) | data formatting | bytes 4980736
  177.0 0.7 fusion.16
  177.7 0.0 copy-start.10
  177.7 1.0 multiply_reduce_fusion
  178.7 0.5 copy-done.1
  179.2 1.3 fusion
  180.5 0.1 copy.24
  180.7 0.9 slice.94
  181.6 0.6 sqrt.8
  (38 shorter events, 0.3 us)
Async XLA Ops:
  0.6 1.7 copy-start
  4.0 10.4 %copy-start.9 = (s32[608,2]{0,1:T(2,128)S(1)}, s32[608,2]{0,1:T(2,128)}, u32[]{:S(2)}) copy-start(s32[608,2]{0,1:T(2,128)} %param.7) | copy-start | bytes 14596
  4.0 170.5 %all-to-all-start = ((bf16[32,19,8,256]{3,2,1,0:T(8,128)(2,1)}), bf16[32,19,8,256]{3,2,1,0:T(8,128)(2,1)}, u32[]{:S(2)}, u32[]{:S(2)}) async-start(bf16[32,19,8,256]{3,2,1,0:T(8,128)(2,1)} %copy_bitcast_fusion), calls=%async_computation | async-start | bytes 4980736 | tf_op jit(solution)/shard_map/all_to_all | solution.py:64
  42.5 23.9 %copy-start.6 = (f32[149,149]{1,0:T(8,128)}, f32[149,149]{1,0:T(8,128)S(1)}, u32[]{:S(2)}) copy-start(f32[149,149]{1,0:T(8,128)S(1)} %select_select_fusion) | copy-start | bytes 266416
  62.6 2.7 %copy-start.7 = (f32[2,128,128]{1,2,0:T(8,128)}, f32[2,128,128]{1,2,0:T(8,128)S(1)}, u32[]{:S(2)}) copy-start(f32[2,128,128]{1,2,0:T(8,128)S(1)} %custom-call.19) | copy-start | bytes 393220
  63.4 0.7 copy-start.2
  168.3 2.2 %copy-start.3 = (f32[128,608]{0,1:T(8,128)S(1)}, f32[128,608]{0,1:T(8,128)}, u32[]{:S(2)}) copy-start(f32[128,608]{0,1:T(8,128)} %copy-done.2) | copy-start | bytes 933892
  168.3 3.5 %copy-start.8 = (f32[2,128,128]{1,2,0:T(8,128)S(1)}, f32[2,128,128]{1,2,0:T(8,128)}, u32[]{:S(2)}) copy-start(f32[2,128,128]{1,2,0:T(8,128)} %copy-done.7) | copy-start | bytes 393220
  168.4 4.0 %copy-start.4 = (f32[608,225]{1,0:T(8,128)S(1)}, f32[608,225]{1,0:T(8,128)}, u32[]{:S(2)}) copy-start(f32[608,225]{1,0:T(8,128)} %reshape.238) | copy-start | bytes 1641604
  168.4 4.0 %copy-start.11 = (s32[149]{0:T(256)S(1)}, s32[149]{0:T(256)}, u32[]{:S(2)}) copy-start(s32[149]{0:T(256)} %param.8) | copy-start | bytes 1792
  168.4 4.0 %copy-start.12 = (s32[225]{0:T(256)S(1)}, s32[225]{0:T(256)}, u32[]{:S(2)}) copy-start(s32[225]{0:T(256)} %constant.175.clone) | copy-start | bytes 2704
  168.4 4.5 %copy-start.5 = (f32[450,225]{1,0:T(8,128)S(1)}, f32[450,225]{1,0:T(8,128)}, u32[]{:S(2)}) copy-start(f32[450,225]{1,0:T(8,128)} %constant.176.clone) | copy-start | bytes 1215004
  177.7 1.5 copy-start.1
  177.7 1.5 copy-start.10

commit v2 on v1

--- a/solution.py
+++ b/solution.py
@@ -4,7 +4,10 @@
 import jax.numpy as jnp
 import numpy as np
 from jax import lax
+from jax.experimental import pallas as pl
+from jax.experimental.pallas import tpu as pltpu
 from jax.sharding import PartitionSpec as P
+
 
 BAND = 8
 FREQS = 2 * BAND - 1
@@ -18,12 +21,50 @@
     ).astype(jnp.float32)
 
 
+def sweep_kernel(normal_ref, out_ref):
+    size, width = out_ref.shape
+    out_ref[...] = normal_ref[...]
+    lane = lax.broadcasted_iota(jnp.int32, (size, width), 1)
+    top = lax.broadcasted_iota(jnp.int32, (1, width), 1)
+
+    def step(k, carry):
+        whole = out_ref[...]
+        row = out_ref[pl.ds(k, 1), :]
+        col = jnp.sum(jnp.where(lane == k, whole, 0.0), axis=1, keepdims=True)
+        pivot = jnp.sum(jnp.where(top == k, row, 0.0), axis=1, keepdims=True)
+        inv = 1.0 / pivot
+        scaled = jnp.where(top == k, inv, row * inv)
+        out_ref[...] = jnp.where(lane == k, -col * inv, whole - col * scaled)
+        out_ref[pl.ds(k, 1), :] = scaled
+        return carry
+
+    lax.fori_loop(0, size, step, 0)
+
+
 def build_inverse(network, solved):
-    design = design_of(network, solved)
-    normal = jnp.dot(design.T, design, precision=HIGH)
-    factor = jnp.linalg.cholesky(normal)
-    pinv = jax.scipy.linalg.cho_solve((factor, True), design.T)
-    return (pinv.astype(jnp.bfloat16), design.astype(jnp.bfloat16))
+    design = design_of(network, solved).astype(jnp.bfloat16)
+    normal = lax.dot_general(
+        design, design, (((0,), (0,)), ((), ())), preferred_element_type=jnp.float32
+    )
+    size, width = -(-solved // 8) * 8, -(-solved // 128) * 128
+    padded = jnp.pad(normal, ((0, size - solved), (0, width - solved)))
+    at = jnp.arange(size)
+    ones = jnp.where(at >= solved, 1.0, 0.0).astype(jnp.float32)
+    padded = padded + jnp.where(at[:, None] == jnp.arange(width)[None, :], ones[:, None], 0.0)
+    inverse = pl.pallas_call(
+        sweep_kernel,
+        out_shape=jax.ShapeDtypeStruct((size, width), jnp.float32),
+        in_specs=[pl.BlockSpec(memory_space=pltpu.VMEM)],
+        out_specs=pl.BlockSpec(memory_space=pltpu.VMEM),
+        cost_estimate=pl.CostEstimate(
+            flops=int(3e7), bytes_accessed=300000, transcendentals=0
+        ),
+        name="sweep",
+    )(padded)[:solved, :solved]
+    pinv = lax.dot_general(
+        inverse, design.astype(jnp.float32), (((1,), (1,)), ((), ())), precision=HIGH
+    )
+    return (pinv.astype(jnp.bfloat16), design)
 
 
 def basis(positions, length):
@@ -52,6 +93,38 @@
     return out.reshape(FREQS * FREQS * 2, FREQS * FREQS)
 
 
+def swapped(value, grp_bits, dev_bits):
+    devs = 8
+    return lax.ppermute(
+        value,
+        ("grp", "dev"),
+        [
+            (g * devs + d, (g ^ grp_bits) * devs + (d ^ dev_bits))
+            for g in range(32)
+            for d in range(devs)
+        ],
+    )
+
+
+def in_order(own, others, bit):
+    place = lax.axis_index("grp") // bit % 4
+    held = jnp.stack([own, *others])
+    return held[place ^ jnp.arange(4)]
+
+
+def share(local):
+    near = [swapped(local, k << 1, 0) for k in (1, 2, 3)]
+    far = [swapped(local, k << 1, 1) for k in (0, 1, 2, 3)]
+    part = in_order(local, near, 2) + in_order(far[0], far[1:], 2)
+    part = part + swapped(part, 0, 2)
+    part = part + swapped(part, 0, 4)
+    part = in_order(part, [swapped(part, k << 3, 0) for k in (1, 2, 3)], 8)
+    other = swapped(part, 1, 0)
+    first = lax.axis_index("grp") % 2 == 0
+    both = jnp.stack([jnp.where(first, part, other), jnp.where(first, other, part)], axis=2)
+    return both.reshape(-1, local.shape[-1])
+
+
 def on_device(stack, network, bands):
     solved = bands.shape[0]
     groups = lax.axis_size("grp")
@@ -59,9 +132,6 @@
     row_dev = rows_all // groups
     cols_all = col_dev * lax.axis_size("dev")
     pixels = row_dev * col_dev
-
-    packed = stack.reshape(held, groups, row_dev, col_dev).transpose(1, 0, 2, 3)
-    block = lax.all_to_all(packed, "grp", 0, 0, tiled=True)
 
     rows = basis(jnp.arange(rows_all, dtype=jnp.int32), rows_all)
     cols = basis(
@@ -71,8 +141,11 @@
     half = jnp.einsum("ihw,ha->iaw", wide, rows, precision=HIGH)
     local = jnp.einsum("iaw,wb->iab", half, cols, precision=HIGH)
     local = local.reshape(held, FREQS * FREQS)
-    summed = lax.psum(local, "dev")
-    every = lax.all_gather(summed, "grp", axis=0, tiled=True)
+
+    packed = stack.reshape(held, groups, row_dev, col_dev).transpose(1, 0, 2, 3)
+    packed, local = lax.optimization_barrier((packed, local))
+    block = lax.all_to_all(packed, "grp", 0, 0, tiled=True)
+    every = share(local)
 
     pinv, design = build_inverse(network, solved)
     scale = 1.0 / (rows_all * cols_all)

time: 183 us -> 140 us (0.77)
  blocking collectives: 99.7 us -> 0 us
  other arithmetic: 45.4 us -> 2.79 us
  waiting for transfers between devices: 0.01 us -> 41.9 us
  starting transfers between devices: 10.4 us -> 48.8 us
  Pallas kernels: 0 us -> 19.6 us
  local copies, waits for them, and re-layouts: 13.4 us -> 15.5 us
    all_gather x1 -> x0, blocking collectives: 53.9 us -> none  [on_device(): every = lax.all_gather(summed, 'grp', axis=0, tiled=True)]
    psum x1 -> x0, blocking collectives: 45.8 us -> none  [on_device(): summed = lax.psum(local, 'dev')]
    another operation x13 -> x5, other arithmetic: 44.8 us -> 0.18 us  [the longest x2 0.13 us: share(): jnp.stack([jnp.where(first, part, other), jnp.where(first, other, part)],...]
    ppermute x0 -> x13, waiting for transfers between devices: none -> 41.8 us  [swapped(): lax.ppermute(value, ('grp', 'dev'), [(g * devs + d, (g ^ grp_bits) * devs...]
    ppermute x0 -> x13, starting transfers between devices: none -> 38.6 us  [swapped(): lax.ppermute(value, ('grp', 'dev'), [(g * devs + d, (g ^ grp_bits) * devs...]
    pallas_call x0 -> x1, Pallas kernels: none -> 19.6 us  [build_inverse(): pl.pallas_call(sweep_kernel, out_shape=jax.ShapeDtypeStruct((size, width)...]
    another operation x8 -> x0, matrix products: 3.67 us -> none  [the longest x6 3.36 us: build_inverse(): pinv = jax.scipy.linalg.cho_solve((factor, True), design.T)]
    unnamed x31 -> x16, local copies, waits for them, and re-layouts: 8.8 us -> 8.57 us
  transfers between devices with their start and end apart: 1 -> 14, of which waited for: 0 -> 6; matrix products, arithmetic and copies ran while one was open for 32% -> 11% of each run, Pallas kernels for 0% -> 14%
where the time goes in v2:
time: 140 us; the launch traced here: 139 us
  starting transfers between devices  48.8 us (35%)
  waiting for transfers between devices  41.9 us (30%)
  Pallas kernels  19.6 us (14%)
  local copies, waits for them, and re-layouts  15.5 us (11%)
  matrix products  9.9 us (7%)
  other arithmetic  2.79 us (2%)
    ppermute x13, waiting for transfers between devices, swapped(): lax.ppermute(value, ('grp', 'dev'), [(g * devs + d, (g ^ grp_bits) * devs...  41.8 us
    ppermute x13, starting transfers between devices, swapped(): lax.ppermute(value, ('grp', 'dev'), [(g * devs + d, (g ^ grp_bits) * devs...  38.6 us
    pallas_call x1, Pallas kernels, build_inverse(): pl.pallas_call(sweep_kernel, out_shape=jax.ShapeDtypeStruct((size, width)...  19.6 us
    all_to_all x1, starting transfers between devices, on_device(): block = lax.all_to_all(packed, 'grp', 0, 0, tiled=True)  10.2 us
    unnamed x16, local copies, waits for them, and re-layouts  8.57 us
  transfers between devices with their start and end apart: 14, of which 6 were waited for; matrix products, arithmetic and copies ran while one was open for 11% of the time, Pallas kernels for 14%

profile of v2, /device:TPU:1, one launch (start us, length us, event | category | flops | bytes accessed | tf_op | source)
XLA Modules:
  0.0 139.5 jit_solution(14516693354518920945)
XLA Ops:
  0.7 1.7 %copy-done = bf16[19,256,256]{2,1,0:T(8,128)(2,1)S(1)} copy-done((bf16[19,256,256]{2,1,0:T(8,128)(2,1)S(1)}, bf16[19,256,256]{2,1,0:T(8,128)(2,1)}, u32[]{:S(2)}) %copy-start) | copy-done | bytes 2490392
  2.3 1.7 %copy_bitcast_fusion = bf16[32,19,8,256]{3,2,1,0:T(8,128)(2,1)} fusion(bf16[19,256,256]{2,1,0:T(8,128)(2,1)S(1)} %copy-done), kind=kLoop, calls=%fused_computation.5 | loop fusion | bytes 4980736 | tf_op jit(solution)/shard_map/transpose | solution.py:145
  4.0 1.2 convolution_bitcast_fusion
  5.2 0.5 fusion.25
  5.7 0.1 reshape.212
  5.9 10.2 %all-to-all-start = ((bf16[32,19,8,256]{3,2,1,0:T(8,128)(2,1)}), bf16[32,19,8,256]{3,2,1,0:T(8,128)(2,1)}, u32[]{:S(2)}, u32[]{:S(2)}) async-start(bf16[32,19,8,256]{3,2,1,0:T(8,128)(2,1)} %copy_bitcast_fusion), calls=%async_computation | async-start | bytes 4980736 | tf_op jit(solution)/shard_map/all_to_all | solution.py:147
  16.1 4.5 %collective-permute-start.6 = (f32[19,225]{1,0:T(8,128)S(1)}, f32[19,225]{1,0:T(8,128)S(1)}, u32[]{:S(2)}, u32[]{:S(2)}) collective-permute-start(f32[19,225]{1,0:T(8,128)S(1)} %reshape.212), channel_id=1, source_target_pairs={{0,49},{1,48},{2,51},{3,50},{4,53},{5,52},{6,55},{7,54},{8,57},{9,... | collective-permute-start | bytes 51308 | tf_op jit(solution)/shard_map/ppermute | solution.py:98
  20.6 0.3 collective-permute-start.5
  20.8 2.2 %collective-permute-start.4 = (f32[19,225]{1,0:T(8,128)S(1)}, f32[19,225]{1,0:T(8,128)S(1)}, u32[]{:S(2)}, u32[]{:S(2)}) collective-permute-start(f32[19,225]{1,0:T(8,128)S(1)} %reshape.212), channel_id=1, source_target_pairs={{0,17},{1,16},{2,19},{3,18},{4,21},{5,20},{6,23},{7,22},{8,25},{9,... | collective-permute-start | bytes 51308 | tf_op jit(solution)/shard_map/ppermute | solution.py:98
  23.1 3.0 %collective-permute-start.3 = (f32[19,225]{1,0:T(8,128)S(1)}, f32[19,225]{1,0:T(8,128)S(1)}, u32[]{:S(2)}, u32[]{:S(2)}) collective-permute-start(f32[19,225]{1,0:T(8,128)S(1)} %reshape.212), channel_id=1, source_target_pairs={{0,1},{1,0},{2,3},{3,2},{4,5},{5,4},{6,7},{7,6},{8,9},{9,8},{10,11... | collective-permute-start | bytes 51308 | tf_op jit(solution)/shard_map/ppermute | solution.py:98
  26.1 1.3 collective-permute-start.2
  27.5 0.1 sine_select_fusion.1
  27.6 0.2 sine_select_fusion
  27.7 0.6 fusion.3
  28.4 1.5 %broadcast_multiply_fusion = f32[15,15,8,256]{3,2,1,0:T(8,128)} fusion(f32[15,256]{1,0:T(8,128)S(1)} %sine_select_fusion, f32[15,8]{1,0:T(8,128)S(1)} %sine_select_fusion.1), kind=kLoop, calls=%fused_computation.11 | loop fusion | flops 460800 | bytes 1859040 | tf_op jit(solution)/shard_map/mul | solution.py:167
  29.9 15.7 %collective-permute-start.1 = (f32[19,225]{1,0:T(8,128)S(1)}, f32[19,225]{1,0:T(8,128)S(1)}, u32[]{:S(2)}, u32[]{:S(2)}) collective-permute-start(f32[19,225]{1,0:T(8,128)S(1)} %reshape.212), channel_id=1, source_target_pairs={{0,32},{1,33},{2,34},{3,35},{4,36},{5,37},{6,38},{7,39},{8,40},{9,... | collective-permute-start | bytes 51308 | tf_op jit(solution)/shard_map/ppermute | solution.py:98
  45.5 4.8 %collective-permute-done.5 = f32[19,225]{1,0:T(8,128)S(1)} collective-permute-done((f32[19,225]{1,0:T(8,128)S(1)}, f32[19,225]{1,0:T(8,128)S(1)}, u32[]{:S(2)}, u32[]{:S(2)}) %collective-permute-start.5) | collective-permute-done | bytes 17132 | tf_op jit(solution)/shard_map/ppermute | solution.py:98
  50.3 27.8 %collective-permute-done.4 = f32[19,225]{1,0:T(8,128)S(1)} collective-permute-done((f32[19,225]{1,0:T(8,128)S(1)}, f32[19,225]{1,0:T(8,128)S(1)}, u32[]{:S(2)}, u32[]{:S(2)}) %collective-permute-start.4) | collective-permute-done | bytes 17132 | tf_op jit(solution)/shard_map/ppermute | solution.py:98
  78.1 0.6 gather_fusion.1
  78.8 0.6 gather_fusion
  79.3 1.3 collective-permute-start.7
  80.7 2.6 %collective-permute-done.7 = f32[4,19,225]{2,1,0:T(8,128)S(1)} collective-permute-done((f32[4,19,225]{2,1,0:T(8,128)S(1)}, f32[4,19,225]{2,1,0:T(8,128)S(1)}, u32[]{:S(2)}, u32[]{:S(2)}) %collective-permute-start.7) | collective-permute-done | bytes 68432 | tf_op jit(solution)/shard_map/ppermute | solution.py:98
  83.3 2.8 %collective-permute-start.8 = (f32[4,19,225]{2,1,0:T(8,128)S(1)}, f32[4,19,225]{2,1,0:T(8,128)S(1)}, u32[]{:S(2)}, u32[]{:S(2)}) collective-permute-start(f32[4,19,225]{2,1,0:T(8,128)S(1)} %add.132), channel_id=1, source_target_pairs={{0,4},{1,5},{2,6},{3,7},{4,0},{5,1},{6,2},{7,3},{8,12},{9,13},{10,... | collective-permute-start | bytes 205208 | tf_op jit(solution)/shard_map/ppermute | solution.py:98
  86.1 2.2 %collective-permute-done.8 = f32[4,19,225]{2,1,0:T(8,128)S(1)} collective-permute-done((f32[4,19,225]{2,1,0:T(8,128)S(1)}, f32[4,19,225]{2,1,0:T(8,128)S(1)}, u32[]{:S(2)}, u32[]{:S(2)}) %collective-permute-start.8) | collective-permute-done | bytes 68432 | tf_op jit(solution)/shard_map/ppermute | solution.py:98
  88.4 2.7 %collective-permute-start.11 = (f32[4,19,225]{2,1,0:T(8,128)S(1)}, f32[4,19,225]{2,1,0:T(8,128)S(1)}, u32[]{:S(2)}, u32[]{:S(2)}) collective-permute-start(f32[4,19,225]{2,1,0:T(8,128)S(1)} %add.133), channel_id=1, source_target_pairs={{0,192},{1,193},{2,194},{3,195},{4,196},{5,197},{6,198},{7,199},{8... | collective-permute-start | bytes 205208 | tf_op jit(solution)/shard_map/ppermute | solution.py:98
  91.1 0.5 collective-permute-start.10
  91.6 0.1 collective-permute-start.9
  91.8 1.9 %collective-permute-done.11 = f32[4,19,225]{2,1,0:T(8,128)S(1)} collective-permute-done((f32[4,19,225]{2,1,0:T(8,128)S(1)}, f32[4,19,225]{2,1,0:T(8,128)S(1)}, u32[]{:S(2)}, u32[]{:S(2)}) %collective-permute-start.11) | collective-permute-done | bytes 68432 | tf_op jit(solution)/shard_map/ppermute | solution.py:98
  93.7 2.5 %collective-permute-done.10 = f32[4,19,225]{2,1,0:T(8,128)S(1)} collective-permute-done((f32[4,19,225]{2,1,0:T(8,128)S(1)}, f32[4,19,225]{2,1,0:T(8,128)S(1)}, u32[]{:S(2)}, u32[]{:S(2)}) %collective-permute-start.10) | collective-permute-done | bytes 68432 | tf_op jit(solution)/shard_map/ppermute | solution.py:98
  96.2 0.6 gather_fusion.2
  96.8 4.1 %collective-permute-start.12 = (f32[4,4,19,225]{3,2,1,0:T(8,128)S(1)}, f32[4,4,19,225]{3,2,1,0:T(8,128)S(1)}, u32[]{:S(2)}, u32[]{:S(2)}) collective-permute-start(f32[4,4,19,225]{3,2,1,0:T(8,128)S(1)} %gather_fusion.2), channel_id=1, source_target_pairs={{0,8},{1,9},{2,10},{3,11},{4,12},{5,13},{6,14},{7,15},{8,0},{9,1},... | collective-permute-start | bytes 820808 | tf_op jit(solution)/shard_map/ppermute | solution.py:98
  100.9 0.8 select_add_fusion.normal_ref
  101.6 1.6 %pad.22 = f32[232,8,256]{2,1,0:T(8,128)S(1)} pad(f32[225,8,256]{2,1,0:T(8,128)} %bitcast.57, f32[]{:T(128)} %constant.108.clone.1), padding=0_7x0_0x0_0 | pad | bytes 3743748
  103.3 2.1 %copy.16 = f32[29,8,8,256]{3,1,2,0:T(8,128)} copy(f32[29,8,8,256]{3,2,1,0:T(8,128)S(1)} %bitcast.56) | data formatting | bytes 3801088
  105.3 19.6 %sweep.1 = f32[152,256]{1,0:T(8,128)} custom-call(f32[152,256]{1,0:T(8,128)} %select_add_fusion.normal_ref), custom_call_target="tpu_custom_call" | custom-call | flops 30000000 | bytes 300000 | tf_op jit(solution)/shard_map/sweep/pallas_call | solution.py:54
  125.0 1.5 %convolution_convert_fusion = bf16[149,608]{1,0:T(8,128)(2,1)S(1)} fusion(s32[149]{0:T(256)S(1)} %iota_add_fusion.1, s32[608]{0:T(1024)S(1)} %get-tuple-element.8, s32[608]{0:T(1024)S(1)} %get-tuple-element.7, f32[152,256]{1,0:T(8,128)} %sweep.1), kind=kOutput, calls=%fused_computation.8 | convolution fusion | flops 162612640 | bytes 342292 | tf_op jit(solution)/shard_map/dot_general | solution.py:64
  126.7 0.9 reshape.214
  127.6 1.5 %fusion.1 = f32[225,149]{0,1:T(8,128)S(1)} fusion(f32[608,225]{1,0:T(8,128)} %reshape.214, bf16[149,608]{1,0:T(8,128)(2,1)S(1)} %convolution_convert_fusion, s32[225]{0:T(256)S(1)} %copy-done.5, s32[149]{0:T(256)S(1)} %copy-done.4), kind=kOutput, calls=%fused_computation.10 | convolution fusion | flops 244698976 | bytes 863980 | tf_op jit(solution)/shard_map/dot_general | solution.py:152
  129.2 1.6 %fusion.71 = f32[450,149]{1,0:T(8,128)S(1)} fusion(f32[450,225]{1,0:T(8,128)} %constant.132.clone, f32[225,149]{0,1:T(8,128)S(1)} %fusion.1), kind=kOutput, calls=%fused_computation.119 | convolution fusion | flops 181035008 | bytes 807300 | tf_op jit(solution)/shard_map/dot_general | solution.py:161
  130.7 1.0 reshape.216
  131.8 2.5 %copy.15 = bf16[76,8,8,256]{3,1,2,0:T(8,128)(2,1)S(1)} copy(bf16[76,8,8,256]{3,2,1,0:T(8,128)(2,1)} %bitcast.23) | data formatting | bytes 4980736
  134.3 0.7 fusion.70
  135.0 1.0 multiply_reduce_fusion
  136.0 0.5 copy-done.1
  136.5 1.3 fusion
  137.9 0.1 copy.17
  138.0 0.9 slice.19
  138.9 0.6 sqrt.8
  (40 shorter events, 0.4 us)
Async XLA Ops:
  0.6 1.7 %copy-start = (bf16[19,256,256]{2,1,0:T(8,128)(2,1)S(1)}, bf16[19,256,256]{2,1,0:T(8,128)(2,1)}, u32[]{:S(2)}) copy-start(bf16[19,256,256]{2,1,0:T(8,128)(2,1)} %param.6) | copy-start | bytes 7471108
  5.9 21.6 %copy-start.2 = (s32[608,2]{0,1:T(2,128)S(1)}, s32[608,2]{0,1:T(2,128)}, u32[]{:S(2)}) copy-start(s32[608,2]{0,1:T(2,128)} %param.7) | copy-start | bytes 14596
  5.9 125.9 %all-to-all-start = ((bf16[32,19,8,256]{3,2,1,0:T(8,128)(2,1)}), bf16[32,19,8,256]{3,2,1,0:T(8,128)(2,1)}, u32[]{:S(2)}, u32[]{:S(2)}) async-start(bf16[32,19,8,256]{3,2,1,0:T(8,128)(2,1)} %copy_bitcast_fusion), calls=%async_computation | async-start | bytes 4980736 | tf_op jit(solution)/shard_map/all_to_all | solution.py:147
  16.1 13.8 %collective-permute-start.6 = (f32[19,225]{1,0:T(8,128)S(1)}, f32[19,225]{1,0:T(8,128)S(1)}, u32[]{:S(2)}, u32[]{:S(2)}) collective-permute-start(f32[19,225]{1,0:T(8,128)S(1)} %reshape.212), channel_id=1, source_target_pairs={{0,49},{1,48},{2,51},{3,50},{4,53},{5,52},{6,55},{7,54},{8,57},{9,... | collective-permute-start | bytes 51308 | tf_op jit(solution)/shard_map/ppermute | solution.py:98
  20.6 29.7 %collective-permute-start.5 = (f32[19,225]{1,0:T(8,128)S(1)}, f32[19,225]{1,0:T(8,128)S(1)}, u32[]{:S(2)}, u32[]{:S(2)}) collective-permute-start(f32[19,225]{1,0:T(8,128)S(1)} %reshape.212), channel_id=1, source_target_pairs={{0,33},{1,32},{2,35},{3,34},{4,37},{5,36},{6,39},{7,38},{8,41},{9,... | collective-permute-start | bytes 51308 | tf_op jit(solution)/shard_map/ppermute | solution.py:98
  20.8 57.3 %collective-permute-start.4 = (f32[19,225]{1,0:T(8,128)S(1)}, f32[19,225]{1,0:T(8,128)S(1)}, u32[]{:S(2)}, u32[]{:S(2)}) collective-permute-start(f32[19,225]{1,0:T(8,128)S(1)} %reshape.212), channel_id=1, source_target_pairs={{0,17},{1,16},{2,19},{3,18},{4,21},{5,20},{6,23},{7,22},{8,25},{9,... | collective-permute-start | bytes 51308 | tf_op jit(solution)/shard_map/ppermute | solution.py:98
  23.1 55.0 %collective-permute-start.3 = (f32[19,225]{1,0:T(8,128)S(1)}, f32[19,225]{1,0:T(8,128)S(1)}, u32[]{:S(2)}, u32[]{:S(2)}) collective-permute-start(f32[19,225]{1,0:T(8,128)S(1)} %reshape.212), channel_id=1, source_target_pairs={{0,1},{1,0},{2,3},{3,2},{4,5},{5,4},{6,7},{7,6},{8,9},{9,8},{10,11... | collective-permute-start | bytes 51308 | tf_op jit(solution)/shard_map/ppermute | solution.py:98
  26.1 52.7 %collective-permute-start.2 = (f32[19,225]{1,0:T(8,128)S(1)}, f32[19,225]{1,0:T(8,128)S(1)}, u32[]{:S(2)}, u32[]{:S(2)}) collective-permute-start(f32[19,225]{1,0:T(8,128)S(1)} %reshape.212), channel_id=1, source_target_pairs={{0,48},{1,49},{2,50},{3,51},{4,52},{5,53},{6,54},{7,55},{8,56},{9,... | collective-permute-start | bytes 51308 | tf_op jit(solution)/shard_map/ppermute | solution.py:98
  29.9 48.8 %collective-permute-start.1 = (f32[19,225]{1,0:T(8,128)S(1)}, f32[19,225]{1,0:T(8,128)S(1)}, u32[]{:S(2)}, u32[]{:S(2)}) collective-permute-start(f32[19,225]{1,0:T(8,128)S(1)} %reshape.212), channel_id=1, source_target_pairs={{0,32},{1,33},{2,34},{3,35},{4,36},{5,37},{6,38},{7,39},{8,40},{9,... | collective-permute-start | bytes 51308 | tf_op jit(solution)/shard_map/ppermute | solution.py:98
  50.3 28.4 %collective-permute-start = (f32[19,225]{1,0:T(8,128)S(1)}, f32[19,225]{1,0:T(8,128)S(1)}, u32[]{:S(2)}, u32[]{:S(2)}) collective-permute-start(f32[19,225]{1,0:T(8,128)S(1)} %reshape.212), channel_id=1, source_target_pairs={{0,16},{1,17},{2,18},{3,19},{4,20},{5,21},{6,22},{7,23},{8,24},{9,... | collective-permute-start | bytes 51308 | tf_op jit(solution)/shard_map/ppermute | solution.py:98
  79.3 3.9 %collective-permute-start.7 = (f32[4,19,225]{2,1,0:T(8,128)S(1)}, f32[4,19,225]{2,1,0:T(8,128)S(1)}, u32[]{:S(2)}, u32[]{:S(2)}) collective-permute-start(f32[4,19,225]{2,1,0:T(8,128)S(1)} %add.131), channel_id=1, source_target_pairs={{0,2},{1,3},{2,0},{3,1},{4,6},{5,7},{6,4},{7,5},{8,10},{9,11},{10,... | collective-permute-start | bytes 205208 | tf_op jit(solution)/shard_map/ppermute | solution.py:98
  83.3 5.1 %collective-permute-start.8 = (f32[4,19,225]{2,1,0:T(8,128)S(1)}, f32[4,19,225]{2,1,0:T(8,128)S(1)}, u32[]{:S(2)}, u32[]{:S(2)}) collective-permute-start(f32[4,19,225]{2,1,0:T(8,128)S(1)} %add.132), channel_id=1, source_target_pairs={{0,4},{1,5},{2,6},{3,7},{4,0},{5,1},{6,2},{7,3},{8,12},{9,13},{10,... | collective-permute-start | bytes 205208 | tf_op jit(solution)/shard_map/ppermute | solution.py:98
  88.4 5.3 %collective-permute-start.11 = (f32[4,19,225]{2,1,0:T(8,128)S(1)}, f32[4,19,225]{2,1,0:T(8,128)S(1)}, u32[]{:S(2)}, u32[]{:S(2)}) collective-permute-start(f32[4,19,225]{2,1,0:T(8,128)S(1)} %add.133), channel_id=1, source_target_pairs={{0,192},{1,193},{2,194},{3,195},{4,196},{5,197},{6,198},{7,199},{8... | collective-permute-start | bytes 205208 | tf_op jit(solution)/shard_map/ppermute | solution.py:98
  91.1 5.1 %collective-permute-start.10 = (f32[4,19,225]{2,1,0:T(8,128)S(1)}, f32[4,19,225]{2,1,0:T(8,128)S(1)}, u32[]{:S(2)}, u32[]{:S(2)}) collective-permute-start(f32[4,19,225]{2,1,0:T(8,128)S(1)} %add.133), channel_id=1, source_target_pairs={{0,128},{1,129},{2,130},{3,131},{4,132},{5,133},{6,134},{7,135},{8... | collective-permute-start | bytes 205208 | tf_op jit(solution)/shard_map/ppermute | solution.py:98
  91.6 4.5 %collective-permute-start.9 = (f32[4,19,225]{2,1,0:T(8,128)S(1)}, f32[4,19,225]{2,1,0:T(8,128)S(1)}, u32[]{:S(2)}, u32[]{:S(2)}) collective-permute-start(f32[4,19,225]{2,1,0:T(8,128)S(1)} %add.133), channel_id=1, source_target_pairs={{0,64},{1,65},{2,66},{3,67},{4,68},{5,69},{6,70},{7,71},{8,72},{9,... | collective-permute-start | bytes 205208 | tf_op jit(solution)/shard_map/ppermute | solution.py:98
  96.8 29.7 %collective-permute-start.12 = (f32[4,4,19,225]{3,2,1,0:T(8,128)S(1)}, f32[4,4,19,225]{3,2,1,0:T(8,128)S(1)}, u32[]{:S(2)}, u32[]{:S(2)}) collective-permute-start(f32[4,4,19,225]{3,2,1,0:T(8,128)S(1)} %gather_fusion.2), channel_id=1, source_target_pairs={{0,8},{1,9},{2,10},{3,11},{4,12},{5,13},{6,14},{7,15},{8,0},{9,1},... | collective-permute-start | bytes 820808 | tf_op jit(solution)/shard_map/ppermute | solution.py:98
  126.5 1.1 copy-start.4
  126.6 1.1 copy-start.5
  135.0 1.5 %copy-start.1 = (f32[29,8,8,256]{3,1,2,0:T(8,128)S(1)}, f32[29,8,8,256]{3,1,2,0:T(8,128)}, u32[]{:S(2)}) copy-start(f32[29,8,8,256]{3,1,2,0:T(8,128)} %copy.16) | copy-start | bytes 5701636
  135.0 1.5 %copy-start.3 = (f32[225]{0:T(256)S(1)}, f32[225]{0:T(256)}, u32[]{:S(2)}) copy-start(f32[225]{0:T(256)} %constant.133.clone) | copy-start | bytes 2704

commit v3 on v1

v3 whole, which is shorter than its diff:
```python
import math

import jax
import jax.numpy as jnp
import numpy as np
from jax import lax
from jax.experimental import pallas as pl
from jax.experimental.pallas import tpu as pltpu
from jax.sharding import PartitionSpec as P


BAND = 8
FREQS = 2 * BAND - 1
HIGH = lax.Precision.HIGHEST


def design_of(network, solved):
    dates = jnp.arange(1, solved + 1, dtype=jnp.int32)
    return (network[:, 1:2] == dates[None, :]).astype(jnp.float32) - (
        network[:, 0:1] == dates[None, :]
    ).astype(jnp.float32)


def sweep_kernel(normal_ref, out_ref):
    size, width = out_ref.shape
    out_ref[...] = normal_ref[...]
    lane = lax.broadcasted_iota(jnp.int32, (size, width), 1)
    top = lax.broadcasted_iota(jnp.int32, (1, width), 1)

    def pick(row, at):
        return jnp.sum(jnp.where(top == at, row, 0.0), axis=1, keepdims=True)

    def step(i, carry):
        k = 2 * i
        whole = out_ref[...]
        row0 = out_ref[pl.ds(k, 1), :]
        row1 = out_ref[pl.ds(k + 1, 1), :]
        first, second = lane == k, lane == k + 1
        col0 = jnp.sum(jnp.where(first, whole, 0.0), axis=1, keepdims=True)
        col1 = jnp.sum(jnp.where(second, whole, 0.0), axis=1, keepdims=True)
        p, q = pick(row0, k), pick(row0, k + 1)
        t, r = pick(row1, k), pick(row1, k + 1)
        inv = 1.0 / (p * r - q * t)
        row0 = jnp.where(top == k, 1.0, jnp.where(top == k + 1, 0.0, row0))
        row1 = jnp.where(top == k, 0.0, jnp.where(top == k + 1, 1.0, row1))
        new0 = (r * row0 - q * row1) * inv
        new1 = (p * row1 - t * row0) * inv
        rest = jnp.where(first | second, 0.0, whole)
        out_ref[...] = rest - col0 * new0 - col1 * new1
        out_ref[pl.ds(k, 1), :] = new0
        out_ref[pl.ds(k + 1, 1), :] = new1
        return carry

    lax.fori_loop(0, size // 2, step, 0)


def inverse_of(design):
    solved = design.shape[1]
    normal = lax.dot_general(
        design, design, (((0,), (0,)), ((), ())), preferred_element_type=jnp.float32
    )
    size, width = -(-solved // 8) * 8, -(-solved // 128) * 128
    padded = jnp.pad(normal, ((0, size - solved), (0, width - solved)))
    at = jnp.arange(size)
    ones = jnp.where(at >= solved, 1.0, 0.0).astype(jnp.float32)
    padded = padded + jnp.where(at[:, None] == jnp.arange(width)[None, :], ones[:, None], 0.0)
    inverse = pl.pallas_call(
        sweep_kernel,
        out_shape=jax.ShapeDtypeStruct((size, width), jnp.float32),
        in_specs=[pl.BlockSpec(memory_space=pltpu.VMEM)],
        out_specs=pl.BlockSpec(memory_space=pltpu.VMEM),
        cost_estimate=pl.CostEstimate(
            flops=int(3e7), bytes_accessed=300000, transcendentals=0
        ),
        name="sweep",
    )(padded)
    return inverse[:solved, :solved]


def basis(positions, length):
    index = jnp.arange(FREQS, dtype=jnp.int32)
    step = jnp.where(index < BAND, index, index - (BAND - 1))
    turns = positions[:, None] * step[None, :] % length
    angle = turns.astype(jnp.float32) * (2.0 * math.pi / length)
    return jnp.where(index[None, :] < BAND, jnp.cos(angle), jnp.sin(angle))


def mirror():
    out = np.zeros((FREQS, FREQS, 2, FREQS, FREQS), np.float32)
    for k in range(FREQS):
        for l in range(FREQS):
            fk, fl = k - (BAND - 1), l - (BAND - 1)
            ck, cl = abs(fk), abs(fl)
            sk, sl = abs(fk) + BAND - 1, abs(fl) + BAND - 1
            gk, gl = np.sign(fk), np.sign(fl)
            out[k, l, 0, ck, cl] += 1
            if gk * gl:
                out[k, l, 0, sk, sl] -= gk * gl
            if gk:
                out[k, l, 1, sk, cl] -= gk
            if gl:
                out[k, l, 1, ck, sl] -= gl
    return out.reshape(FREQS * FREQS * 2, FREQS * FREQS)


DEVS = 8
STAGED = 8


def permuted(value, move):
    pairs = []
    for g in range(32):
        for d in range(DEVS):
            to_g, to_d = move(g, d)
            pairs.append((g * DEVS + d, to_g * DEVS + to_d))
    return lax.ppermute(value, ("grp", "dev"), pairs)


def over_y(value, k):
    return permuted(value, lambda g, d: (g ^ (k << 3), d))


def over_z(value, k):
    return permuted(value, lambda g, d: (g ^ (k << 1), d))


def over_x(value, k):
    return permuted(value, lambda g, d: (g, d ^ (k << 1)))


def pick(value, at, axis):
    return lax.dynamic_index_in_dim(value, at, axis, keepdims=False)


def on_device(stack, network, bands):
    solved = bands.shape[0]
    grp, dev = lax.axis_index("grp"), lax.axis_index("dev")
    y, z, c, x = grp // 8, grp // 2 % 4, grp % 2, dev // 2
    groups = lax.axis_size("grp")
    held, rows_all, col_dev = stack.shape
    row_dev = rows_all // groups
    cols_all = col_dev * lax.axis_size("dev")
    pixels = row_dev * col_dev
    left = held - STAGED
    modes = FREQS * FREQS

    strips = stack.reshape(held, 4, 4, 2, row_dev, col_dev)
    early = strips[:STAGED]
    planes = [pick(early, z ^ k, 2).transpose(1, 2, 0, 3, 4) for k in range(4)]
    planes[1:] = [over_z(planes[k], k) for k in (1, 2, 3)]

    rows = basis(jnp.arange(rows_all, dtype=jnp.int32), rows_all)
    cols = basis(dev * col_dev + jnp.arange(col_dev, dtype=jnp.int32), cols_all)
    wide = stack.astype(jnp.float32)
    half = jnp.einsum("ihw,ha->iaw", wide, rows, precision=HIGH)
    local = jnp.einsum("iaw,wb->iab", half, cols, precision=HIGH)
    deep = -(-held // 8) * 8
    local = jnp.pad(local.reshape(held, modes), ((0, deep - held), (0, col_dev - modes)))
    local = local + over_x(local, 1)
    local = local + over_x(local, 2)
    near = permuted(local, lambda g, d: (g ^ (d // 2 << 1), d))
    far = permuted(local, lambda g, d: (g ^ (d // 2 << 1), d ^ 1))

    packed = strips[STAGED:].reshape(left, groups, row_dev, col_dev).transpose(1, 0, 2, 3)
    block = lax.all_to_all(packed, "grp", 0, 0, tiled=True)

    design = design_of(network, solved).astype(jnp.bfloat16)
    kc, ky, kz, j = np.meshgrid(
        np.arange(2), np.arange(4), np.arange(4), np.arange(STAGED), indexing="ij"
    )
    order_a = (((y ^ ky) * 4 + (z ^ kz)) * 2 + (c ^ kc)) * held + j
    order_b = np.arange(groups)[:, None] * held + np.arange(STAGED, held)[None, :]
    kc, ky, kr, j = np.meshgrid(
        np.arange(2), np.arange(4), np.arange(4), np.arange(deep), indexing="ij"
    )
    order_f = (((y ^ ky) * 4 + (z ^ x ^ kr)) * 2 + (c ^ kc)) * held + j
    order_f = jnp.where(j < held, order_f, -1)
    order = jnp.concatenate(
        [order_a.reshape(-1), jnp.asarray(order_b.reshape(-1)), order_f.reshape(-1)]
    )
    chosen = (order[:, None] == jnp.arange(held * groups)[None, :]).astype(jnp.bfloat16)
    sorted_design = jnp.dot(chosen, design, preferred_element_type=jnp.float32)
    inverse = inverse_of(design)
    pinv = lax.dot_general(
        inverse, sorted_design, (((1,), (1,)), ((), ())), precision=HIGH
    ).astype(jnp.bfloat16)
    cut_a, cut_b = groups * STAGED, groups * held
    pinv_a, pinv_b, pinv_f = pinv[:, :cut_a], pinv[:, cut_a:cut_b], pinv[:, cut_b:]
    sorted_design = sorted_design.astype(jnp.bfloat16)
    design_a, design_b = sorted_design[:cut_a], sorted_design[cut_a:cut_b]

    total = near + far
    total = jnp.stack([total, over_x(total, 1)])
    total = jnp.concatenate([total, over_x(total, 2)])
    high_part = total.astype(jnp.bfloat16)
    low_part = (total - high_part.astype(jnp.float32)).astype(jnp.bfloat16)
    sums = jnp.stack([high_part, low_part]).reshape(-1, row_dev, col_dev)
    count = sums.shape[0]

    def slabs(value):
        return value.reshape(-1, row_dev, col_dev)

    def toward(k):
        return jnp.stack([pick(p, y ^ k, 0) for p in planes])

    mine = toward(0)
    lines, shared = [mine], [sums]
    for k in (2, 1, 3):
        got = over_y(jnp.concatenate([slabs(toward(k)), sums]), k)
        lines.append(got[:-count].reshape(mine.shape))
        shared.append(got[-count:])
    lines = [lines[0], lines[2], lines[1], lines[3]]
    shared = [shared[0], shared[2], shared[1], shared[3]]
    shared = jnp.stack(shared)
    keep = jnp.stack([pick(p, c, 1) for p in lines])
    give = jnp.stack([pick(p, c ^ 1, 1) for p in lines])
    got = permuted(jnp.concatenate([slabs(give), slabs(shared)]), lambda g, d: (g ^ 1, d))
    part_a = jnp.concatenate([slabs(keep), got[: cut_a // 2]])
    shared = jnp.stack([shared.reshape(4, 2, 4 * deep, col_dev), got[cut_a // 2 :].reshape(4, 2, 4 * deep, col_dev)])

    scale = 1.0 / (rows_all * cols_all)

    def product(piece):
        return lax.dot_general(
            shared[:, :, piece].reshape(-1, col_dev),
            pinv_f,
            (((0,), (1,)), ((), ())),
            preferred_element_type=jnp.float32,
        )[:modes]

    coef = scale * (product(0) + product(1))
    index = np.arange(FREQS)
    step = np.where(index < BAND, index, index - (BAND - 1))
    weight = np.where(step == 0, 1.0, 2.0)
    kmax = np.maximum(step[:, None], step[None, :]).reshape(-1)
    both = (weight[:, None] * weight[None, :]).reshape(-1).astype(np.float32)
    masked = jnp.where(jnp.asarray(kmax)[:, None] < bands[None, :], coef, 0.0)
    signed = jnp.dot(jnp.asarray(mirror()), masked, precision=HIGH)
    spectrum = signed.reshape(FREQS, FREQS, 2, solved).transpose(2, 3, 0, 1)

    row_here = basis(grp * row_dev + jnp.arange(row_dev, dtype=jnp.int32), rows_all)
    waves = row_here.T[:, None, :, None] * cols.T[None, :, None, :]
    waves = waves.reshape(modes, pixels)
    ramp = lax.dot_general(
        masked * jnp.asarray(both)[:, None], waves, (((0,), (0,)), ((), ())), precision=HIGH
    )

    flat_a = part_a.reshape(-1, pixels)
    flat_b = block.reshape(-1, pixels)
    series = jnp.dot(pinv_a, flat_a, preferred_element_type=jnp.float32) + jnp.dot(
        pinv_b, flat_b, preferred_element_type=jnp.float32
    )
    deramped = (series - ramp).astype(jnp.bfloat16).reshape(solved, row_dev, col_dev)
    rounded = series.astype(jnp.bfloat16)
    energy = 0.0
    for flat, some in ((flat_a, design_a), (flat_b, design_b)):
        resid = flat.astype(jnp.float32) - jnp.dot(
            some, rounded, preferred_element_type=jnp.float32
        )
        energy = energy + jnp.sum(resid * resid, axis=0)
    misfit = jnp.sqrt(energy / (held * groups) + 1e-06).reshape(row_dev, col_dev)
    return (deramped, misfit, spectrum)


def solution(mesh):
    return jax.shard_map(
        on_device,
        mesh=mesh,
        in_specs=(P("grp", None, "dev"), P(), P()),
        out_specs=(P(None, "grp", "dev"), P("grp", "dev"), P()),
        check_vma=False,
    )
```

time: 183 us -> 157 us (0.86)
  blocking collectives: 99.7 us -> 0 us
  waiting for transfers between devices: 0.01 us -> 39.5 us
  other arithmetic: 45.4 us -> 8.05 us
  starting transfers between devices: 10.4 us -> 43.5 us
  local copies, waits for them, and re-layouts: 13.4 us -> 32.2 us
  Pallas kernels: 0 us -> 11.5 us
  matrix products: 11 us -> 19.4 us
    all_gather x1 -> x0, blocking collectives: 53.9 us -> none  [on_device(): every = lax.all_gather(summed, 'grp', axis=0, tiled=True)]
    psum x1 -> x0, blocking collectives: 45.8 us -> none  [on_device(): summed = lax.psum(local, 'dev')]
    another operation x13 -> x8, other arithmetic: 44.8 us -> 2.21 us  [the longest x1 1.1 us: on_device(): keep = jnp.stack([pick(p, c, 1) for p in lines])]
    ppermute x0 -> x13, waiting for transfers between devices: none -> 39.5 us  [permuted(): return lax.ppermute(value, ('grp', 'dev'), pairs)]
    ppermute x0 -> x13, starting transfers between devices: none -> 34.9 us  [permuted(): return lax.ppermute(value, ('grp', 'dev'), pairs)]
    pallas_call x0 -> x1, Pallas kernels: none -> 11.5 us  [inverse_of(): pl.pallas_call(sweep_kernel, out_shape=jax.ShapeDtypeStruct((size, width)...]
    slice x0 -> x10, local copies, waits for them, and re-layouts: none -> 9.77 us  [the longest x3 4.65 us: on_device(): shared.append(got[-count:])]
    dot_general x4 -> x9, matrix products: 3.69 us -> 13.2 us  [the longest x2 3 us: on_device(): jnp.dot(some, rounded, preferred_element_type=jnp.float32)]
  transfers between devices with their start and end apart: 1 -> 14, of which waited for: 0 -> 6; matrix products, arithmetic and copies ran while one was open for 32% -> 30% of each run, Pallas kernels for 0% -> 7%
where the time goes in v3:
time: 157 us; the launch traced here: 156 us
  starting transfers between devices  43.5 us (28%)
  waiting for transfers between devices  39.5 us (25%)
  local copies, waits for them, and re-layouts  32.2 us (21%)
  matrix products  19.4 us (12%)
  Pallas kernels  11.5 us (7%)
  other arithmetic  8.05 us (5%)
    ppermute x13, waiting for transfers between devices, permuted(): return lax.ppermute(value, ('grp', 'dev'), pairs)  39.5 us
    ppermute x13, starting transfers between devices, permuted(): return lax.ppermute(value, ('grp', 'dev'), pairs)  34.9 us
    pallas_call x1, Pallas kernels, inverse_of(): pl.pallas_call(sweep_kernel, out_shape=jax.ShapeDtypeStruct((size, width)...  11.5 us
    all_to_all x1, starting transfers between devices, on_device(): block = lax.all_to_all(packed, 'grp', 0, 0, tiled=True)  8.64 us
    unnamed x73, local copies, waits for them, and re-layouts  4.82 us
    slice x3, local copies, waits for them, and re-layouts, on_device(): shared.append(got[-count:])  4.65 us
    dynamic_slice x4, local copies, waits for them, and re-layouts, pick(): return lax.dynamic_index_in_dim(value, at, axis, keepdims=False)  3.87 us
    another operation x4, local copies, waits for them, and re-layouts, on_device(): give = jnp.stack([pick(p, c ^ 1, 1) for p in lines])  3.67 us
  transfers between devices with their start and end apart: 14, of which 6 were waited for; matrix products, arithmetic and copies ran while one was open for 30% of the time, Pallas kernels for 7%

profile of v3, /device:TPU:1, one launch (start us, length us, event | category | flops | bytes accessed | tf_op | source)
XLA Modules:
  0.0 155.6 jit_solution(7299884674553609385)
XLA Ops:
  0.7 3.1 %convolution_bitcast_fusion = f32[19,15,256]{2,1,0:T(8,128)S(1)} fusion(bf16[19,256,256]{2,1,0:T(8,128)(2,1)} %param.16, s32[15]{0:T(128)S(1)} %add_select_fusion.5, pred[15]{0:T(512)(128)(4,1)S(1)} %iota_compare_fusion.3), kind=kOutput, calls=%fused_computation.15 | convolution fusion | flops 224190720 | bytes 2782283 | tf_op jit(solution)/shard_map/ihw,ha->iaw/dot_general | solution.py:155
  5.1 2.0 %collective-permute-start.3 = (f32[24,256]{1,0:T(8,128)}, f32[24,256]{1,0:T(8,128)}, u32[]{:S(2)}, u32[]{:S(2)}) collective-permute-start(f32[24,256]{1,0:T(8,128)} %pad.9), channel_id=1, source_target_pairs={{0,2},{1,3},{2,0},{3,1},{4,6},{5,7},{6,4},{7,5},{8,10},{9,11},{10,... | collective-permute-start | bytes 73736 | tf_op jit(solution)/shard_map/ppermute | solution.py:116
  8.1 3.0 %collective-permute-start.1 = (bf16[4,2,8,8,256]{4,3,1,2,0:T(8,128)(2,1)}, bf16[4,2,8,8,256]{4,3,1,2,0:T(8,128)(2,1)}, u32[]{:S(2)}, u32[]{:S(2)}) collective-permute-start(bf16[4,2,8,8,256]{4,3,1,2,0:T(8,128)(2,1)} %bitcast.117), channel_id=1, source_target_pairs={{0,32},{1,33},{2,34},{3,35},{4,36},{5,37},{6,38},{7,39},{8,40},{9,... | collective-permute-start | bytes 786440 | tf_op jit(solution)/shard_map/ppermute | solution.py:116
  11.9 1.4 collective-permute-start.2
  14.2 1.2 copy_bitcast_fusion
  15.5 8.6 %all-to-all-start = ((bf16[32,11,8,256]{3,2,1,0:T(8,128)(2,1)}), bf16[32,11,8,256]{3,2,1,0:T(8,128)(2,1)S(1)}, u32[]{:S(2)}, u32[]{:S(2)}) async-start(bf16[32,11,8,256]{3,2,1,0:T(8,128)(2,1)} %copy_bitcast_fusion), calls=%async_computation | async-start | bytes 2883584 | tf_op jit(solution)/shard_map/all_to_all | solution.py:165
  25.8 2.4 %collective-permute-start.4 = (f32[24,256]{1,0:T(8,128)S(1)}, f32[24,256]{1,0:T(8,128)S(1)}, u32[]{:S(2)}, u32[]{:S(2)}) collective-permute-start(f32[24,256]{1,0:T(8,128)S(1)} %pad_add_fusion), channel_id=1, source_target_pairs={{0,4},{1,5},{2,6},{3,7},{4,0},{5,1},{6,2},{7,3},{8,12},{9,13},{10,... | collective-permute-start | bytes 73736 | tf_op jit(solution)/shard_map/ppermute | solution.py:116
  28.3 1.7 %collective-permute-done.4 = f32[24,256]{1,0:T(8,128)S(1)} collective-permute-done((f32[24,256]{1,0:T(8,128)S(1)}, f32[24,256]{1,0:T(8,128)S(1)}, u32[]{:S(2)}, u32[]{:S(2)}) %collective-permute-start.4) | collective-permute-done | bytes 24608 | tf_op jit(solution)/shard_map/ppermute | solution.py:116
  30.0 4.7 %collective-permute-start.6 = (f32[24,256]{1,0:T(8,128)S(1)}, f32[24,256]{1,0:T(8,128)S(1)}, u32[]{:S(2)}, u32[]{:S(2)}) collective-permute-start(f32[24,256]{1,0:T(8,128)S(1)} %add.226), channel_id=1, source_target_pairs={{0,1},{1,0},{2,19},{3,18},{4,37},{5,36},{6,55},{7,54},{8,9},{9,8},... | collective-permute-start | bytes 73736 | tf_op jit(solution)/shard_map/ppermute | solution.py:116
  35.6 21.7 %collective-permute-done.6 = f32[24,256]{1,0:T(8,128)S(1)} collective-permute-done((f32[24,256]{1,0:T(8,128)S(1)}, f32[24,256]{1,0:T(8,128)S(1)}, u32[]{:S(2)}, u32[]{:S(2)}) %collective-permute-start.6) | collective-permute-done | bytes 24608 | tf_op jit(solution)/shard_map/ppermute | solution.py:116
  57.3 13.9 %collective-permute-start.7 = (f32[24,256]{1,0:T(8,128)S(1)}, f32[24,256]{1,0:T(8,128)S(1)}, u32[]{:S(2)}, u32[]{:S(2)}) collective-permute-start(f32[24,256]{1,0:T(8,128)S(1)} %add.227), channel_id=1, source_target_pairs={{0,2},{1,3},{2,0},{3,1},{4,6},{5,7},{6,4},{7,5},{8,10},{9,11},{10,... | collective-permute-start | bytes 73736 | tf_op jit(solution)/shard_map/ppermute | solution.py:116
  71.2 2.1 %fusion.88 = (bf16[1376,149]{0,1:T(8,128)(2,1)}, f32[1376,149]{0,1:T(8,128)}) fusion(s32[149]{0:T(256)S(1)} %iota_add_fusion.1, s32[608]{0:T(1024)S(1)} %get-tuple-element.4, s32[608]{0:T(1024)S(1)} %get-tuple-element.3, s32[1376]{0:T(1024)S(1)} %concatenate.54), kind=kOutput, calls=%fused_computation.182 | convolution fusion | flops 250894368 | bytes 1241108 | tf_op jit(solution)/shard_map/dot_general | solution.py:182
  73.5 1.0 dynamic-slice_bitcast_fusion.14
  74.5 3.5 %collective-permute-done.8 = f32[2,24,256]{2,1,0:T(8,128)S(1)} collective-permute-done((f32[2,24,256]{2,1,0:T(8,128)S(1)}, f32[2,24,256]{2,1,0:T(8,128)S(1)}, u32[]{:S(2)}, u32[]{:S(2)}) %collective-permute-start.8) | collective-permute-done | bytes 49184 | tf_op jit(solution)/shard_map/ppermute | solution.py:116
  78.6 1.0 constant_dynamic-slice_fusion.10
  79.6 1.0 constant_dynamic-slice_fusion.9
  80.6 1.0 constant_dynamic-slice_fusion.11
  82.5 1.0 pad_maximum_fusion.4
  83.5 1.3 collective-permute-start.9
  84.8 2.6 %collective-permute-start.10 = (bf16[88,8,256]{2,1,0:T(8,128)(2,1)}, bf16[88,8,256]{2,1,0:T(8,128)(2,1)}, u32[]{:S(2)}, u32[]{:S(2)}) collective-permute-start(bf16[88,8,256]{2,1,0:T(8,128)(2,1)} %get-tuple-element.45), channel_id=1, source_target_pairs={{0,128},{1,129},{2,130},{3,131},{4,132},{5,133},{6,134},{7,135},{8... | collective-permute-start | bytes 1081352 | tf_op jit(solution)/shard_map/ppermute | solution.py:116
  87.4 1.3 fusion.12
  88.7 1.6 %dynamic-slice_bitcast_fusion.6 = (bf16[1,4,8,8,256]{4,3,2,1,0:T(8,128)(2,1)S(1)}, bf16[1,4,8,8,256]{4,3,2,1,0:T(8,128)(2,1)}) fusion(bf16[4,2,8,8,256]{4,3,1,2,0:T(8,128)(2,1)} %get-tuple-element.49, s32[]{:T(128)S(6)} %select_n.196, s32[]{:T(128)S(6)} %select_n.184), kind=kLoop, calls=%fused_computation.60 | loop fusion | bytes 524296 | tf_op jit(solution)/shard_map/stack | solution.py:216
  91.1 1.0 slice.97
  92.1 9.2 %collective-permute-done.10 = bf16[88,8,256]{2,1,0:T(8,128)(2,1)} collective-permute-done((bf16[88,8,256]{2,1,0:T(8,128)(2,1)}, bf16[88,8,256]{2,1,0:T(8,128)(2,1)}, u32[]{:S(2)}, u32[]{:S(2)}) %collective-permute-start.10) | collective-permute-done | bytes 360480 | tf_op jit(solution)/shard_map/ppermute | solution.py:116
  101.3 1.0 slice.98
  103.7 2.6 %collective-permute-done.11 = bf16[88,8,256]{2,1,0:T(8,128)(2,1)} collective-permute-done((bf16[88,8,256]{2,1,0:T(8,128)(2,1)}, bf16[88,8,256]{2,1,0:T(8,128)(2,1)}, u32[]{:S(2)}, u32[]{:S(2)}) %collective-permute-start.11) | collective-permute-done | bytes 360480 | tf_op jit(solution)/shard_map/ppermute | solution.py:116
  106.3 1.0 slice.99
  108.0 1.6 %fusion.85 = (bf16[24,8,256]{2,1,0:T(8,128)(2,1)}, bf16[1,24,8,256]{3,2,1,0:T(8,128)(2,1)S(1)}) fusion(bf16[88,8,256]{2,1,0:T(8,128)(2,1)} %collective-permute-done.9), kind=kLoop, calls=%fused_computation.179 | loop fusion | bytes 294912 | tf_op jit(solution)/shard_map/slice | solution.py:211
  109.6 1.5 fusion.86
  111.1 1.5 fusion.87
  112.7 1.0 pad_maximum_fusion
  113.7 2.6 %collective-permute-start.12 = (bf16[224,8,256]{2,1,0:T(8,128)(2,1)}, bf16[224,8,256]{2,1,0:T(8,128)(2,1)}, u32[]{:S(2)}, u32[]{:S(2)}) collective-permute-start(bf16[224,8,256]{2,1,0:T(8,128)(2,1)} %pad_maximum_fusion), channel_id=1, source_target_pairs={{0,8},{1,9},{2,10},{3,11},{4,12},{5,13},{6,14},{7,15},{8,0},{9,1},... | collective-permute-start | bytes 2752520 | tf_op jit(solution)/shard_map/ppermute | solution.py:116
  117.9 11.5 %sweep.1 = f32[152,256]{1,0:T(8,128)} custom-call(f32[152,256]{1,0:T(8,128)} %select_add_fusion.normal_ref), custom_call_target="tpu_custom_call" | custom-call | flops 30000000 | bytes 300000 | tf_op jit(solution)/shard_map/sweep/pallas_call | solution.py:67
  129.4 2.1 %convolution_convert_fusion = bf16[149,1376]{1,0:T(8,128)(2,1)S(1)} fusion(f32[1376,149]{0,1:T(8,128)} %get-tuple-element.48, f32[152,256]{1,0:T(8,128)} %sweep.1), kind=kOutput, calls=%fused_computation.9 | convolution fusion | flops 366787936 | bytes 1385792 | tf_op jit(solution)/shard_map/dot_general | solution.py:184
  131.6 1.1 subtract_convert_fusion.3
  132.7 1.1 pad_maximum_fusion.5
  134.8 1.1 slice.103
  135.9 0.9 copy.58
  136.8 1.0 slice.105
  139.0 1.3 fusion.89
  140.3 2.1 %reshape.400 = f32[15,15,2,149]{3,2,1,0:T(2,128)} reshape(f32[450,149]{1,0:T(8,128)} %fusion.89) | data formatting | bytes 536400 | tf_op jit(solution)/shard_map/reshape | solution.py:239
  142.4 1.9 %constant_dynamic-update-slice_fusion = bf16[256,2048]{1,0:T(8,128)(2,1)} fusion(bf16[256,2048]{1,0:T(8,128)(2,1)} %constant_dynamic-update-slice_fusion.1, bf16[128,2048]{1,0:T(8,128)(2,1)} %bitcast.130), kind=kLoop, calls=%fused_computation.157 | loop fusion | bytes 1048576 | tf_op jit(solution)/shard_map/concatenate | solution.py:218
  144.3 2.7 %fusion.28 = f32[149,2048]{1,0:T(8,128)} fusion(bf16[256,2048]{1,0:T(8,128)(2,1)} %constant_dynamic-update-slice_fusion, bf16[149,1376]{1,0:T(8,128)(2,1)} %copy-done.4), kind=kOutput, calls=%fused_computation.72 | convolution fusion | flops 156237824 | bytes 2347008 | tf_op jit(solution)/shard_map/dot_general | solution.py:250
  148.2 1.4 convolution_add_fusion
  149.6 1.6 %fusion.5 = f32[2048]{0:T(1024)S(1)} fusion(bf16[352,2048]{1,0:T(8,128)(2,1)S(1)} %bitcast.123, f32[149,2048]{1,0:T(8,128)S(1)} %convolution_add_fusion, bf16[1376,149]{0,1:T(8,128)(2,1)} %get-tuple-element.47), kind=kOutput, calls=%fused_computation.11 | convolution fusion | flops 218013696 | bytes 2787328 | tf_op jit(solution)/shard_map/dot_general | solution.py:257
  151.3 1.4 fusion.6
  153.3 1.3 fusion.3
  154.7 0.9 slice.113
  (132 shorter events, 16.8 us)
Async XLA Ops:
  0.6 6.5 %copy-start = (bf16[19,256,256]{2,1,0:T(8,128)(2,1)S(1)}, bf16[19,256,256]{2,1,0:T(8,128)(2,1)}, u32[]{:S(2)}) copy-start(bf16[19,256,256]{2,1,0:T(8,128)(2,1)} %param.16) | copy-start | bytes 7471108
  0.7 3.1 %copy-start.21 = (pred[15]{0:T(512)(128)(4,1)}, pred[15]{0:T(512)(128)(4,1)S(1)}, u32[]{:S(2)}) copy-start(pred[15]{0:T(512)(128)(4,1)S(1)} %iota_compare_fusion.3) | copy-start | bytes 49
  0.7 3.1 %copy-start.23 = (s32[15]{0:T(128)}, s32[15]{0:T(128)S(1)}, u32[]{:S(2)}) copy-start(s32[15]{0:T(128)S(1)} %add_select_fusion.5) | copy-start | bytes 184
  0.7 3.1 %copy-start.26 = (s32[256]{0:T(256)}, s32[256]{0:T(256)S(1)}, u32[]{:S(2)}) copy-start(s32[256]{0:T(256)S(1)} %iota_add_fusion) | copy-start | bytes 3076
  4.4 2.7 %copy-start.10 = (f32[19,225]{1,0:T(8,128)}, f32[19,225]{1,0:T(8,128)S(1)}, u32[]{:S(2)}) copy-start(f32[19,225]{1,0:T(8,128)S(1)} %reshape.386) | copy-start | bytes 51304
  5.1 20.0 %collective-permute-start.3 = (f32[24,256]{1,0:T(8,128)}, f32[24,256]{1,0:T(8,128)}, u32[]{:S(2)}, u32[]{:S(2)}) collective-permute-start(f32[24,256]{1,0:T(8,128)} %pad.9), channel_id=1, source_target_pairs={{0,2},{1,3},{2,0},{3,1},{4,6},{5,7},{6,4},{7,5},{8,10},{9,11},{10,... | collective-permute-start | bytes 73736 | tf_op jit(solution)/shard_map/ppermute | solution.py:116
  7.2 8.3 %copy-start.2 = (bf16[8,256,256]{2,1,0:T(8,128)(2,1)}, bf16[8,256,256]{2,1,0:T(8,128)(2,1)S(1)}, u32[]{:S(2)}) copy-start(bf16[8,256,256]{2,1,0:T(8,128)(2,1)S(1)} %slice.74) | copy-start | bytes 3145732
  8.1 70.5 %collective-permute-start.1 = (bf16[4,2,8,8,256]{4,3,1,2,0:T(8,128)(2,1)}, bf16[4,2,8,8,256]{4,3,1,2,0:T(8,128)(2,1)}, u32[]{:S(2)}, u32[]{:S(2)}) collective-permute-start(bf16[4,2,8,8,256]{4,3,1,2,0:T(8,128)(2,1)} %bitcast.117), channel_id=1, source_target_pairs={{0,32},{1,33},{2,34},{3,35},{4,36},{5,37},{6,38},{7,39},{8,40},{9,... | collective-permute-start | bytes 786440 | tf_op jit(solution)/shard_map/ppermute | solution.py:116
  11.9 67.7 %collective-permute-start.2 = (bf16[4,2,8,8,256]{4,3,1,2,0:T(8,128)(2,1)}, bf16[4,2,8,8,256]{4,3,1,2,0:T(8,128)(2,1)}, u32[]{:S(2)}, u32[]{:S(2)}) collective-permute-start(bf16[4,2,8,8,256]{4,3,1,2,0:T(8,128)(2,1)} %bitcast.116), channel_id=1, source_target_pairs={{0,48},{1,49},{2,50},{3,51},{4,52},{5,53},{6,54},{7,55},{8,56},{9,... | collective-permute-start | bytes 786440 | tf_op jit(solution)/shard_map/ppermute | solution.py:116
  14.0 66.6 %collective-permute-start = (bf16[4,2,8,8,256]{4,3,1,2,0:T(8,128)(2,1)}, bf16[4,2,8,8,256]{4,3,1,2,0:T(8,128)(2,1)}, u32[]{:S(2)}, u32[]{:S(2)}) collective-permute-start(bf16[4,2,8,8,256]{4,3,1,2,0:T(8,128)(2,1)} %bitcast.118), channel_id=1, source_target_pairs={{0,16},{1,17},{2,18},{3,19},{4,20},{5,21},{6,22},{7,23},{8,24},{9,... | collective-permute-start | bytes 786440 | tf_op jit(solution)/shard_map/ppermute | solution.py:116
  15.5 8.8 %copy-start.22 = (pred[15]{0:T(512)(128)(4,1)S(1)}, pred[15]{0:T(512)(128)(4,1)}, u32[]{:S(2)}) copy-start(pred[15]{0:T(512)(128)(4,1)} %copy-done.21) | copy-start | bytes 49
  15.5 8.8 %copy-start.24 = (s32[15]{0:T(128)S(1)}, s32[15]{0:T(128)}, u32[]{:S(2)}) copy-start(s32[15]{0:T(128)} %copy-done.23) | copy-start | bytes 184
  15.5 8.8 %copy-start.27 = (s32[256]{0:T(256)S(1)}, s32[256]{0:T(256)}, u32[]{:S(2)}) copy-start(s32[256]{0:T(256)} %copy-done.26) | copy-start | bytes 3076
  15.5 9.5 %copy-start.13 = (s32[2,4,4,8]{3,2,1,0:T(4,128)S(1)}, s32[2,4,4,8]{3,2,1,0:T(4,128)}, u32[]{:S(2)}) copy-start(s32[2,4,4,8]{3,2,1,0:T(4,128)} %constant.335.clone) | copy-start | bytes 3076
  15.5 9.5 %copy-start.11 = (f32[19,225]{1,0:T(8,128)S(1)}, f32[19,225]{1,0:T(8,128)}, u32[]{:S(2)}) copy-start(f32[19,225]{1,0:T(8,128)} %copy-done.10) | copy-start | bytes 51304
  15.5 131.4 %all-to-all-start = ((bf16[32,11,8,256]{3,2,1,0:T(8,128)(2,1)}), bf16[32,11,8,256]{3,2,1,0:T(8,128)(2,1)S(1)}, u32[]{:S(2)}, u32[]{:S(2)}) async-start(bf16[32,11,8,256]{3,2,1,0:T(8,128)(2,1)} %copy_bitcast_fusion), calls=%async_computation | async-start | bytes 2883584 | tf_op jit(solution)/shard_map/all_to_all | solution.py:165
  24.2 0.7 copy-start.17
  24.2 0.7 copy-start.18
  24.2 0.7 copy-start.19
  24.2 0.7 copy-start.20
  24.2 0.7 copy-start.28
  24.2 0.7 copy-start.14
  24.2 0.7 copy-start.15
  24.2 0.7 copy-start.16
  24.3 4.0 %copy-start.25 = (s32[608,2]{0,1:T(2,128)S(1)}, s32[608,2]{0,1:T(2,128)}, u32[]{:S(2)}) copy-start(s32[608,2]{0,1:T(2,128)} %param.17) | copy-start | bytes 14596
  24.3 11.2 %copy-start.29 = (s32[352]{0:T(512)S(1)}, s32[352]{0:T(512)}, u32[]{:S(2)}) copy-start(s32[352]{0:T(512)} %constant.341.clone) | copy-start | bytes 4228
  25.8 4.2 %collective-permute-start.4 = (f32[24,256]{1,0:T(8,128)S(1)}, f32[24,256]{1,0:T(8,128)S(1)}, u32[]{:S(2)}, u32[]{:S(2)}) collective-permute-start(f32[24,256]{1,0:T(8,128)S(1)} %pad_add_fusion), channel_id=1, source_target_pairs={{0,4},{1,5},{2,6},{3,7},{4,0},{5,1},{6,2},{7,3},{8,12},{9,13},{10,... | collective-permute-start | bytes 73736 | tf_op jit(solution)/shard_map/ppermute | solution.py:116
  30.0 27.3 %collective-permute-start.6 = (f32[24,256]{1,0:T(8,128)S(1)}, f32[24,256]{1,0:T(8,128)S(1)}, u32[]{:S(2)}, u32[]{:S(2)}) collective-permute-start(f32[24,256]{1,0:T(8,128)S(1)} %add.226), channel_id=1, source_target_pairs={{0,1},{1,0},{2,19},{3,18},{4,37},{5,36},{6,55},{7,54},{8,9},{9,8},... | collective-permute-start | bytes 73736 | tf_op jit(solution)/shard_map/ppermute | solution.py:116
  34.6 22.7 %collective-permute-start.5 = (f32[24,256]{1,0:T(8,128)S(1)}, f32[24,256]{1,0:T(8,128)S(1)}, u32[]{:S(2)}, u32[]{:S(2)}) collective-permute-start(f32[24,256]{1,0:T(8,128)S(1)} %add.226), channel_id=1, source_target_pairs={{0,0},{1,1},{2,18},{3,19},{4,36},{5,37},{6,54},{7,55},{8,8},{9,9},... | collective-permute-start | bytes 73736 | tf_op jit(solution)/shard_map/ppermute | solution.py:116
  57.3 16.1 %collective-permute-start.7 = (f32[24,256]{1,0:T(8,128)S(1)}, f32[24,256]{1,0:T(8,128)S(1)}, u32[]{:S(2)}, u32[]{:S(2)}) collective-permute-start(f32[24,256]{1,0:T(8,128)S(1)} %add.227), channel_id=1, source_target_pairs={{0,2},{1,3},{2,0},{3,1},{4,6},{5,7},{6,4},{7,5},{8,10},{9,11},{10,... | collective-permute-start | bytes 73736 | tf_op jit(solution)/shard_map/ppermute | solution.py:116
  73.4 4.5 %collective-permute-start.8 = (f32[2,24,256]{2,1,0:T(8,128)S(1)}, f32[2,24,256]{2,1,0:T(8,128)S(1)}, u32[]{:S(2)}, u32[]{:S(2)}) collective-permute-start(f32[2,24,256]{2,1,0:T(8,128)S(1)} %pad_maximum_fusion.14), channel_id=1, source_target_pairs={{0,4},{1,5},{2,6},{3,7},{4,0},{5,1},{6,2},{7,3},{8,12},{9,13},{10,... | collective-permute-start | bytes 147464 | tf_op jit(solution)/shard_map/ppermute | solution.py:116
  83.5 7.6 %collective-permute-start.9 = (bf16[88,8,256]{2,1,0:T(8,128)(2,1)}, bf16[88,8,256]{2,1,0:T(8,128)(2,1)}, u32[]{:S(2)}, u32[]{:S(2)}) collective-permute-start(bf16[88,8,256]{2,1,0:T(8,128)(2,1)} %get-tuple-element.44), channel_id=1, source_target_pairs={{0,64},{1,65},{2,66},{3,67},{4,68},{5,69},{6,70},{7,71},{8,72},{9,... | collective-permute-start | bytes 1081352 | tf_op jit(solution)/shard_map/ppermute | solution.py:116
  84.8 16.5 %collective-permute-start.10 = (bf16[88,8,256]{2,1,0:T(8,128)(2,1)}, bf16[88,8,256]{2,1,0:T(8,128)(2,1)}, u32[]{:S(2)}, u32[]{:S(2)}) collective-permute-start(bf16[88,8,256]{2,1,0:T(8,128)(2,1)} %get-tuple-element.45), channel_id=1, source_target_pairs={{0,128},{1,129},{2,130},{3,131},{4,132},{5,133},{6,134},{7,135},{8... | collective-permute-start | bytes 1081352 | tf_op jit(solution)/shard_map/ppermute | solution.py:116
  88.7 17.5 %collective-permute-start.11 = (bf16[88,8,256]{2,1,0:T(8,128)(2,1)}, bf16[88,8,256]{2,1,0:T(8,128)(2,1)}, u32[]{:S(2)}, u32[]{:S(2)}) collective-permute-start(bf16[88,8,256]{2,1,0:T(8,128)(2,1)} %get-tuple-element.46), channel_id=1, source_target_pairs={{0,192},{1,193},{2,194},{3,195},{4,196},{5,197},{6,198},{7,199},{8... | collective-permute-start | bytes 1081352 | tf_op jit(solution)/shard_map/ppermute | solution.py:116
  108.0 8.3 %copy-start.12 = (f32[149,149]{1,0:T(8,128)S(1)}, f32[149,149]{1,0:T(8,128)}, u32[]{:S(2)}) copy-start(f32[149,149]{1,0:T(8,128)} %fusion.12) | copy-start | bytes 266416
  113.7 21.1 %collective-permute-start.12 = (bf16[224,8,256]{2,1,0:T(8,128)(2,1)}, bf16[224,8,256]{2,1,0:T(8,128)(2,1)}, u32[]{:S(2)}, u32[]{:S(2)}) collective-permute-start(bf16[224,8,256]{2,1,0:T(8,128)(2,1)} %pad_maximum_fusion), channel_id=1, source_target_pairs={{0,8},{1,9},{2,10},{3,11},{4,12},{5,13},{6,14},{7,15},{8,0},{9,1},... | collective-permute-start | bytes 2752520 | tf_op jit(solution)/shard_map/ppermute | solution.py:116
  117.9 14.8 %copy-start.5 = (bf16[1,4,8,8,256]{4,3,2,1,0:T(8,128)(2,1)S(1)}, bf16[1,4,8,8,256]{4,3,2,1,0:T(8,128)(2,1)}, u32[]{:S(2)}) copy-start(bf16[1,4,8,8,256]{4,3,2,1,0:T(8,128)(2,1)} %get-tuple-element.23) | copy-start | bytes 393220
  131.6 6.8 %copy-start.4 = (bf16[149,1376]{1,0:T(8,128)(2,1)}, bf16[149,1376]{1,0:T(8,128)(2,1)S(1)}, u32[]{:S(2)}) copy-start(bf16[149,1376]{1,0:T(8,128)(2,1)S(1)} %convolution_convert_fusion) | copy-start | bytes 1230148
  133.9 3.9 %copy-start.7 = (bf16[24,8,256]{2,1,0:T(8,128)(2,1)S(1)}, bf16[24,8,256]{2,1,0:T(8,128)(2,1)}, u32[]{:S(2)}) copy-start(bf16[24,8,256]{2,1,0:T(8,128)(2,1)} %get-tuple-element.16) | copy-start | bytes 294916
  133.9 3.9 %copy-start.8 = (bf16[24,8,256]{2,1,0:T(8,128)(2,1)S(1)}, bf16[24,8,256]{2,1,0:T(8,128)(2,1)}, u32[]{:S(2)}) copy-start(bf16[24,8,256]{2,1,0:T(8,128)(2,1)} %get-tuple-element.18) | copy-start | bytes 294916
  133.9 3.9 %copy-start.9 = (bf16[24,8,256]{2,1,0:T(8,128)(2,1)S(1)}, bf16[24,8,256]{2,1,0:T(8,128)(2,1)}, u32[]{:S(2)}) copy-start(bf16[24,8,256]{2,1,0:T(8,128)(2,1)} %get-tuple-element.20) | copy-start | bytes 294916
  137.8 0.7 copy-start.31
  137.9 0.7 copy-start.32
  138.0 1.0 copy-start.6
  146.9 1.3 copy-start.1
  149.6 1.6 %copy-start.3 = (bf16[256,2048]{1,0:T(8,128)(2,1)S(1)}, bf16[256,2048]{1,0:T(8,128)(2,1)}, u32[]{:S(2)}) copy-start(bf16[256,2048]{1,0:T(8,128)(2,1)} %constant_dynamic-update-slice_fusion) | copy-start | bytes 3145732
  151.3 2.0 %copy-start.30 = (f32[225]{0:T(256)S(1)}, f32[225]{0:T(256)}, u32[]{:S(2)}) copy-start(f32[225]{0:T(256)} %constant.344.clone) | copy-start | bytes 2704

commit v4 on v3

--- a/solution.py
+++ b/solution.py
@@ -104,7 +104,6 @@
 
 
 DEVS = 8
-STAGED = 8
 
 
 def permuted(value, move):
@@ -120,16 +119,8 @@
     return permuted(value, lambda g, d: (g ^ (k << 3), d))
 
 
-def over_z(value, k):
-    return permuted(value, lambda g, d: (g ^ (k << 1), d))
-
-
 def over_x(value, k):
     return permuted(value, lambda g, d: (g, d ^ (k << 1)))
-
-
-def pick(value, at, axis):
-    return lax.dynamic_index_in_dim(value, at, axis, keepdims=False)
 
 
 def on_device(stack, network, bands):
@@ -140,14 +131,15 @@
     held, rows_all, col_dev = stack.shape
     row_dev = rows_all // groups
     cols_all = col_dev * lax.axis_size("dev")
-    pixels = row_dev * col_dev
-    left = held - STAGED
     modes = FREQS * FREQS
-
-    strips = stack.reshape(held, 4, 4, 2, row_dev, col_dev)
-    early = strips[:STAGED]
-    planes = [pick(early, z ^ k, 2).transpose(1, 2, 0, 3, 4) for k in range(4)]
-    planes[1:] = [over_z(planes[k], k) for k in (1, 2, 3)]
+    ifgs = held * groups
+    span = col_dev // 2
+
+    strips = stack.reshape(held, groups, row_dev, col_dev)
+    blocks = []
+    for part in range(2):
+        packed = strips[..., part * span : (part + 1) * span].transpose(1, 0, 2, 3)
+        blocks.append(lax.all_to_all(packed, "grp", 0, 0, tiled=True))
 
     rows = basis(jnp.arange(rows_all, dtype=jnp.int32), rows_all)
     cols = basis(dev * col_dev + jnp.arange(col_dev, dtype=jnp.int32), cols_all)
@@ -161,74 +153,33 @@
     near = permuted(local, lambda g, d: (g ^ (d // 2 << 1), d))
     far = permuted(local, lambda g, d: (g ^ (d // 2 << 1), d ^ 1))
 
-    packed = strips[STAGED:].reshape(left, groups, row_dev, col_dev).transpose(1, 0, 2, 3)
-    block = lax.all_to_all(packed, "grp", 0, 0, tiled=True)
-
     design = design_of(network, solved).astype(jnp.bfloat16)
-    kc, ky, kz, j = np.meshgrid(
-        np.arange(2), np.arange(4), np.arange(4), np.arange(STAGED), indexing="ij"
-    )
-    order_a = (((y ^ ky) * 4 + (z ^ kz)) * 2 + (c ^ kc)) * held + j
-    order_b = np.arange(groups)[:, None] * held + np.arange(STAGED, held)[None, :]
     kc, ky, kr, j = np.meshgrid(
         np.arange(2), np.arange(4), np.arange(4), np.arange(deep), indexing="ij"
     )
-    order_f = (((y ^ ky) * 4 + (z ^ x ^ kr)) * 2 + (c ^ kc)) * held + j
-    order_f = jnp.where(j < held, order_f, -1)
-    order = jnp.concatenate(
-        [order_a.reshape(-1), jnp.asarray(order_b.reshape(-1)), order_f.reshape(-1)]
-    )
-    chosen = (order[:, None] == jnp.arange(held * groups)[None, :]).astype(jnp.bfloat16)
-    sorted_design = jnp.dot(chosen, design, preferred_element_type=jnp.float32)
+    order = (((y ^ ky) * 4 + (z ^ x ^ kr)) * 2 + (c ^ kc)) * held + j
+    order = jnp.where(j < held, order, -1).reshape(-1)
     inverse = inverse_of(design)
     pinv = lax.dot_general(
-        inverse, sorted_design, (((1,), (1,)), ((), ())), precision=HIGH
+        inverse, design.astype(jnp.float32), (((1,), (1,)), ((), ())), precision=HIGH
     ).astype(jnp.bfloat16)
-    cut_a, cut_b = groups * STAGED, groups * held
-    pinv_a, pinv_b, pinv_f = pinv[:, :cut_a], pinv[:, cut_a:cut_b], pinv[:, cut_b:]
-    sorted_design = sorted_design.astype(jnp.bfloat16)
-    design_a, design_b = sorted_design[:cut_a], sorted_design[cut_a:cut_b]
+    chosen = (order[:, None] == jnp.arange(ifgs)[None, :]).astype(jnp.bfloat16)
+    pinv_f = lax.dot_general(
+        chosen, pinv, (((1,), (1,)), ((), ())), preferred_element_type=jnp.float32
+    )
 
     total = near + far
     total = jnp.stack([total, over_x(total, 1)])
-    total = jnp.concatenate([total, over_x(total, 2)])
-    high_part = total.astype(jnp.bfloat16)
-    low_part = (total - high_part.astype(jnp.float32)).astype(jnp.bfloat16)
-    sums = jnp.stack([high_part, low_part]).reshape(-1, row_dev, col_dev)
-    count = sums.shape[0]
-
-    def slabs(value):
-        return value.reshape(-1, row_dev, col_dev)
-
-    def toward(k):
-        return jnp.stack([pick(p, y ^ k, 0) for p in planes])
-
-    mine = toward(0)
-    lines, shared = [mine], [sums]
-    for k in (2, 1, 3):
-        got = over_y(jnp.concatenate([slabs(toward(k)), sums]), k)
-        lines.append(got[:-count].reshape(mine.shape))
-        shared.append(got[-count:])
-    lines = [lines[0], lines[2], lines[1], lines[3]]
-    shared = [shared[0], shared[2], shared[1], shared[3]]
-    shared = jnp.stack(shared)
-    keep = jnp.stack([pick(p, c, 1) for p in lines])
-    give = jnp.stack([pick(p, c ^ 1, 1) for p in lines])
-    got = permuted(jnp.concatenate([slabs(give), slabs(shared)]), lambda g, d: (g ^ 1, d))
-    part_a = jnp.concatenate([slabs(keep), got[: cut_a // 2]])
-    shared = jnp.stack([shared.reshape(4, 2, 4 * deep, col_dev), got[cut_a // 2 :].reshape(4, 2, 4 * deep, col_dev)])
+    total = jnp.concatenate([total, over_x(total, 2)]).reshape(-1, col_dev)
+    lines = [over_y(total, k) for k in (1, 2, 3)]
+    total = jnp.concatenate([total, *lines])
+    other = permuted(total, lambda g, d: (g ^ 1, d))
+    total = jnp.concatenate([total, other])
 
     scale = 1.0 / (rows_all * cols_all)
-
-    def product(piece):
-        return lax.dot_general(
-            shared[:, :, piece].reshape(-1, col_dev),
-            pinv_f,
-            (((0,), (1,)), ((), ())),
-            preferred_element_type=jnp.float32,
-        )[:modes]
-
-    coef = scale * (product(0) + product(1))
+    coef = scale * lax.dot_general(
+        total, pinv_f, (((0,), (0,)), ((), ())), precision=HIGH
+    )[:modes]
     index = np.arange(FREQS)
     step = np.where(index < BAND, index, index - (BAND - 1))
     weight = np.where(step == 0, 1.0, 2.0)
@@ -237,29 +188,25 @@
     masked = jnp.where(jnp.asarray(kmax)[:, None] < bands[None, :], coef, 0.0)
     signed = jnp.dot(jnp.asarray(mirror()), masked, precision=HIGH)
     spectrum = signed.reshape(FREQS, FREQS, 2, solved).transpose(2, 3, 0, 1)
-
+    weighed = masked * jnp.asarray(both)[:, None]
     row_here = basis(grp * row_dev + jnp.arange(row_dev, dtype=jnp.int32), rows_all)
-    waves = row_here.T[:, None, :, None] * cols.T[None, :, None, :]
-    waves = waves.reshape(modes, pixels)
-    ramp = lax.dot_general(
-        masked * jnp.asarray(both)[:, None], waves, (((0,), (0,)), ((), ())), precision=HIGH
-    )
-
-    flat_a = part_a.reshape(-1, pixels)
-    flat_b = block.reshape(-1, pixels)
-    series = jnp.dot(pinv_a, flat_a, preferred_element_type=jnp.float32) + jnp.dot(
-        pinv_b, flat_b, preferred_element_type=jnp.float32
-    )
-    deramped = (series - ramp).astype(jnp.bfloat16).reshape(solved, row_dev, col_dev)
-    rounded = series.astype(jnp.bfloat16)
-    energy = 0.0
-    for flat, some in ((flat_a, design_a), (flat_b, design_b)):
-        resid = flat.astype(jnp.float32) - jnp.dot(
-            some, rounded, preferred_element_type=jnp.float32
+
+    images, misfits = [], []
+    for part, block in enumerate(blocks):
+        here = cols[part * span : (part + 1) * span]
+        waves = row_here.T[:, None, :, None] * here.T[None, :, None, :]
+        ramp = lax.dot_general(
+            weighed, waves.reshape(modes, -1), (((0,), (0,)), ((), ())), precision=HIGH
         )
-        energy = energy + jnp.sum(resid * resid, axis=0)
-    misfit = jnp.sqrt(energy / (held * groups) + 1e-06).reshape(row_dev, col_dev)
-    return (deramped, misfit, spectrum)
+        flat = block.reshape(ifgs, row_dev * span)
+        series = jnp.dot(pinv, flat, preferred_element_type=jnp.float32)
+        image = (series - ramp).astype(jnp.bfloat16)
+        images.append(image.reshape(solved, row_dev, span))
+        model = jnp.dot(design, series.astype(jnp.bfloat16), preferred_element_type=jnp.float32)
+        resid = flat.astype(jnp.float32) - model
+        misfit = jnp.sqrt(jnp.mean(resid * resid, axis=0) + 1e-06)
+        misfits.append(misfit.reshape(row_dev, span))
+    return (jnp.concatenate(images, axis=2), jnp.concatenate(misfits, axis=1), spectrum)
 
 
 def solution(mesh):

time: 157 us -> 101 us (0.64)
  waiting for transfers between devices: 39.5 us -> 17.1 us
  local copies, waits for them, and re-layouts: 32.2 us -> 9.85 us
  starting transfers between devices: 43.5 us -> 39.1 us
  matrix products: 19.4 us -> 16 us
  other arithmetic: 8.05 us -> 5.4 us
    ppermute x13 -> x10, waiting for transfers between devices: 39.5 us -> 13.5 us  [permuted(): return lax.ppermute(value, ('grp', 'dev'), pairs)]
    ppermute x13 -> x10, starting transfers between devices: 34.9 us -> 22.2 us  [permuted(): return lax.ppermute(value, ('grp', 'dev'), pairs)]
    slice x10 -> x1, local copies, waits for them, and re-layouts: 9.77 us -> 1.51 us  [on_device(): packed = strips[..., part * span:(part + 1) * span].transpose(1, 0, 2, 3)]
    all_to_all x1 -> x2, starting transfers between devices: 8.64 us -> 16.9 us  [on_device(): blocks.append(lax.all_to_all(packed, 'grp', 0, 0, tiled=True))]
    dynamic_slice x4 -> x0, local copies, waits for them, and re-layouts: 3.87 us -> none  [pick(): return lax.dynamic_index_in_dim(value, at, axis, keepdims=False)]
    another operation x7 -> x0, local copies, waits for them, and re-layouts: 3.72 us -> none  [the longest x4 3.67 us: on_device(): give = jnp.stack([pick(p, c ^ 1, 1) for p in lines])]
    all_to_all x1 -> x2, waiting for transfers between devices: 0.01 us -> 3.61 us  [on_device(): blocks.append(lax.all_to_all(packed, 'grp', 0, 0, tiled=True))]
    dot_general x9, matrix products: 13.2 us -> 10.5 us  [the longest x2 2.74 us: on_device(): series = jnp.dot(pinv, flat, preferred_element_type=jnp.float32)]
  transfers between devices with their start and end apart: 14 -> 12, of which waited for: 6 -> 6; matrix products, arithmetic and copies ran while one was open for 30% -> 22% of each run, Pallas kernels for 7% -> 11%
where the time goes in v4:
time: 101 us; the launch traced here: 100 us
  starting transfers between devices  39.1 us (39%)
  waiting for transfers between devices  17.1 us (17%)
  matrix products  16 us (16%)
  Pallas kernels  11.4 us (11%)
  local copies, waits for them, and re-layouts  9.85 us (10%)
  other arithmetic  5.4 us (5%)
  between operations  1.11 us (1%)
    ppermute x10, starting transfers between devices, permuted(): return lax.ppermute(value, ('grp', 'dev'), pairs)  22.2 us
    all_to_all x2, starting transfers between devices, on_device(): blocks.append(lax.all_to_all(packed, 'grp', 0, 0, tiled=True))  16.9 us
    ppermute x10, waiting for transfers between devices, permuted(): return lax.ppermute(value, ('grp', 'dev'), pairs)  13.5 us
    pallas_call x1, Pallas kernels, inverse_of(): pl.pallas_call(sweep_kernel, out_shape=jax.ShapeDtypeStruct((size, width)...  11.4 us
    unnamed x46, local copies, waits for them, and re-layouts  5.25 us
    all_to_all x2, waiting for transfers between devices, on_device(): blocks.append(lax.all_to_all(packed, 'grp', 0, 0, tiled=True))  3.61 us
    dot_general x1, matrix products, on_device(): half = jnp.einsum('ihw,ha->iaw', wide, rows, precision=HIGH)  3.05 us
    dot_general x2, matrix products, on_device(): series = jnp.dot(pinv, flat, preferred_element_type=jnp.float32)  2.74 us
  transfers between devices with their start and end apart: 12, of which 6 were waited for; matrix products, arithmetic and copies ran while one was open for 22% of the time, Pallas kernels for 11%

profile of v4, /device:TPU:1, one launch (start us, length us, event | category | flops | bytes accessed | tf_op | source)
XLA Modules:
  0.0 100.0 jit_solution(12861752762605627558)
XLA Ops:
  0.7 3.1 %convolution_bitcast_fusion = f32[19,15,256]{2,1,0:T(8,128)S(1)} fusion(bf16[19,256,256]{2,1,0:T(8,128)(2,1)} %param.11, s32[15]{0:T(128)S(1)} %add_select_fusion.4, pred[15]{0:T(512)(128)(4,1)S(1)} %iota_compare_fusion.3), kind=kOutput, calls=%fused_computation.14 | convolution fusion | flops 224190720 | bytes 2782283 | tf_op jit(solution)/shard_map/ihw,ha->iaw/dot_general | solution.py:147
  3.7 0.5 fusion.38
  4.4 2.1 %collective-permute-start = (f32[24,256]{1,0:T(8,128)S(1)}, f32[24,256]{1,0:T(8,128)S(1)}, u32[]{:S(2)}, u32[]{:S(2)}) collective-permute-start(f32[24,256]{1,0:T(8,128)S(1)} %pad.9), channel_id=1, source_target_pairs={{0,2},{1,3},{2,0},{3,1},{4,6},{5,7},{6,4},{7,5},{8,10},{9,11},{10,... | collective-permute-start | bytes 73736 | tf_op jit(solution)/shard_map/ppermute | solution.py:115
  6.5 1.5 %fusion.67 = (bf16[19,32,8,128]{3,2,1,0:T(8,128)(2,1)S(1)}, bf16[19,32,8,128]{3,2,1,0:T(8,128)(2,1)}) fusion(bf16[19,32,8,256]{3,2,1,0:T(8,128)(2,1)S(1)} %bitcast.63), kind=kLoop, calls=%fused_computation.118 | loop fusion | bytes 4980736 | tf_op jit(solution)/shard_map/slice | solution.py:141
  8.0 1.3 %copy.42 = bf16[19,32,8,128]{3,2,0,1:T(8,128)(2,1)} copy(bf16[19,32,8,128]{3,2,1,0:T(8,128)(2,1)S(1)} %get-tuple-element.5) | data formatting | bytes 2490368
  9.3 9.8 %all-to-all-start = ((bf16[32,19,8,128]{3,2,1,0:T(8,128)(2,1)}), bf16[32,19,8,128]{3,2,1,0:T(8,128)(2,1)S(1)}, u32[]{:S(2)}, u32[]{:S(2)}) async-start(bf16[32,19,8,128]{3,2,1,0:T(8,128)(2,1)} %bitcast.62), calls=%async_computation | async-start | bytes 2490368 | tf_op jit(solution)/shard_map/all_to_all | solution.py:142
  19.2 0.1 sine_select_fusion.1
  19.3 0.2 sine_select_fusion
  19.5 1.1 %broadcast_multiply_fusion.1 = (f32[15,15,8,128]{3,2,1,0:T(8,128)}, f32[15,15,8,128]{3,2,1,0:T(8,128)S(1)}) fusion(f32[15,128]{1,0:T(8,128)S(1)} %get-tuple-element.7, f32[15,8]{1,0:T(8,128)S(1)} %sine_select_fusion.1, f32[15,128]{1,0:T(8,128)S(1)} %get-tuple-element.8), kind=kLoop, calls=%fused_computation.25 | loop fusion | flops 460800 | bytes 1859040 | tf_op jit(solution)/shard_map/mul | solution.py:197
  20.6 0.6 fusion.12
  21.3 2.5 %collective-permute-start.1 = (f32[24,256]{1,0:T(8,128)S(1)}, f32[24,256]{1,0:T(8,128)S(1)}, u32[]{:S(2)}, u32[]{:S(2)}) collective-permute-start(f32[24,256]{1,0:T(8,128)S(1)} %pad_add_fusion), channel_id=1, source_target_pairs={{0,4},{1,5},{2,6},{3,7},{4,0},{5,1},{6,2},{7,3},{8,12},{9,13},{10,... | collective-permute-start | bytes 73736 | tf_op jit(solution)/shard_map/ppermute | solution.py:115
  23.8 2.0 %collective-permute-done.1 = f32[24,256]{1,0:T(8,128)S(1)} collective-permute-done((f32[24,256]{1,0:T(8,128)S(1)}, f32[24,256]{1,0:T(8,128)S(1)}, u32[]{:S(2)}, u32[]{:S(2)}) %collective-permute-start.1) | collective-permute-done | bytes 24608 | tf_op jit(solution)/shard_map/ppermute | solution.py:115
  25.8 0.7 collective-permute-start.2
  26.5 4.3 %collective-permute-start.3 = (f32[24,256]{1,0:T(8,128)S(1)}, f32[24,256]{1,0:T(8,128)S(1)}, u32[]{:S(2)}, u32[]{:S(2)}) collective-permute-start(f32[24,256]{1,0:T(8,128)S(1)} %add.111), channel_id=1, source_target_pairs={{0,1},{1,0},{2,19},{3,18},{4,37},{5,36},{6,55},{7,54},{8,9},{9,8},... | collective-permute-start | bytes 73736 | tf_op jit(solution)/shard_map/ppermute | solution.py:115
  30.8 0.8 select_add_fusion.normal_ref
  31.5 11.4 %sweep.1 = f32[152,256]{1,0:T(8,128)} custom-call(f32[152,256]{1,0:T(8,128)} %select_add_fusion.normal_ref), custom_call_target="tpu_custom_call" | custom-call | flops 30000000 | bytes 300000 | tf_op jit(solution)/shard_map/sweep/pallas_call | solution.py:67
  43.0 2.2 %collective-permute-done.3 = f32[24,256]{1,0:T(8,128)S(1)} collective-permute-done((f32[24,256]{1,0:T(8,128)S(1)}, f32[24,256]{1,0:T(8,128)S(1)}, u32[]{:S(2)}, u32[]{:S(2)}) %collective-permute-start.3) | collective-permute-done | bytes 24608 | tf_op jit(solution)/shard_map/ppermute | solution.py:115
  45.1 7.5 %collective-permute-start.4 = (f32[24,256]{1,0:T(8,128)S(1)}, f32[24,256]{1,0:T(8,128)S(1)}, u32[]{:S(2)}, u32[]{:S(2)}) collective-permute-start(f32[24,256]{1,0:T(8,128)S(1)} %add.112), channel_id=1, source_target_pairs={{0,2},{1,3},{2,0},{3,1},{4,6},{5,7},{6,4},{7,5},{8,10},{9,11},{10,... | collective-permute-start | bytes 73736 | tf_op jit(solution)/shard_map/ppermute | solution.py:115
  52.6 2.1 %convolution_convert_fusion = bf16[149,608]{1,0:T(8,128)(2,1)} fusion(s32[149]{0:T(256)S(1)} %iota_add_fusion.1, s32[608]{0:T(1024)S(1)} %get-tuple-element.4, s32[608]{0:T(1024)S(1)} %get-tuple-element.3, f32[152,256]{1,0:T(8,128)} %sweep.1), kind=kOutput, calls=%fused_computation.15 | convolution fusion | flops 162612640 | bytes 342292 | tf_op jit(solution)/shard_map/dot_general | solution.py:163
  54.7 1.3 %copy.41 = bf16[19,32,8,128]{3,2,0,1:T(8,128)(2,1)} copy(bf16[19,32,8,128]{3,2,1,0:T(8,128)(2,1)S(1)} %copy-done.1) | data formatting | bytes 2490368
  56.2 7.1 %all-to-all-start.1 = ((bf16[32,19,8,128]{3,2,1,0:T(8,128)(2,1)}), bf16[32,19,8,128]{3,2,1,0:T(8,128)(2,1)S(1)}, u32[]{:S(2)}, u32[]{:S(2)}) async-start(bf16[32,19,8,128]{3,2,1,0:T(8,128)(2,1)} %bitcast.66), calls=%async_computation.1 | async-start | bytes 2490368 | tf_op jit(solution)/shard_map/all_to_all | solution.py:142
  63.3 0.8 add_select_fusion.2
  64.2 0.9 pad_maximum_fusion.2
  65.1 1.4 %collective-permute-start.6 = (f32[96,256]{1,0:T(8,128)S(1)}, f32[96,256]{1,0:T(8,128)S(1)}, u32[]{:S(2)}, u32[]{:S(2)}) collective-permute-start(f32[96,256]{1,0:T(8,128)S(1)} %bitcast.79), channel_id=1, source_target_pairs={{0,64},{1,65},{2,66},{3,67},{4,68},{5,69},{6,70},{7,71},{8,72},{9,... | collective-permute-start | bytes 294920 | tf_op jit(solution)/shard_map/ppermute | solution.py:115
  66.5 2.4 %collective-permute-start.7 = (f32[96,256]{1,0:T(8,128)S(1)}, f32[96,256]{1,0:T(8,128)S(1)}, u32[]{:S(2)}, u32[]{:S(2)}) collective-permute-start(f32[96,256]{1,0:T(8,128)S(1)} %bitcast.80), channel_id=1, source_target_pairs={{0,128},{1,129},{2,130},{3,131},{4,132},{5,133},{6,134},{7,135},{8... | collective-permute-start | bytes 294920 | tf_op jit(solution)/shard_map/ppermute | solution.py:115
  69.0 1.5 %fusion = f32[768,149]{1,0:T(8,128)S(1)} fusion(bf16[149,608]{1,0:T(8,128)(2,1)} %convolution_convert_fusion, s32[768]{0:T(1024)S(1)} %eq.76), kind=kOutput, calls=%fused_computation.3 | convolution fusion | flops 139616256 | bytes 641984 | tf_op jit(solution)/shard_map/dot_general | solution.py:167
  70.5 1.1 %copy.24 = f32[29,8,8,128]{3,1,2,0:T(8,128)} copy(f32[29,8,8,128]{3,2,1,0:T(8,128)S(1)} %bitcast.72) | data formatting | bytes 1900544
  71.7 0.2 copy.27
  71.9 2.4 %collective-permute-done.6 = f32[96,256]{1,0:T(8,128)S(1)} collective-permute-done((f32[96,256]{1,0:T(8,128)S(1)}, f32[96,256]{1,0:T(8,128)S(1)}, u32[]{:S(2)}, u32[]{:S(2)}) %collective-permute-start.6) | collective-permute-done | bytes 98336 | tf_op jit(solution)/shard_map/ppermute | solution.py:115
  74.3 5.6 %collective-permute-done.7 = f32[96,256]{1,0:T(8,128)S(1)} collective-permute-done((f32[96,256]{1,0:T(8,128)S(1)}, f32[96,256]{1,0:T(8,128)S(1)}, u32[]{:S(2)}, u32[]{:S(2)}) %collective-permute-start.7) | collective-permute-done | bytes 98336 | tf_op jit(solution)/shard_map/ppermute | solution.py:115
  79.9 1.2 %collective-permute-start.9 = (f32[384,256]{1,0:T(8,128)S(1)}, f32[384,256]{1,0:T(8,128)S(1)}, u32[]{:S(2)}, u32[]{:S(2)}) collective-permute-start(f32[384,256]{1,0:T(8,128)S(1)} %pad_maximum_fusion.1), channel_id=1, source_target_pairs={{0,8},{1,9},{2,10},{3,11},{4,12},{5,13},{6,14},{7,15},{8,0},{9,1},... | collective-permute-start | bytes 1179656 | tf_op jit(solution)/shard_map/ppermute | solution.py:115
  81.2 1.3 %collective-permute-done.9 = f32[384,256]{1,0:T(8,128)S(1)} collective-permute-done((f32[384,256]{1,0:T(8,128)S(1)}, f32[384,256]{1,0:T(8,128)S(1)}, u32[]{:S(2)}, u32[]{:S(2)}) %collective-permute-start.9) | collective-permute-done | bytes 393248 | tf_op jit(solution)/shard_map/ppermute | solution.py:115
  82.6 1.4 %fusion.7 = f32[225,149]{0,1:T(8,128)S(1)} fusion(f32[768,149]{1,0:T(8,128)S(1)} %fusion, f32[768,256]{1,0:T(8,128)S(1)} %constant_dynamic-update-slice_fusion, s32[225]{0:T(256)S(1)} %copy-done.14, s32[149]{0:T(256)S(1)} %copy-done.13), kind=kOutput, calls=%fused_computation.17 | convolution fusion | flops 309066976 | bytes 1379756 | tf_op jit(solution)/shard_map/dot_general | solution.py:180
  84.0 0.6 copy-done.4
  84.7 1.3 %fusion.68 = f32[450,149]{1,0:T(8,128)} fusion(f32[450,225]{1,0:T(8,128)S(1)} %copy-done.8, f32[225,149]{0,1:T(8,128)S(1)} %fusion.7), kind=kOutput, calls=%fused_computation.119 | convolution fusion | flops 181035008 | bytes 807300 | tf_op jit(solution)/shard_map/dot_general | solution.py:189
  86.0 2.1 %reshape.152 = f32[15,15,2,149]{3,2,1,0:T(2,128)} reshape(f32[450,149]{1,0:T(8,128)} %fusion.68) | data formatting | bytes 536400 | tf_op jit(solution)/shard_map/reshape | solution.py:190
  88.1 1.4 %fusion.3 = f32[149,1024]{1,0:T(8,128)S(1)} fusion(bf16[149,608]{1,0:T(8,128)(2,1)} %convolution_convert_fusion, bf16[76,8,8,128]{3,2,1,0:T(8,128)(2,1)S(1)} %bitcast.64), kind=kOutput, calls=%fused_computation.8 | convolution fusion | flops 185532416 | bytes 2036672 | tf_op jit(solution)/shard_map/dot_general | solution.py:202
  89.5 0.7 fusion.5
  90.3 0.7 slice.39
  91.1 0.6 multiply_reduce_fusion.1
  91.7 3.6 %all-to-all-done.1 = bf16[32,19,8,128]{3,2,1,0:T(8,128)(2,1)S(1)} async-done(((bf16[32,19,8,128]{3,2,1,0:T(8,128)(2,1)}), bf16[32,19,8,128]{3,2,1,0:T(8,128)(2,1)S(1)}, u32[]{:S(2)}, u32[]{:S(2)}) %all-to-all-start.1) | async-done | bytes 1245216 | tf_op jit(solution)/shard_map/all_to_all | solution.py:142
  95.3 1.3 %fusion.1 = f32[149,1024]{1,0:T(8,128)S(1)} fusion(bf16[149,608]{1,0:T(8,128)(2,1)} %convolution_convert_fusion, bf16[76,8,8,128]{3,2,1,0:T(8,128)(2,1)S(1)} %bitcast.67), kind=kOutput, calls=%fused_computation.6 | convolution fusion | flops 185532416 | bytes 2036672 | tf_op jit(solution)/shard_map/dot_general | solution.py:202
  96.6 0.6 multiply_reduce_fusion
  97.2 0.3 copy-done.6
  97.5 0.7 fusion.6
  98.4 0.1 copy-done.7
  98.5 0.9 pad_maximum_fusion
  99.4 0.6 pad_maximum_fusion.4
  (66 shorter events, 0.9 us)
Async XLA Ops:
  0.7 5.9 %copy-start = (bf16[19,256,256]{2,1,0:T(8,128)(2,1)S(1)}, bf16[19,256,256]{2,1,0:T(8,128)(2,1)}, u32[]{:S(2)}) copy-start(bf16[19,256,256]{2,1,0:T(8,128)(2,1)} %param.11) | copy-start | bytes 7471108
  4.4 16.8 %collective-permute-start = (f32[24,256]{1,0:T(8,128)S(1)}, f32[24,256]{1,0:T(8,128)S(1)}, u32[]{:S(2)}, u32[]{:S(2)}) collective-permute-start(f32[24,256]{1,0:T(8,128)S(1)} %pad.9), channel_id=1, source_target_pairs={{0,2},{1,3},{2,0},{3,1},{4,6},{5,7},{6,4},{7,5},{8,10},{9,11},{10,... | collective-permute-start | bytes 73736 | tf_op jit(solution)/shard_map/ppermute | solution.py:115
  9.3 9.8 %copy-start.10 = (s32[608,2]{0,1:T(2,128)S(1)}, s32[608,2]{0,1:T(2,128)}, u32[]{:S(2)}) copy-start(s32[608,2]{0,1:T(2,128)} %param.12) | copy-start | bytes 14596
  9.3 46.8 %all-to-all-start = ((bf16[32,19,8,128]{3,2,1,0:T(8,128)(2,1)}), bf16[32,19,8,128]{3,2,1,0:T(8,128)(2,1)S(1)}, u32[]{:S(2)}, u32[]{:S(2)}) async-start(bf16[32,19,8,128]{3,2,1,0:T(8,128)(2,1)} %bitcast.62), calls=%async_computation | async-start | bytes 2490368 | tf_op jit(solution)/shard_map/all_to_all | solution.py:142
  19.1 33.5 %copy-start.15 = (s32[149]{0:T(256)}, s32[149]{0:T(256)S(1)}, u32[]{:S(2)}) copy-start(s32[149]{0:T(256)S(1)} %iota_add_fusion.1) | copy-start | bytes 1792
  20.6 34.1 %copy-start.1 = (bf16[19,32,8,128]{3,2,1,0:T(8,128)(2,1)S(1)}, bf16[19,32,8,128]{3,2,1,0:T(8,128)(2,1)}, u32[]{:S(2)}) copy-start(bf16[19,32,8,128]{3,2,1,0:T(8,128)(2,1)} %get-tuple-element.6) | copy-start | bytes 3735556
  21.3 4.6 %collective-permute-start.1 = (f32[24,256]{1,0:T(8,128)S(1)}, f32[24,256]{1,0:T(8,128)S(1)}, u32[]{:S(2)}, u32[]{:S(2)}) collective-permute-start(f32[24,256]{1,0:T(8,128)S(1)} %pad_add_fusion), channel_id=1, source_target_pairs={{0,4},{1,5},{2,6},{3,7},{4,0},{5,1},{6,2},{7,3},{8,12},{9,13},{10,... | collective-permute-start | bytes 73736 | tf_op jit(solution)/shard_map/ppermute | solution.py:115
  25.8 17.1 %collective-permute-start.2 = (f32[24,256]{1,0:T(8,128)S(1)}, f32[24,256]{1,0:T(8,128)S(1)}, u32[]{:S(2)}, u32[]{:S(2)}) collective-permute-start(f32[24,256]{1,0:T(8,128)S(1)} %add.111), channel_id=1, source_target_pairs={{0,0},{1,1},{2,18},{3,19},{4,36},{5,37},{6,54},{7,55},{8,8},{9,9},... | collective-permute-start | bytes 73736 | tf_op jit(solution)/shard_map/ppermute | solution.py:115
  26.5 18.6 %collective-permute-start.3 = (f32[24,256]{1,0:T(8,128)S(1)}, f32[24,256]{1,0:T(8,128)S(1)}, u32[]{:S(2)}, u32[]{:S(2)}) collective-permute-start(f32[24,256]{1,0:T(8,128)S(1)} %add.111), channel_id=1, source_target_pairs={{0,1},{1,0},{2,19},{3,18},{4,37},{5,36},{6,55},{7,54},{8,9},{9,8},... | collective-permute-start | bytes 73736 | tf_op jit(solution)/shard_map/ppermute | solution.py:115
  45.1 10.9 %collective-permute-start.4 = (f32[24,256]{1,0:T(8,128)S(1)}, f32[24,256]{1,0:T(8,128)S(1)}, u32[]{:S(2)}, u32[]{:S(2)}) collective-permute-start(f32[24,256]{1,0:T(8,128)S(1)} %add.112), channel_id=1, source_target_pairs={{0,2},{1,3},{2,0},{3,1},{4,6},{5,7},{6,4},{7,5},{8,10},{9,11},{10,... | collective-permute-start | bytes 73736 | tf_op jit(solution)/shard_map/ppermute | solution.py:115
  56.0 8.2 %collective-permute-start.5 = (f32[2,24,256]{2,1,0:T(8,128)S(1)}, f32[2,24,256]{2,1,0:T(8,128)}, u32[]{:S(2)}, u32[]{:S(2)}) collective-permute-start(f32[2,24,256]{2,1,0:T(8,128)S(1)} %pad_maximum_fusion.3), channel_id=1, source_target_pairs={{0,4},{1,5},{2,6},{3,7},{4,0},{5,1},{6,2},{7,3},{8,12},{9,13},{10,... | collective-permute-start | bytes 147464 | tf_op jit(solution)/shard_map/ppermute | solution.py:115
  56.1 7.2 %copy-start.9 = (s32[2,4,4,24]{3,2,1,0:T(4,128)S(1)}, s32[2,4,4,24]{3,2,1,0:T(4,128)}, u32[]{:S(2)}) copy-start(s32[2,4,4,24]{3,2,1,0:T(4,128)} %constant.142.clone) | copy-start | bytes 9220
  56.1 7.2 %copy-start.12 = (pred[2,4,4,24]{3,2,1,0:T(4,128)(4,1)S(1)}, pred[2,4,4,24]{3,2,1,0:T(4,128)(4,1)}, u32[]{:S(2)}) copy-start(pred[2,4,4,24]{3,2,1,0:T(4,128)(4,1)} %constant.146.clone) | copy-start | bytes 2308
  56.2 39.1 %all-to-all-start.1 = ((bf16[32,19,8,128]{3,2,1,0:T(8,128)(2,1)}), bf16[32,19,8,128]{3,2,1,0:T(8,128)(2,1)S(1)}, u32[]{:S(2)}, u32[]{:S(2)}) async-start(bf16[32,19,8,128]{3,2,1,0:T(8,128)(2,1)} %bitcast.66), calls=%async_computation.1 | async-start | bytes 2490368 | tf_op jit(solution)/shard_map/all_to_all | solution.py:142
  64.2 6.2 %copy-start.3 = (f32[15,15,8,128]{3,2,1,0:T(8,128)S(1)}, f32[15,15,8,128]{3,2,1,0:T(8,128)}, u32[]{:S(2)}) copy-start(f32[15,15,8,128]{3,2,1,0:T(8,128)} %get-tuple-element.9) | copy-start | bytes 2764804
  65.1 9.2 %collective-permute-start.6 = (f32[96,256]{1,0:T(8,128)S(1)}, f32[96,256]{1,0:T(8,128)S(1)}, u32[]{:S(2)}, u32[]{:S(2)}) collective-permute-start(f32[96,256]{1,0:T(8,128)S(1)} %bitcast.79), channel_id=1, source_target_pairs={{0,64},{1,65},{2,66},{3,67},{4,68},{5,69},{6,70},{7,71},{8,72},{9,... | collective-permute-start | bytes 294920 | tf_op jit(solution)/shard_map/ppermute | solution.py:115
  66.5 13.4 %collective-permute-start.7 = (f32[96,256]{1,0:T(8,128)S(1)}, f32[96,256]{1,0:T(8,128)S(1)}, u32[]{:S(2)}, u32[]{:S(2)}) collective-permute-start(f32[96,256]{1,0:T(8,128)S(1)} %bitcast.80), channel_id=1, source_target_pairs={{0,128},{1,129},{2,130},{3,131},{4,132},{5,133},{6,134},{7,135},{8... | collective-permute-start | bytes 294920 | tf_op jit(solution)/shard_map/ppermute | solution.py:115
  68.9 11.0 %collective-permute-start.8 = (f32[96,256]{1,0:T(8,128)S(1)}, f32[96,256]{1,0:T(8,128)S(1)}, u32[]{:S(2)}, u32[]{:S(2)}) collective-permute-start(f32[96,256]{1,0:T(8,128)S(1)} %bitcast.81), channel_id=1, source_target_pairs={{0,192},{1,193},{2,194},{3,195},{4,196},{5,197},{6,198},{7,199},{8... | collective-permute-start | bytes 294920 | tf_op jit(solution)/shard_map/ppermute | solution.py:115
  71.9 10.7 %copy-start.13 = (s32[149]{0:T(256)S(1)}, s32[149]{0:T(256)}, u32[]{:S(2)}) copy-start(s32[149]{0:T(256)} %param.13) | copy-start | bytes 1792
  71.9 10.7 %copy-start.14 = (s32[225]{0:T(256)S(1)}, s32[225]{0:T(256)}, u32[]{:S(2)}) copy-start(s32[225]{0:T(256)} %constant.147.clone) | copy-start | bytes 2704
  79.9 2.6 %collective-permute-start.9 = (f32[384,256]{1,0:T(8,128)S(1)}, f32[384,256]{1,0:T(8,128)S(1)}, u32[]{:S(2)}, u32[]{:S(2)}) collective-permute-start(f32[384,256]{1,0:T(8,128)S(1)} %pad_maximum_fusion.1), channel_id=1, source_target_pairs={{0,8},{1,9},{2,10},{3,11},{4,12},{5,13},{6,14},{7,15},{8,0},{9,1},... | collective-permute-start | bytes 1179656 | tf_op jit(solution)/shard_map/ppermute | solution.py:115
  81.2 3.5 %copy-start.8 = (f32[450,225]{1,0:T(8,128)S(1)}, f32[450,225]{1,0:T(8,128)}, u32[]{:S(2)}) copy-start(f32[450,225]{1,0:T(8,128)} %constant.148.clone) | copy-start | bytes 1215004
  84.0 0.7 copy-start.4
  88.1 1.4 %copy-start.2 = (f32[29,8,8,128]{3,1,2,0:T(8,128)S(1)}, f32[29,8,8,128]{3,1,2,0:T(8,128)}, u32[]{:S(2)}) copy-start(f32[29,8,8,128]{3,1,2,0:T(8,128)} %copy.24) | copy-start | bytes 2850820
  88.1 1.4 %copy-start.5 = (f32[225,149]{0,1:T(8,128)S(1)}, f32[225,149]{0,1:T(8,128)}, u32[]{:S(2)}) copy-start(f32[225,149]{0,1:T(8,128)} %copy-done.4) | copy-start | bytes 402304
  88.1 1.4 %copy-start.11 = (f32[225]{0:T(256)S(1)}, f32[225]{0:T(256)}, u32[]{:S(2)}) copy-start(f32[225]{0:T(256)} %constant.149.clone) | copy-start | bytes 2704
  89.5 1.6 %copy-start.16 = (s32[149]{0:T(256)S(1)}, s32[149]{0:T(256)}, u32[]{:S(2)}) copy-start(s32[149]{0:T(256)} %copy-done.15) | copy-start | bytes 1792
  96.6 0.9 copy-start.6
  97.5 1.0 copy-start.7

commit v5 on v4

--- a/solution.py
+++ b/solution.py
@@ -1,3 +1,4 @@
+import functools
 import math
 
 import jax
@@ -100,7 +101,7 @@
                 out[k, l, 1, sk, cl] -= gk
             if gl:
                 out[k, l, 1, ck, sl] -= gl
-    return out.reshape(FREQS * FREQS * 2, FREQS * FREQS)
+    return out.transpose(2, 0, 1, 3, 4).reshape(2, FREQS * FREQS, FREQS * FREQS)
 
 
 DEVS = 8
@@ -121,6 +122,31 @@
 
 def over_x(value, k):
     return permuted(value, lambda g, d: (g, d ^ (k << 1)))
+
+
+def pack_kernel(part, strips_ref, out_ref, sems):
+    held, span = out_ref.shape[1], out_ref.shape[3]
+    copies = [
+        pltpu.make_async_copy(
+            strips_ref.at[i, :, :, pl.ds(part * span, span)], out_ref.at[:, i], sems.at[i]
+        )
+        for i in range(held)
+    ]
+    for copy in copies:
+        copy.start()
+    for copy in copies:
+        copy.wait()
+
+
+def pack(strips, part, span):
+    held, groups, row_dev, _ = strips.shape
+    return pl.pallas_call(
+        functools.partial(pack_kernel, part),
+        out_shape=jax.ShapeDtypeStruct((groups, held, row_dev, span), strips.dtype),
+        in_specs=[pl.BlockSpec(memory_space=pl.ANY)],
+        out_specs=pl.BlockSpec(memory_space=pltpu.VMEM),
+        scratch_shapes=[pltpu.SemaphoreType.DMA((held,))],
+    )(strips)
 
 
 def on_device(stack, network, bands):
@@ -138,7 +164,7 @@
     strips = stack.reshape(held, groups, row_dev, col_dev)
     blocks = []
     for part in range(2):
-        packed = strips[..., part * span : (part + 1) * span].transpose(1, 0, 2, 3)
+        packed = pack(strips, part, span)
         blocks.append(lax.all_to_all(packed, "grp", 0, 0, tiled=True))
 
     rows = basis(jnp.arange(rows_all, dtype=jnp.int32), rows_all)
@@ -177,17 +203,15 @@
     total = jnp.concatenate([total, other])
 
     scale = 1.0 / (rows_all * cols_all)
-    coef = scale * lax.dot_general(
-        total, pinv_f, (((0,), (0,)), ((), ())), precision=HIGH
-    )[:modes]
+    coef = scale * lax.dot_general(total, pinv_f, (((0,), (0,)), ((), ())), precision=HIGH)[:modes]
     index = np.arange(FREQS)
     step = np.where(index < BAND, index, index - (BAND - 1))
     weight = np.where(step == 0, 1.0, 2.0)
     kmax = np.maximum(step[:, None], step[None, :]).reshape(-1)
     both = (weight[:, None] * weight[None, :]).reshape(-1).astype(np.float32)
     masked = jnp.where(jnp.asarray(kmax)[:, None] < bands[None, :], coef, 0.0)
-    signed = jnp.dot(jnp.asarray(mirror()), masked, precision=HIGH)
-    spectrum = signed.reshape(FREQS, FREQS, 2, solved).transpose(2, 3, 0, 1)
+    signed = [jnp.dot(jnp.asarray(part), masked, precision=HIGH) for part in mirror()]
+    spectrum = jnp.stack(signed).reshape(2, FREQS, FREQS, solved).transpose(0, 3, 1, 2)
     weighed = masked * jnp.asarray(both)[:, None]
     row_here = basis(grp * row_dev + jnp.arange(row_dev, dtype=jnp.int32), rows_all)
 
@@ -202,7 +226,9 @@
         series = jnp.dot(pinv, flat, preferred_element_type=jnp.float32)
         image = (series - ramp).astype(jnp.bfloat16)
         images.append(image.reshape(solved, row_dev, span))
-        model = jnp.dot(design, series.astype(jnp.bfloat16), preferred_element_type=jnp.float32)
+        model = jnp.dot(
+            design, series.astype(jnp.bfloat16), preferred_element_type=jnp.float32
+        )
         resid = flat.astype(jnp.float32) - model
         misfit = jnp.sqrt(jnp.mean(resid * resid, axis=0) + 1e-06)
         misfits.append(misfit.reshape(row_dev, span))

time: 101 us -> 103 us (1.020)
  Pallas kernels: 11.4 us -> 16.4 us
  local copies, waits for them, and re-layouts: 9.85 us -> 4.98 us
  waiting for transfers between devices: 17.1 us -> 21.4 us
  matrix products: 16 us -> 14.3 us
    pallas_call x0 -> x2, Pallas kernels: none -> 5.01 us  [pack(): pl.pallas_call(functools.partial(pack_kernel, part), out_shape=jax.ShapeD...]
    all_to_all x2, waiting for transfers between devices: 3.61 us -> 7.52 us  [on_device(): blocks.append(lax.all_to_all(packed, 'grp', 0, 0, tiled=True))]
    reshape x1 -> x0, local copies, waits for them, and re-layouts: 2.06 us -> none  [on_device(): spectrum = signed.reshape(FREQS, FREQS, 2, solved).transpose(2, 3, 0, 1)]
    dot_general x2, matrix products: 2.74 us -> 0.8 us  [on_device(): series = jnp.dot(pinv, flat, preferred_element_type=jnp.float32)]
    slice x1 -> x0, local copies, waits for them, and re-layouts: 1.51 us -> none  [on_device(): packed = strips[..., part * span:(part + 1) * span].transpose(1, 0, 2, 3)]
    unnamed x46 -> x39, local copies, waits for them, and re-layouts: 5.25 us -> 4.61 us
  transfers between devices with their start and end apart: 12 -> 12, of which waited for: 6 -> 5; matrix products, arithmetic and copies ran while one was open for 22% -> 15% of each run, Pallas kernels for 11% -> 16%
where the time goes in v5:
time: 103 us; the launch traced here: 102 us
  starting transfers between devices  39 us (38%)
  waiting for transfers between devices  21.4 us (21%)
  Pallas kernels  16.4 us (16%)
  matrix products  14.3 us (14%)
  local copies, waits for them, and re-layouts  4.98 us (5%)
  other arithmetic  4.68 us (5%)
  between operations  1.16 us (1%)
    ppermute x10, starting transfers between devices, permuted(): return lax.ppermute(value, ('grp', 'dev'), pairs)  21.7 us
    all_to_all x2, starting transfers between devices, on_device(): blocks.append(lax.all_to_all(packed, 'grp', 0, 0, tiled=True))  17.4 us
    ppermute x10, waiting for transfers between devices, permuted(): return lax.ppermute(value, ('grp', 'dev'), pairs)  13.9 us
    pallas_call x1, Pallas kernels, inverse_of(): pl.pallas_call(sweep_kernel, out_shape=jax.ShapeDtypeStruct((size, width)...  11.4 us
    all_to_all x2, waiting for transfers between devices, on_device(): blocks.append(lax.all_to_all(packed, 'grp', 0, 0, tiled=True))  7.52 us
    pallas_call x2, Pallas kernels, pack(): pl.pallas_call(functools.partial(pack_kernel, part), out_shape=jax.ShapeD...  5.01 us
    unnamed x39, local copies, waits for them, and re-layouts  4.61 us
    dot_general x1, matrix products, on_device(): half = jnp.einsum('ihw,ha->iaw', wide, rows, precision=HIGH)  2.9 us
  transfers between devices with their start and end apart: 12, of which 5 were waited for; matrix products, arithmetic and copies ran while one was open for 15% of the time, Pallas kernels for 16%

profile of v5, /device:TPU:1, one launch (start us, length us, event | category | flops | bytes accessed | tf_op | source)
XLA Modules:
  0.0 102.0 jit_solution(6762475580689182376)
XLA Ops:
  0.7 2.9 %convolution_bitcast_fusion = f32[19,15,256]{2,1,0:T(8,128)S(1)} fusion(bf16[19,256,256]{2,1,0:T(8,128)(2,1)} %param.12, s32[15]{0:T(128)S(1)} %add_select_fusion.4, pred[15]{0:T(512)(128)(4,1)S(1)} %iota_compare_fusion.3), kind=kOutput, calls=%fused_computation.12 | convolution fusion | flops 224190720 | bytes 2782283 | tf_op jit(solution)/shard_map/ihw,ha->iaw/dot_general | solution.py:173
  3.6 0.5 fusion.38
  4.1 0.1 reshape.149
  4.3 2.1 %collective-permute-start = (f32[24,256]{1,0:T(8,128)S(1)}, f32[24,256]{1,0:T(8,128)S(1)}, u32[]{:S(2)}, u32[]{:S(2)}) collective-permute-start(f32[24,256]{1,0:T(8,128)S(1)} %pad.9), channel_id=1, source_target_pairs={{0,2},{1,3},{2,0},{3,1},{4,6},{5,7},{6,4},{7,5},{8,10},{9,11},{10,... | collective-permute-start | bytes 73736 | tf_op jit(solution)/shard_map/ppermute | solution.py:116
  6.4 2.5 %shard_map.140 = bf16[32,19,8,128]{3,2,1,0:T(8,128)(2,1)} custom-call(bf16[19,32,8,256]{3,2,1,0:T(8,128)(2,1)} %bitcast.60), custom_call_target="tpu_custom_call" | custom-call | tf_op jit(solution)/shard_map/pallas_call | solution.py:143
  8.9 9.7 %all-to-all-start.1 = ((bf16[32,19,8,128]{3,2,1,0:T(8,128)(2,1)}), bf16[32,19,8,128]{3,2,1,0:T(8,128)(2,1)S(1)}, u32[]{:S(2)}, u32[]{:S(2)}) async-start(bf16[32,19,8,128]{3,2,1,0:T(8,128)(2,1)} %shard_map.140), calls=%async_computation.1 | async-start | bytes 2490368 | tf_op jit(solution)/shard_map/all_to_all | solution.py:168
  18.6 0.1 sine_select_fusion.1
  18.8 0.2 sine_select_fusion
  18.9 1.1 %broadcast_multiply_fusion.1 = (f32[15,15,8,128]{3,2,1,0:T(8,128)S(1)}, f32[15,15,8,128]{3,2,1,0:T(8,128)}) fusion(f32[15,128]{1,0:T(8,128)S(1)} %get-tuple-element.8, f32[15,8]{1,0:T(8,128)S(1)} %sine_select_fusion.1, f32[15,128]{1,0:T(8,128)S(1)} %get-tuple-element.9), kind=kLoop, calls=%fused_computation.24 | loop fusion | flops 460800 | bytes 1859040 | tf_op jit(solution)/shard_map/mul | solution.py:221
  20.1 0.6 fusion.12
  20.7 2.5 %collective-permute-start.1 = (f32[24,256]{1,0:T(8,128)S(1)}, f32[24,256]{1,0:T(8,128)S(1)}, u32[]{:S(2)}, u32[]{:S(2)}) collective-permute-start(f32[24,256]{1,0:T(8,128)S(1)} %pad_add_fusion), channel_id=1, source_target_pairs={{0,4},{1,5},{2,6},{3,7},{4,0},{5,1},{6,2},{7,3},{8,12},{9,13},{10,... | collective-permute-start | bytes 73736 | tf_op jit(solution)/shard_map/ppermute | solution.py:116
  23.3 2.0 %collective-permute-done.1 = f32[24,256]{1,0:T(8,128)S(1)} collective-permute-done((f32[24,256]{1,0:T(8,128)S(1)}, f32[24,256]{1,0:T(8,128)S(1)}, u32[]{:S(2)}, u32[]{:S(2)}) %collective-permute-start.1) | collective-permute-done | bytes 24608 | tf_op jit(solution)/shard_map/ppermute | solution.py:116
  25.3 4.2 %collective-permute-start.3 = (f32[24,256]{1,0:T(8,128)S(1)}, f32[24,256]{1,0:T(8,128)S(1)}, u32[]{:S(2)}, u32[]{:S(2)}) collective-permute-start(f32[24,256]{1,0:T(8,128)S(1)} %add.111), channel_id=1, source_target_pairs={{0,1},{1,0},{2,19},{3,18},{4,37},{5,36},{6,55},{7,54},{8,9},{9,8},... | collective-permute-start | bytes 73736 | tf_op jit(solution)/shard_map/ppermute | solution.py:116
  29.5 0.7 collective-permute-start.2
  30.2 0.8 select_add_fusion.normal_ref
  30.9 11.4 %sweep.1 = f32[152,256]{1,0:T(8,128)} custom-call(f32[152,256]{1,0:T(8,128)} %select_add_fusion.normal_ref), custom_call_target="tpu_custom_call" | custom-call | flops 30000000 | bytes 300000 | tf_op jit(solution)/shard_map/sweep/pallas_call | solution.py:68
  42.3 2.2 %collective-permute-done.3 = f32[24,256]{1,0:T(8,128)S(1)} collective-permute-done((f32[24,256]{1,0:T(8,128)S(1)}, f32[24,256]{1,0:T(8,128)S(1)}, u32[]{:S(2)}, u32[]{:S(2)}) %collective-permute-start.3) | collective-permute-done | bytes 24608 | tf_op jit(solution)/shard_map/ppermute | solution.py:116
  44.6 7.5 %collective-permute-start.4 = (f32[24,256]{1,0:T(8,128)S(1)}, f32[24,256]{1,0:T(8,128)S(1)}, u32[]{:S(2)}, u32[]{:S(2)}) collective-permute-start(f32[24,256]{1,0:T(8,128)S(1)} %add.112), channel_id=1, source_target_pairs={{0,2},{1,3},{2,0},{3,1},{4,6},{5,7},{6,4},{7,5},{8,10},{9,11},{10,... | collective-permute-start | bytes 73736 | tf_op jit(solution)/shard_map/ppermute | solution.py:116
  52.1 2.2 %convolution_convert_fusion = bf16[149,608]{1,0:T(8,128)(2,1)} fusion(s32[149]{0:T(256)S(1)} %iota_add_fusion.1, s32[608]{0:T(1024)S(1)} %get-tuple-element.7, s32[608]{0:T(1024)S(1)} %get-tuple-element.6, f32[152,256]{1,0:T(8,128)} %sweep.1), kind=kOutput, calls=%fused_computation.13 | convolution fusion | flops 162612640 | bytes 342292 | tf_op jit(solution)/shard_map/dot_general | solution.py:189
  54.3 0.1 collective-permute-start.5
  54.5 2.5 %shard_map.139 = bf16[32,19,8,128]{3,2,1,0:T(8,128)(2,1)} custom-call(bf16[19,32,8,256]{3,2,1,0:T(8,128)(2,1)} %bitcast.61), custom_call_target="tpu_custom_call" | custom-call | tf_op jit(solution)/shard_map/pallas_call | solution.py:143
  57.0 0.1 eq.76
  57.1 7.7 %all-to-all-start = ((bf16[32,19,8,128]{3,2,1,0:T(8,128)(2,1)}), bf16[32,19,8,128]{3,2,1,0:T(8,128)(2,1)S(1)}, u32[]{:S(2)}, u32[]{:S(2)}) async-start(bf16[32,19,8,128]{3,2,1,0:T(8,128)(2,1)} %shard_map.139), calls=%async_computation | async-start | bytes 2490368 | tf_op jit(solution)/shard_map/all_to_all | solution.py:168
  64.9 0.9 pad_maximum_fusion.2
  65.7 2.6 %collective-permute-start.8 = (f32[96,256]{1,0:T(8,128)S(1)}, f32[96,256]{1,0:T(8,128)S(1)}, u32[]{:S(2)}, u32[]{:S(2)}) collective-permute-start(f32[96,256]{1,0:T(8,128)S(1)} %bitcast.76), channel_id=1, source_target_pairs={{0,192},{1,193},{2,194},{3,195},{4,196},{5,197},{6,198},{7,199},{8... | collective-permute-start | bytes 294920 | tf_op jit(solution)/shard_map/ppermute | solution.py:116
  68.4 0.5 collective-permute-start.7
  68.9 0.1 collective-permute-start.6
  69.0 1.5 %fusion = f32[768,149]{1,0:T(8,128)S(1)} fusion(bf16[149,608]{1,0:T(8,128)(2,1)} %convolution_convert_fusion, s32[768]{0:T(1024)S(1)} %eq.76), kind=kOutput, calls=%fused_computation.3 | convolution fusion | flops 139616256 | bytes 641984 | tf_op jit(solution)/shard_map/dot_general | solution.py:193
  70.6 1.1 %copy.26 = f32[29,8,8,128]{3,1,2,0:T(8,128)} copy(f32[29,8,8,128]{3,2,1,0:T(8,128)S(1)} %bitcast.69) | data formatting | bytes 1900544
  71.8 1.1 %copy.23 = f32[29,8,8,128]{3,1,2,0:T(8,128)} copy(f32[29,8,8,128]{3,2,1,0:T(8,128)S(1)} %bitcast.68) | data formatting | bytes 1900544
  72.9 8.3 %collective-permute-done.8 = f32[96,256]{1,0:T(8,128)S(1)} collective-permute-done((f32[96,256]{1,0:T(8,128)S(1)}, f32[96,256]{1,0:T(8,128)S(1)}, u32[]{:S(2)}, u32[]{:S(2)}) %collective-permute-start.8) | collective-permute-done | bytes 98336 | tf_op jit(solution)/shard_map/ppermute | solution.py:116
  81.2 1.2 %collective-permute-start.9 = (f32[384,256]{1,0:T(8,128)S(1)}, f32[384,256]{1,0:T(8,128)S(1)}, u32[]{:S(2)}, u32[]{:S(2)}) collective-permute-start(f32[384,256]{1,0:T(8,128)S(1)} %pad_maximum_fusion.1), channel_id=1, source_target_pairs={{0,8},{1,9},{2,10},{3,11},{4,12},{5,13},{6,14},{7,15},{8,0},{9,1},... | collective-permute-start | bytes 1179656 | tf_op jit(solution)/shard_map/ppermute | solution.py:116
  82.5 1.3 %collective-permute-done.9 = f32[384,256]{1,0:T(8,128)S(1)} collective-permute-done((f32[384,256]{1,0:T(8,128)S(1)}, f32[384,256]{1,0:T(8,128)S(1)}, u32[]{:S(2)}, u32[]{:S(2)}) %collective-permute-start.9) | collective-permute-done | bytes 393248 | tf_op jit(solution)/shard_map/ppermute | solution.py:116
  83.9 1.4 %fusion.7 = f32[225,149]{0,1:T(8,128)S(1)} fusion(f32[768,149]{1,0:T(8,128)S(1)} %fusion, f32[768,256]{1,0:T(8,128)S(1)} %constant_dynamic-update-slice_fusion, s32[225]{0:T(256)S(1)} %copy-done.13, s32[149]{0:T(256)S(1)} %copy-done.12), kind=kOutput, calls=%fused_computation.15 | convolution fusion | flops 309066976 | bytes 1379756 | tf_op jit(solution)/shard_map/dot_general | solution.py:206
  85.3 0.4 fusion.68
  85.7 1.3 %fusion.67 = f32[225,149]{1,0:T(8,128)S(1)} fusion(f32[225,225]{1,0:T(8,128)} %constant.150.clone, f32[225,149]{0,1:T(8,128)S(1)} %fusion.7), kind=kOutput, calls=%fused_computation.117 | convolution fusion | flops 90517504 | bytes 470700 | tf_op jit(solution)/shard_map/dot_general | solution.py:213
  87.2 1.1 %copy.19 = f32[2,149,15,15]{1,0,3,2:T(2,128)} copy(f32[2,149,15,15]{1,3,2,0:T(8,128)S(1)} %maximum_bitcast_fusion) | data formatting | bytes 536400
  88.3 0.4 fusion.1
  88.7 0.6 multiply_reduce_fusion
  89.3 7.5 %all-to-all-done = bf16[32,19,8,128]{3,2,1,0:T(8,128)(2,1)S(1)} async-done(((bf16[32,19,8,128]{3,2,1,0:T(8,128)(2,1)}), bf16[32,19,8,128]{3,2,1,0:T(8,128)(2,1)S(1)}, u32[]{:S(2)}, u32[]{:S(2)}) %all-to-all-start) | async-done | bytes 1245216 | tf_op jit(solution)/shard_map/all_to_all | solution.py:168
  96.8 0.4 fusion.3
  97.3 0.6 multiply_reduce_fusion.1
  97.9 0.6 copy-done.1
  98.4 0.8 fusion.6
  99.3 0.3 copy-done
  99.6 0.7 fusion.5
  100.5 0.6 pad_maximum_fusion.4
  101.1 0.9 pad_maximum_fusion
  (63 shorter events, 0.7 us)
Async XLA Ops:
  4.3 16.4 %collective-permute-start = (f32[24,256]{1,0:T(8,128)S(1)}, f32[24,256]{1,0:T(8,128)S(1)}, u32[]{:S(2)}, u32[]{:S(2)}) collective-permute-start(f32[24,256]{1,0:T(8,128)S(1)} %pad.9), channel_id=1, source_target_pairs={{0,2},{1,3},{2,0},{3,1},{4,6},{5,7},{6,4},{7,5},{8,10},{9,11},{10,... | collective-permute-start | bytes 73736 | tf_op jit(solution)/shard_map/ppermute | solution.py:116
  8.9 9.7 %copy-start.9 = (s32[608,2]{0,1:T(2,128)S(1)}, s32[608,2]{0,1:T(2,128)}, u32[]{:S(2)}) copy-start(s32[608,2]{0,1:T(2,128)} %param.13) | copy-start | bytes 14596
  8.9 48.2 %all-to-all-start.1 = ((bf16[32,19,8,128]{3,2,1,0:T(8,128)(2,1)}), bf16[32,19,8,128]{3,2,1,0:T(8,128)(2,1)S(1)}, u32[]{:S(2)}, u32[]{:S(2)}) async-start(bf16[32,19,8,128]{3,2,1,0:T(8,128)(2,1)} %shard_map.140), calls=%async_computation.1 | async-start | bytes 2490368 | tf_op jit(solution)/shard_map/all_to_all | solution.py:168
  20.0 34.4 %copy-start.5 = (s32[2,4,4,24]{3,2,1,0:T(4,128)S(1)}, s32[2,4,4,24]{3,2,1,0:T(4,128)}, u32[]{:S(2)}) copy-start(s32[2,4,4,24]{3,2,1,0:T(4,128)} %constant.147.clone) | copy-start | bytes 9220
  20.0 34.4 %copy-start.6 = (s32[2,4,4,24]{3,2,1,0:T(4,128)S(1)}, s32[2,4,4,24]{3,2,1,0:T(4,128)}, u32[]{:S(2)}) copy-start(s32[2,4,4,24]{3,2,1,0:T(4,128)} %constant.146.clone) | copy-start | bytes 9220
  20.0 34.4 %copy-start.7 = (s32[2,4,4,24]{3,2,1,0:T(4,128)S(1)}, s32[2,4,4,24]{3,2,1,0:T(4,128)}, u32[]{:S(2)}) copy-start(s32[2,4,4,24]{3,2,1,0:T(4,128)} %constant.145.clone) | copy-start | bytes 9220
  20.0 34.4 %copy-start.8 = (s32[2,4,4,24]{3,2,1,0:T(4,128)S(1)}, s32[2,4,4,24]{3,2,1,0:T(4,128)}, u32[]{:S(2)}) copy-start(s32[2,4,4,24]{3,2,1,0:T(4,128)} %constant.144.clone) | copy-start | bytes 9220
  20.0 34.4 %copy-start.11 = (pred[2,4,4,24]{3,2,1,0:T(4,128)(4,1)S(1)}, pred[2,4,4,24]{3,2,1,0:T(4,128)(4,1)}, u32[]{:S(2)}) copy-start(pred[2,4,4,24]{3,2,1,0:T(4,128)(4,1)} %constant.148.clone) | copy-start | bytes 2308
  20.7 4.6 %collective-permute-start.1 = (f32[24,256]{1,0:T(8,128)S(1)}, f32[24,256]{1,0:T(8,128)S(1)}, u32[]{:S(2)}, u32[]{:S(2)}) collective-permute-start(f32[24,256]{1,0:T(8,128)S(1)} %pad_add_fusion), channel_id=1, source_target_pairs={{0,4},{1,5},{2,6},{3,7},{4,0},{5,1},{6,2},{7,3},{8,12},{9,13},{10,... | collective-permute-start | bytes 73736 | tf_op jit(solution)/shard_map/ppermute | solution.py:116
  25.3 19.3 %collective-permute-start.3 = (f32[24,256]{1,0:T(8,128)S(1)}, f32[24,256]{1,0:T(8,128)S(1)}, u32[]{:S(2)}, u32[]{:S(2)}) collective-permute-start(f32[24,256]{1,0:T(8,128)S(1)} %add.111), channel_id=1, source_target_pairs={{0,1},{1,0},{2,19},{3,18},{4,37},{5,36},{6,55},{7,54},{8,9},{9,8},... | collective-permute-start | bytes 73736 | tf_op jit(solution)/shard_map/ppermute | solution.py:116
  29.5 15.1 %collective-permute-start.2 = (f32[24,256]{1,0:T(8,128)S(1)}, f32[24,256]{1,0:T(8,128)S(1)}, u32[]{:S(2)}, u32[]{:S(2)}) collective-permute-start(f32[24,256]{1,0:T(8,128)S(1)} %add.111), channel_id=1, source_target_pairs={{0,0},{1,1},{2,18},{3,19},{4,36},{5,37},{6,54},{7,55},{8,8},{9,9},... | collective-permute-start | bytes 73736 | tf_op jit(solution)/shard_map/ppermute | solution.py:116
  44.6 9.7 %collective-permute-start.4 = (f32[24,256]{1,0:T(8,128)S(1)}, f32[24,256]{1,0:T(8,128)S(1)}, u32[]{:S(2)}, u32[]{:S(2)}) collective-permute-start(f32[24,256]{1,0:T(8,128)S(1)} %add.112), channel_id=1, source_target_pairs={{0,2},{1,3},{2,0},{3,1},{4,6},{5,7},{6,4},{7,5},{8,10},{9,11},{10,... | collective-permute-start | bytes 73736 | tf_op jit(solution)/shard_map/ppermute | solution.py:116
  54.3 10.5 %collective-permute-start.5 = (f32[2,24,256]{2,1,0:T(8,128)S(1)}, f32[2,24,256]{2,1,0:T(8,128)}, u32[]{:S(2)}, u32[]{:S(2)}) collective-permute-start(f32[2,24,256]{2,1,0:T(8,128)S(1)} %pad_maximum_fusion.3), channel_id=1, source_target_pairs={{0,4},{1,5},{2,6},{3,7},{4,0},{5,1},{6,2},{7,3},{8,12},{9,13},{10,... | collective-permute-start | bytes 147464 | tf_op jit(solution)/shard_map/ppermute | solution.py:116
  57.1 39.7 %all-to-all-start = ((bf16[32,19,8,128]{3,2,1,0:T(8,128)(2,1)}), bf16[32,19,8,128]{3,2,1,0:T(8,128)(2,1)S(1)}, u32[]{:S(2)}, u32[]{:S(2)}) async-start(bf16[32,19,8,128]{3,2,1,0:T(8,128)(2,1)} %shard_map.139), calls=%async_computation | async-start | bytes 2490368 | tf_op jit(solution)/shard_map/all_to_all | solution.py:168
  64.8 5.7 %copy-start.2 = (f32[15,15,8,128]{3,2,1,0:T(8,128)S(1)}, f32[15,15,8,128]{3,2,1,0:T(8,128)}, u32[]{:S(2)}) copy-start(f32[15,15,8,128]{3,2,1,0:T(8,128)} %get-tuple-element.11) | copy-start | bytes 2764804
  65.7 15.5 %collective-permute-start.8 = (f32[96,256]{1,0:T(8,128)S(1)}, f32[96,256]{1,0:T(8,128)S(1)}, u32[]{:S(2)}, u32[]{:S(2)}) collective-permute-start(f32[96,256]{1,0:T(8,128)S(1)} %bitcast.76), channel_id=1, source_target_pairs={{0,192},{1,193},{2,194},{3,195},{4,196},{5,197},{6,198},{7,199},{8... | collective-permute-start | bytes 294920 | tf_op jit(solution)/shard_map/ppermute | solution.py:116
  68.4 12.8 %collective-permute-start.7 = (f32[96,256]{1,0:T(8,128)S(1)}, f32[96,256]{1,0:T(8,128)S(1)}, u32[]{:S(2)}, u32[]{:S(2)}) collective-permute-start(f32[96,256]{1,0:T(8,128)S(1)} %bitcast.77), channel_id=1, source_target_pairs={{0,128},{1,129},{2,130},{3,131},{4,132},{5,133},{6,134},{7,135},{8... | collective-permute-start | bytes 294920 | tf_op jit(solution)/shard_map/ppermute | solution.py:116
  68.9 12.3 %collective-permute-start.6 = (f32[96,256]{1,0:T(8,128)S(1)}, f32[96,256]{1,0:T(8,128)S(1)}, u32[]{:S(2)}, u32[]{:S(2)}) collective-permute-start(f32[96,256]{1,0:T(8,128)S(1)} %bitcast.78), channel_id=1, source_target_pairs={{0,64},{1,65},{2,66},{3,67},{4,68},{5,69},{6,70},{7,71},{8,72},{9,... | collective-permute-start | bytes 294920 | tf_op jit(solution)/shard_map/ppermute | solution.py:116
  72.9 11.0 %copy-start.12 = (s32[149]{0:T(256)S(1)}, s32[149]{0:T(256)}, u32[]{:S(2)}) copy-start(s32[149]{0:T(256)} %param.14) | copy-start | bytes 1792
  72.9 11.0 %copy-start.13 = (s32[225]{0:T(256)S(1)}, s32[225]{0:T(256)}, u32[]{:S(2)}) copy-start(s32[225]{0:T(256)} %constant.149.clone) | copy-start | bytes 2704
  81.2 2.6 %collective-permute-start.9 = (f32[384,256]{1,0:T(8,128)S(1)}, f32[384,256]{1,0:T(8,128)S(1)}, u32[]{:S(2)}, u32[]{:S(2)}) collective-permute-start(f32[384,256]{1,0:T(8,128)S(1)} %pad_maximum_fusion.1), channel_id=1, source_target_pairs={{0,8},{1,9},{2,10},{3,11},{4,12},{5,13},{6,14},{7,15},{8,0},{9,1},... | collective-permute-start | bytes 1179656 | tf_op jit(solution)/shard_map/ppermute | solution.py:116
  82.5 2.8 %copy-start.4 = (f32[225,225]{1,0:T(8,128)S(1)}, f32[225,225]{1,0:T(8,128)}, u32[]{:S(2)}) copy-start(f32[225,225]{1,0:T(8,128)} %constant.151.clone) | copy-start | bytes 607504
  87.1 1.2 %copy-start.3 = (bf16[149,608]{1,0:T(8,128)(2,1)S(1)}, bf16[149,608]{1,0:T(8,128)(2,1)}, u32[]{:S(2)}) copy-start(bf16[149,608]{1,0:T(8,128)(2,1)} %convolution_convert_fusion) | copy-start | bytes 543556
  97.2 1.2 %copy-start.1 = (f32[29,8,8,128]{3,1,2,0:T(8,128)S(1)}, f32[29,8,8,128]{3,1,2,0:T(8,128)}, u32[]{:S(2)}) copy-start(f32[29,8,8,128]{3,1,2,0:T(8,128)} %copy.26) | copy-start | bytes 2850820
  97.2 1.2 %copy-start.10 = (f32[225]{0:T(256)S(1)}, f32[225]{0:T(256)}, u32[]{:S(2)}) copy-start(f32[225]{0:T(256)} %constant.152.clone) | copy-start | bytes 2704
  98.4 1.2 %copy-start = (f32[29,8,8,128]{3,1,2,0:T(8,128)S(1)}, f32[29,8,8,128]{3,1,2,0:T(8,128)}, u32[]{:S(2)}) copy-start(f32[29,8,8,128]{3,1,2,0:T(8,128)} %copy.23) | copy-start | bytes 2850820

commit v6 on v4

--- a/solution.py
+++ b/solution.py
@@ -119,8 +119,39 @@
     return permuted(value, lambda g, d: (g ^ (k << 3), d))
 
 
+def over_z(value, k):
+    return permuted(value, lambda g, d: (g ^ (k << 1), d))
+
+
 def over_x(value, k):
     return permuted(value, lambda g, d: (g, d ^ (k << 1)))
+
+
+HBM = pl.BlockSpec(memory_space=pl.ANY)
+
+
+def copied(plan, scalars, arrays, shapes):
+    def body(*refs):
+        some, rest = refs[: len(scalars)], refs[len(scalars) :]
+        ins, outs, sem = rest[: len(arrays)], rest[len(arrays) : -1], rest[-1]
+        pairs = plan([ref[0] for ref in some], ins, outs)
+        copies = [
+            pltpu.make_async_copy(source, target, sem.at[i])
+            for i, (source, target) in enumerate(pairs)
+        ]
+        for copy in copies:
+            copy.start()
+        for copy in copies:
+            copy.wait()
+
+    return pl.pallas_call(
+        body,
+        out_shape=[jax.ShapeDtypeStruct(shape, arrays[0].dtype) for shape in shapes],
+        in_specs=[pl.BlockSpec(memory_space=pltpu.SMEM)] * len(scalars)
+        + [HBM] * len(arrays),
+        out_specs=[HBM] * len(shapes),
+        scratch_shapes=[pltpu.SemaphoreType.DMA((32,))],
+    )(*[jnp.reshape(v, (1,)) for v in scalars], *arrays)
 
 
 def on_device(stack, network, bands):
@@ -134,12 +165,22 @@
     modes = FREQS * FREQS
     ifgs = held * groups
     span = col_dev // 2
-
-    strips = stack.reshape(held, groups, row_dev, col_dev)
-    blocks = []
-    for part in range(2):
-        packed = strips[..., part * span : (part + 1) * span].transpose(1, 0, 2, 3)
-        blocks.append(lax.all_to_all(packed, "grp", 0, 0, tiled=True))
+    tile = (row_dev, span)
+    quad = 4 * held
+
+    strips = stack.reshape(held, 4, 4, 2, row_dev, col_dev)
+
+    def plane_plan(scalars, ins, outs):
+        return [
+            (ins[0].at[:, i, scalars[0] ^ k, j, :, pl.ds(0, span)], outs[k].at[i, j])
+            for k in range(4)
+            for i in range(4)
+            for j in range(2)
+        ]
+
+    planes = copied(plane_plan, [z], [strips], [(4, 2, held, *tile)] * 4)
+    planes = list(planes)
+    planes[1:] = [over_z(planes[k], k) for k in (1, 2, 3)]
 
     rows = basis(jnp.arange(rows_all, dtype=jnp.int32), rows_all)
     cols = basis(dev * col_dev + jnp.arange(col_dev, dtype=jnp.int32), cols_all)
@@ -153,33 +194,88 @@
     near = permuted(local, lambda g, d: (g ^ (d // 2 << 1), d))
     far = permuted(local, lambda g, d: (g ^ (d // 2 << 1), d ^ 1))
 
+    def bulk_plan(scalars, ins, outs):
+        return [
+            (ins[0].at[i, :, :, pl.ds(span, span)], outs[0].at[:, i]) for i in range(held)
+        ]
+
+    (packed,) = copied(
+        bulk_plan, [], [stack.reshape(held, groups, row_dev, col_dev)], [(groups, held, *tile)]
+    )
+    block = lax.all_to_all(packed, "grp", 0, 0, tiled=True)
+
     design = design_of(network, solved).astype(jnp.bfloat16)
-    kc, ky, kr, j = np.meshgrid(
-        np.arange(2), np.arange(4), np.arange(4), np.arange(deep), indexing="ij"
-    )
-    order = (((y ^ ky) * 4 + (z ^ x ^ kr)) * 2 + (c ^ kc)) * held + j
-    order = jnp.where(j < held, order, -1).reshape(-1)
+
+    def arrival(plane, depth):
+        kc, ky, kz, j = np.meshgrid(
+            np.arange(2), np.arange(4), np.arange(4), np.arange(depth), indexing="ij"
+        )
+        order = (((y ^ ky) * 4 + (plane ^ kz)) * 2 + (c ^ kc)) * held + j
+        return jnp.where(j < held, order, -1).reshape(-1)
+
+    def one_hot(order):
+        return (order[:, None] == jnp.arange(ifgs)[None, :]).astype(jnp.bfloat16)
+
+    design_a = jnp.dot(
+        one_hot(arrival(z, held)), design, preferred_element_type=jnp.float32
+    ).astype(jnp.bfloat16)
     inverse = inverse_of(design)
-    pinv = lax.dot_general(
-        inverse, design.astype(jnp.float32), (((1,), (1,)), ((), ())), precision=HIGH
-    ).astype(jnp.bfloat16)
-    chosen = (order[:, None] == jnp.arange(ifgs)[None, :]).astype(jnp.bfloat16)
+    pinv, pinv_a = (
+        lax.dot_general(
+            inverse, some.astype(jnp.float32), (((1,), (1,)), ((), ())), precision=HIGH
+        ).astype(jnp.bfloat16)
+        for some in (design, design_a)
+    )
     pinv_f = lax.dot_general(
-        chosen, pinv, (((1,), (1,)), ((), ())), preferred_element_type=jnp.float32
+        one_hot(arrival(z ^ x, deep)),
+        pinv,
+        (((1,), (1,)), ((), ())),
+        preferred_element_type=jnp.float32,
     )
 
     total = near + far
     total = jnp.stack([total, over_x(total, 1)])
-    total = jnp.concatenate([total, over_x(total, 2)]).reshape(-1, col_dev)
-    lines = [over_y(total, k) for k in (1, 2, 3)]
-    total = jnp.concatenate([total, *lines])
-    other = permuted(total, lambda g, d: (g ^ 1, d))
-    total = jnp.concatenate([total, other])
-
+    total = jnp.concatenate([total, over_x(total, 2)]).reshape(4 * deep, 2, span)
+    total = total.transpose(1, 0, 2)
+    top = lax.reduce_precision(total, 8, 7)
+    sums = jnp.stack([top, total - top]).astype(jnp.bfloat16).reshape(-1, *tile)
+    count = sums.shape[0]
+
+    def line_plan(scalars, ins, outs):
+        pairs = [
+            (ins[kz].at[scalars[0] ^ k, j], outs[k].at[pl.ds(j * quad + kz * held, held)])
+            for k in range(4)
+            for kz in range(4)
+            for j in range(2)
+        ]
+        return pairs
+
+    lines = copied(line_plan, [y], planes, [(2 * quad, *tile)] * 4)
+    lines = [jnp.concatenate([line, sums]) for line in lines]
+    lines[1:] = [over_y(lines[k], k) for k in (1, 2, 3)]
+
+    def core_plan(scalars, ins, outs):
+        keep, give = outs
+        pairs = []
+        for k in range(4):
+            at = pl.ds(k * quad, quad)
+            pairs.append((ins[k].at[pl.ds(scalars[0] * quad, quad)], keep.at[at]))
+            pairs.append((ins[k].at[pl.ds((1 - scalars[0]) * quad, quad)], give.at[at]))
+            pairs.append(
+                (ins[k].at[pl.ds(2 * quad, count)], give.at[pl.ds(4 * quad + k * count, count)])
+            )
+        return pairs
+
+    keep, give = copied(core_plan, [c], lines, [(4 * quad, *tile), (4 * quad + 4 * count, *tile)])
+    got = permuted(give, lambda g, d: (g ^ 1, d))
+
+    def combined(value):
+        pieces = value[4 * quad :].reshape(4, 2, 2, 4 * deep, span).astype(jnp.float32)
+        return (pieces[:, 0] + pieces[:, 1]).transpose(0, 2, 1, 3).reshape(-1, col_dev)
+
+    total = jnp.concatenate([combined(give), combined(got)])
     scale = 1.0 / (rows_all * cols_all)
-    coef = scale * lax.dot_general(
-        total, pinv_f, (((0,), (0,)), ((), ())), precision=HIGH
-    )[:modes]
+    coef = scale * lax.dot_general(total, pinv_f, (((0,), (0,)), ((), ())), precision=HIGH)[:modes]
     index = np.arange(FREQS)
     step = np.where(index < BAND, index, index - (BAND - 1))
     weight = np.where(step == 0, 1.0, 2.0)
@@ -191,20 +287,30 @@
     weighed = masked * jnp.asarray(both)[:, None]
     row_here = basis(grp * row_dev + jnp.arange(row_dev, dtype=jnp.int32), rows_all)
 
+    cut = 4 * quad
+    first = [(keep, pinv_a[:, :cut], design_a[:cut]), (got[:cut], pinv_a[:, cut:], design_a[cut:])]
     images, misfits = [], []
-    for part, block in enumerate(blocks):
+    for part, pieces in enumerate((first, [(block, pinv, design)])):
         here = cols[part * span : (part + 1) * span]
         waves = row_here.T[:, None, :, None] * here.T[None, :, None, :]
         ramp = lax.dot_general(
             weighed, waves.reshape(modes, -1), (((0,), (0,)), ((), ())), precision=HIGH
         )
-        flat = block.reshape(ifgs, row_dev * span)
-        series = jnp.dot(pinv, flat, preferred_element_type=jnp.float32)
+        series = 0.0
+        for held_block, some_pinv, _ in pieces:
+            flat = held_block.reshape(-1, row_dev * span)
+            series = series + jnp.dot(some_pinv, flat, preferred_element_type=jnp.float32)
         image = (series - ramp).astype(jnp.bfloat16)
         images.append(image.reshape(solved, row_dev, span))
-        model = jnp.dot(design, series.astype(jnp.bfloat16), preferred_element_type=jnp.float32)
-        resid = flat.astype(jnp.float32) - model
-        misfit = jnp.sqrt(jnp.mean(resid * resid, axis=0) + 1e-06)
+        energy = 0.0
+        for held_block, _, some_design in pieces:
+            flat = held_block.reshape(-1, row_dev * span)
+            model = jnp.dot(
+                some_design, series.astype(jnp.bfloat16), preferred_element_type=jnp.float32
+            )
+            resid = flat.astype(jnp.float32) - model
+            energy = energy + jnp.sum(resid * resid, axis=0)
+        misfit = jnp.sqrt(energy / ifgs + 1e-06)
         misfits.append(misfit.reshape(row_dev, span))
     return (jnp.concatenate(images, axis=2), jnp.concatenate(misfits, axis=1), spectrum)
 

time: 101 us -> 273 us (2.70)
  Pallas kernels: 11.4 us -> 180 us
  waiting for transfers between devices: 17.1 us -> 24.3 us
  starting transfers between devices: 39.1 us -> 36.2 us
    pallas_call x0 -> x4, Pallas kernels: none -> 168 us  [copied(): pl.pallas_call(body, out_shape=[jax.ShapeDtypeStruct(shape, arrays[0].dty...]
    ppermute x10 -> x13, waiting for transfers between devices: 13.5 us -> 24.3 us  [permuted(): return lax.ppermute(value, ('grp', 'dev'), pairs)]
    all_to_all x2 -> x1, starting transfers between devices: 16.9 us -> 9.53 us  [on_device(): block = lax.all_to_all(packed, 'grp', 0, 0, tiled=True)]
    ppermute x10 -> x13, starting transfers between devices: 22.2 us -> 26.6 us  [permuted(): return lax.ppermute(value, ('grp', 'dev'), pairs)]
    all_to_all x2 -> x1, waiting for transfers between devices: 3.61 us -> 0.01 us  [on_device(): block = lax.all_to_all(packed, 'grp', 0, 0, tiled=True)]
    dot_general x6 -> x10, matrix products: 7.53 us -> 7.57 us  [the longest x2 2.73 us: on_device(): lax.dot_general(inverse, some.astype(jnp.float32), (((1,), (1,)), ((), ()...]
  transfers between devices with their start and end apart: 12 -> 14, of which waited for: 6 -> 6; matrix products, arithmetic and copies ran while one was open for 22% -> 9% of each run, Pallas kernels for 11% -> 52%
where the time goes in v6:
time: 273 us; the launch traced here: 272 us
  Pallas kernels  180 us (66%)
  starting transfers between devices  36.2 us (13%)
  waiting for transfers between devices  24.3 us (9%)
  matrix products  14.2 us (5%)
  local copies, waits for them, and re-layouts  9.65 us (4%)
  other arithmetic  6.89 us (3%)
    pallas_call x4, Pallas kernels, copied(): pl.pallas_call(body, out_shape=[jax.ShapeDtypeStruct(shape, arrays[0].dty...  168 us
    ppermute x13, starting transfers between devices, permuted(): return lax.ppermute(value, ('grp', 'dev'), pairs)  26.6 us
    ppermute x13, waiting for transfers between devices, permuted(): return lax.ppermute(value, ('grp', 'dev'), pairs)  24.3 us
    pallas_call x1, Pallas kernels, inverse_of(): pl.pallas_call(sweep_kernel, out_shape=jax.ShapeDtypeStruct((size, width)...  11.4 us
    all_to_all x1, starting transfers between devices, on_device(): block = lax.all_to_all(packed, 'grp', 0, 0, tiled=True)  9.53 us
  transfers between devices with their start and end apart: 14, of which 6 were waited for; matrix products, arithmetic and copies ran while one was open for 9% of the time, Pallas kernels for 52%

profile of v6, /device:TPU:1, one launch (start us, length us, event | category | flops | bytes accessed | tf_op | source)
XLA Modules:
  0.0 272.5 jit_solution(12553179062750937778)
XLA Ops:
  0.7 39.1 %shard_map.175 = (bf16[4,2,19,8,128]{4,3,2,1,0:T(8,128)(2,1)}, bf16[4,2,19,8,128]{4,3,2,1,0:T(8,128)(2,1)}, bf16[4,2,19,8,128]{4,3,2,1,0:T(8,128)(2,1)}, bf16[4,2,19,8,128]{4,3,2,1,0:T(8,128)(2,1)}) custom-call(s32[1]{0:T(128)} %bitcast.2.refs_0_, bf16[19,4,4,2,8,256]{5,4,3,2,1,0:T(8,128)(2,1)} %bitcast.96), custom_call_target="tpu_custom_call" | custom-call | tf_op jit(solution)/shard_map/pallas_call | solution.py:147
  39.8 2.5 collective-permute-start
  42.3 3.0 %collective-permute-start.1 = (bf16[4,2,19,8,128]{4,3,2,1,0:T(8,128)(2,1)}, bf16[4,2,19,8,128]{4,3,2,1,0:T(8,128)(2,1)}, u32[]{:S(2)}, u32[]{:S(2)}) collective-permute-start(bf16[4,2,19,8,128]{4,3,2,1,0:T(8,128)(2,1)} %get-tuple-element.15), channel_id=1, source_target_pairs={{0,32},{1,33},{2,34},{3,35},{4,36},{5,37},{6,38},{7,39},{8,40},{9,... | collective-permute-start | bytes 933896 | tf_op jit(solution)/shard_map/ppermute | solution.py:115
  45.4 1.2 convolution_bitcast_fusion
  46.6 0.5 fusion.57
  47.2 1.3 collective-permute-start.3
  48.5 39.1 %shard_map.178 = bf16[32,19,8,128]{3,2,1,0:T(8,128)(2,1)} custom-call(bf16[19,32,8,256]{3,2,1,0:T(8,128)(2,1)} %bitcast.97), custom_call_target="tpu_custom_call" | custom-call | tf_op jit(solution)/shard_map/pallas_call | solution.py:147
  87.7 9.5 %all-to-all-start = ((bf16[32,19,8,128]{3,2,1,0:T(8,128)(2,1)}), bf16[32,19,8,128]{3,2,1,0:T(8,128)(2,1)S(1)}, u32[]{:S(2)}, u32[]{:S(2)}) async-start(bf16[32,19,8,128]{3,2,1,0:T(8,128)(2,1)} %shard_map.178), calls=%async_computation | async-start | bytes 2490368 | tf_op jit(solution)/shard_map/all_to_all | solution.py:205
  97.5 0.6 fusion.19
  98.2 0.8 fusion.8
  99.0 0.7 select_add_fusion.normal_ref
  99.8 11.4 %sweep.1 = f32[152,256]{1,0:T(8,128)} custom-call(f32[152,256]{1,0:T(8,128)} %select_add_fusion.normal_ref), custom_call_target="tpu_custom_call" | custom-call | flops 30000000 | bytes 300000 | tf_op jit(solution)/shard_map/sweep/pallas_call | solution.py:67
  111.2 1.2 convolution_convert_fusion.1
  112.5 2.5 collective-permute-start.4
  115.0 1.5 convolution_convert_fusion
  116.5 0.5 collective-permute-done.4
  117.1 0.7 collective-permute-start.5
  117.7 4.3 %collective-permute-start.6 = (f32[24,256]{1,0:T(8,128)S(1)}, f32[24,256]{1,0:T(8,128)S(1)}, u32[]{:S(2)}, u32[]{:S(2)}) collective-permute-start(f32[24,256]{1,0:T(8,128)S(1)} %add.145), channel_id=1, source_target_pairs={{0,1},{1,0},{2,19},{3,18},{4,37},{5,36},{6,55},{7,54},{8,9},{9,8},... | collective-permute-start | bytes 73736 | tf_op jit(solution)/shard_map/ppermute | solution.py:115
  122.2 2.3 collective-permute-done.6
  124.5 5.7 %collective-permute-start.7 = (f32[24,256]{1,0:T(8,128)S(1)}, f32[24,256]{1,0:T(8,128)S(1)}, u32[]{:S(2)}, u32[]{:S(2)}) collective-permute-start(f32[24,256]{1,0:T(8,128)S(1)} %add.146), channel_id=1, source_target_pairs={{0,2},{1,3},{2,0},{3,1},{4,6},{5,7},{6,4},{7,5},{8,10},{9,11},{10,... | collective-permute-start | bytes 73736 | tf_op jit(solution)/shard_map/ppermute | solution.py:115
  130.2 1.2 collective-permute-done.7
  131.4 1.8 collective-permute-start.8
  133.2 2.6 collective-permute-done.8
  136.2 0.7 copy-done.9
  136.9 39.1 %shard_map.176 = (bf16[152,8,128]{2,1,0:T(8,128)(2,1)}, bf16[152,8,128]{2,1,0:T(8,128)(2,1)}, bf16[152,8,128]{2,1,0:T(8,128)(2,1)}, bf16[152,8,128]{2,1,0:T(8,128)(2,1)}) custom-call(s32[1]{0:T(128)} %bitcast.1.refs_0_, bf16[4,2,19,8,128]{4,3,2,1,0:T(8,128)(2,1)} %get-tuple-element.13.refs_1_, bf16[4,2,19,8,128]{4,3,2,1,0:T(8,128)(2,1)} %copy-done.9, ...), custom_call_target="tpu_custom_call" | custom-call | tf_op jit(solution)/shard_map/pallas_call | solution.py:147
  176.1 2.1 pad_maximum_fusion.2
  178.2 2.9 %collective-permute-start.10 = (bf16[200,8,128]{2,1,0:T(8,128)(2,1)S(1)}, bf16[200,8,128]{2,1,0:T(8,128)(2,1)}, u32[]{:S(2)}, u32[]{:S(2)}) collective-permute-start(bf16[200,8,128]{2,1,0:T(8,128)(2,1)S(1)} %get-tuple-element.31), channel_id=1, source_target_pairs={{0,128},{1,129},{2,130},{3,131},{4,132},{5,133},{6,134},{7,135},{8... | collective-permute-start | bytes 1228808 | tf_op jit(solution)/shard_map/ppermute | solution.py:115
  181.1 0.9 collective-permute-start.11
  182.3 6.1 %collective-permute-done.10.refs_3_ = bf16[200,8,128]{2,1,0:T(8,128)(2,1)} collective-permute-done((bf16[200,8,128]{2,1,0:T(8,128)(2,1)S(1)}, bf16[200,8,128]{2,1,0:T(8,128)(2,1)}, u32[]{:S(2)}, u32[]{:S(2)}) %collective-permute-start.10) | collective-permute-done | bytes 409632 | tf_op jit(solution)/shard_map/ppermute | solution.py:115
  188.4 11.5 %collective-permute-done.11.refs_4_ = bf16[200,8,128]{2,1,0:T(8,128)(2,1)} collective-permute-done((bf16[200,8,128]{2,1,0:T(8,128)(2,1)S(1)}, bf16[200,8,128]{2,1,0:T(8,128)(2,1)}, u32[]{:S(2)}, u32[]{:S(2)}) %collective-permute-start.11) | collective-permute-done | bytes 409632 | tf_op jit(solution)/shard_map/ppermute | solution.py:115
  200.0 51.0 %shard_map.177 = (bf16[304,8,128]{2,1,0:T(8,128)(2,1)}, bf16[496,8,128]{2,1,0:T(8,128)(2,1)}) custom-call(s32[1]{0:T(128)} %bitcast.refs_0_, bf16[200,8,128]{2,1,0:T(8,128)(2,1)} %get-tuple-element.32.refs_1_, bf16[200,8,128]{2,1,0:T(8,128)(2,1)} %collective-permute-done.9.refs_2_, bf16[200,8,128]{2,1,0:T(8,128)(2,1)} %collective-permute-done.10.refs_3_, ...), custom_call_target="tpu_custom_call" | custom-call | tf_op jit(solution)/shard_map/pallas_call | solution.py:147
  251.0 1.1 collective-permute-start.12
  252.0 0.7 add_select_fusion.2
  253.4 0.5 fusion
  253.9 1.0 slice.57
  255.1 0.5 copy_add_fusion.1
  256.5 1.0 slice.75
  258.2 1.2 slice.72
  259.3 1.4 fusion.9
  261.5 0.7 fusion.6
  262.3 0.7 slice.82
  263.0 1.3 fusion.89
  264.4 2.1 reshape.197
  266.4 1.4 multiply_reduce_fusion.1
  269.2 0.6 multiply_reduce_fusion
  270.1 0.7 fusion.7
  271.0 0.6 pad_maximum_fusion.10
  271.6 0.9 pad_maximum_fusion.6
  (111 shorter events, 5.7 us)
Async XLA Ops:
  0.7 44.7 %copy-start = (bf16[19,256,256]{2,1,0:T(8,128)(2,1)S(1)}, bf16[19,256,256]{2,1,0:T(8,128)(2,1)}, u32[]{:S(2)}) copy-start(bf16[19,256,256]{2,1,0:T(8,128)(2,1)} %param.16) | copy-start | bytes 7471108
  39.8 96.4 %collective-permute-start = (bf16[4,2,19,8,128]{4,3,2,1,0:T(8,128)(2,1)}, bf16[4,2,19,8,128]{4,3,2,1,0:T(8,128)(2,1)S(1)}, u32[]{:S(2)}, u32[]{:S(2)}) collective-permute-start(bf16[4,2,19,8,128]{4,3,2,1,0:T(8,128)(2,1)} %get-tuple-element.14), channel_id=1, source_target_pairs={{0,16},{1,17},{2,18},{3,19},{4,20},{5,21},{6,22},{7,23},{8,24},{9,... | collective-permute-start | bytes 933896 | tf_op jit(solution)/shard_map/ppermute | solution.py:115
  42.3 93.9 %collective-permute-start.1 = (bf16[4,2,19,8,128]{4,3,2,1,0:T(8,128)(2,1)}, bf16[4,2,19,8,128]{4,3,2,1,0:T(8,128)(2,1)}, u32[]{:S(2)}, u32[]{:S(2)}) collective-permute-start(bf16[4,2,19,8,128]{4,3,2,1,0:T(8,128)(2,1)} %get-tuple-element.15), channel_id=1, source_target_pairs={{0,32},{1,33},{2,34},{3,35},{4,36},{5,37},{6,38},{7,39},{8,40},{9,... | collective-permute-start | bytes 933896 | tf_op jit(solution)/shard_map/ppermute | solution.py:115
  45.3 90.9 %collective-permute-start.2 = (bf16[4,2,19,8,128]{4,3,2,1,0:T(8,128)(2,1)}, bf16[4,2,19,8,128]{4,3,2,1,0:T(8,128)(2,1)}, u32[]{:S(2)}, u32[]{:S(2)}) collective-permute-start(bf16[4,2,19,8,128]{4,3,2,1,0:T(8,128)(2,1)} %get-tuple-element.16), channel_id=1, source_target_pairs={{0,48},{1,49},{2,50},{3,51},{4,52},{5,53},{6,54},{7,55},{8,56},{9,... | collective-permute-start | bytes 933896 | tf_op jit(solution)/shard_map/ppermute | solution.py:115
  47.2 65.2 %collective-permute-start.3 = (f32[24,256]{1,0:T(8,128)S(1)}, f32[24,256]{1,0:T(8,128)S(1)}, u32[]{:S(2)}, u32[]{:S(2)}) collective-permute-start(f32[24,256]{1,0:T(8,128)S(1)} %pad.9), channel_id=1, source_target_pairs={{0,2},{1,3},{2,0},{3,1},{4,6},{5,7},{6,4},{7,5},{8,10},{9,11},{10,... | collective-permute-start | bytes 73736 | tf_op jit(solution)/shard_map/ppermute | solution.py:115
  87.7 9.7 %copy-start.17 = (s32[2,4,4,19]{3,2,1,0:T(4,128)S(1)}, s32[2,4,4,19]{3,2,1,0:T(4,128)}, u32[]{:S(2)}) copy-start(s32[2,4,4,19]{3,2,1,0:T(4,128)} %constant.155.clone) | copy-start | bytes 7300
  87.7 9.7 %copy-start.18 = (s32[2,4,4,19]{3,2,1,0:T(4,128)S(1)}, s32[2,4,4,19]{3,2,1,0:T(4,128)}, u32[]{:S(2)}) copy-start(s32[2,4,4,19]{3,2,1,0:T(4,128)} %constant.156.clone) | copy-start | bytes 7300
  87.7 9.7 %copy-start.19 = (s32[2,4,4,19]{3,2,1,0:T(4,128)S(1)}, s32[2,4,4,19]{3,2,1,0:T(4,128)}, u32[]{:S(2)}) copy-start(s32[2,4,4,19]{3,2,1,0:T(4,128)} %constant.157.clone) | copy-start | bytes 7300
  87.7 9.6 %copy-start.20 = (s32[2,4,4,19]{3,2,1,0:T(4,128)S(1)}, s32[2,4,4,19]{3,2,1,0:T(4,128)}, u32[]{:S(2)}) copy-start(s32[2,4,4,19]{3,2,1,0:T(4,128)} %constant.158.clone) | copy-start | bytes 7300
  87.7 9.8 %copy-start.21 = (s32[608,2]{0,1:T(2,128)S(1)}, s32[608,2]{0,1:T(2,128)}, u32[]{:S(2)}) copy-start(s32[608,2]{0,1:T(2,128)} %param.17) | copy-start | bytes 14596
  87.7 180.6 %all-to-all-start = ((bf16[32,19,8,128]{3,2,1,0:T(8,128)(2,1)}), bf16[32,19,8,128]{3,2,1,0:T(8,128)(2,1)S(1)}, u32[]{:S(2)}, u32[]{:S(2)}) async-start(bf16[32,19,8,128]{3,2,1,0:T(8,128)(2,1)} %shard_map.178), calls=%async_computation | async-start | bytes 2490368 | tf_op jit(solution)/shard_map/all_to_all | solution.py:205
  97.3 17.8 %copy-start.28 = (s32[149]{0:T(256)}, s32[149]{0:T(256)S(1)}, u32[]{:S(2)}) copy-start(s32[149]{0:T(256)S(1)} %iota_add_fusion.1) | copy-start | bytes 1792
  97.5 17.5 %copy-start.24 = (s32[608]{0:T(1024)}, s32[608]{0:T(1024)S(1)}, u32[]{:S(2)}) copy-start(s32[608]{0:T(1024)S(1)} %get-tuple-element.24) | copy-start | bytes 7300
  99.0 83.1 %copy-start.12 = (bf16[608,149]{0,1:T(8,128)(2,1)}, bf16[608,149]{0,1:T(8,128)(2,1)S(1)}, u32[]{:S(2)}) copy-start(bf16[608,149]{0,1:T(8,128)(2,1)S(1)} %fusion.8) | copy-start | bytes 543556
  112.5 143.2 %copy-start.4 = (bf16[149,608]{1,0:T(8,128)(2,1)}, bf16[149,608]{1,0:T(8,128)(2,1)S(1)}, u32[]{:S(2)}) copy-start(bf16[149,608]{1,0:T(8,128)(2,1)S(1)} %convolution_convert_fusion.1) | copy-start | bytes 543556
  112.5 4.6 %collective-permute-start.4 = (f32[24,256]{1,0:T(8,128)S(1)}, f32[24,256]{1,0:T(8,128)S(1)}, u32[]{:S(2)}, u32[]{:S(2)}) collective-permute-start(f32[24,256]{1,0:T(8,128)S(1)} %pad_add_fusion), channel_id=1, source_target_pairs={{0,4},{1,5},{2,6},{3,7},{4,0},{5,1},{6,2},{7,3},{8,12},{9,13},{10,... | collective-permute-start | bytes 73736 | tf_op jit(solution)/shard_map/ppermute | solution.py:115
  116.5 136.9 %copy-start.10 = (bf16[149,608]{1,0:T(8,128)(2,1)}, bf16[149,608]{1,0:T(8,128)(2,1)S(1)}, u32[]{:S(2)}) copy-start(bf16[149,608]{1,0:T(8,128)(2,1)S(1)} %convolution_convert_fusion) | copy-start | bytes 543556
  117.1 5.1 %collective-permute-start.5 = (f32[24,256]{1,0:T(8,128)S(1)}, f32[24,256]{1,0:T(8,128)S(1)}, u32[]{:S(2)}, u32[]{:S(2)}) collective-permute-start(f32[24,256]{1,0:T(8,128)S(1)} %add.145), channel_id=1, source_target_pairs={{0,0},{1,1},{2,18},{3,19},{4,36},{5,37},{6,54},{7,55},{8,8},{9,9},... | collective-permute-start | bytes 73736 | tf_op jit(solution)/shard_map/ppermute | solution.py:115
  117.7 6.8 %collective-permute-start.6 = (f32[24,256]{1,0:T(8,128)S(1)}, f32[24,256]{1,0:T(8,128)S(1)}, u32[]{:S(2)}, u32[]{:S(2)}) collective-permute-start(f32[24,256]{1,0:T(8,128)S(1)} %add.145), channel_id=1, source_target_pairs={{0,1},{1,0},{2,19},{3,18},{4,37},{5,36},{6,55},{7,54},{8,9},{9,8},... | collective-permute-start | bytes 73736 | tf_op jit(solution)/shard_map/ppermute | solution.py:115
  124.5 6.9 %collective-permute-start.7 = (f32[24,256]{1,0:T(8,128)S(1)}, f32[24,256]{1,0:T(8,128)S(1)}, u32[]{:S(2)}, u32[]{:S(2)}) collective-permute-start(f32[24,256]{1,0:T(8,128)S(1)} %add.146), channel_id=1, source_target_pairs={{0,2},{1,3},{2,0},{3,1},{4,6},{5,7},{6,4},{7,5},{8,10},{9,11},{10,... | collective-permute-start | bytes 73736 | tf_op jit(solution)/shard_map/ppermute | solution.py:115
  131.4 4.4 %collective-permute-start.8 = (f32[2,24,256]{2,1,0:T(8,128)S(1)}, f32[2,24,256]{2,1,0:T(8,128)S(1)}, u32[]{:S(2)}, u32[]{:S(2)}) collective-permute-start(f32[2,24,256]{2,1,0:T(8,128)S(1)} %pad_maximum_fusion.9), channel_id=1, source_target_pairs={{0,4},{1,5},{2,6},{3,7},{4,0},{5,1},{6,2},{7,3},{8,12},{9,13},{10,... | collective-permute-start | bytes 147464 | tf_op jit(solution)/shard_map/ppermute | solution.py:115
  136.2 0.7 copy-start.9
  178.2 10.2 %collective-permute-start.10 = (bf16[200,8,128]{2,1,0:T(8,128)(2,1)S(1)}, bf16[200,8,128]{2,1,0:T(8,128)(2,1)}, u32[]{:S(2)}, u32[]{:S(2)}) collective-permute-start(bf16[200,8,128]{2,1,0:T(8,128)(2,1)S(1)} %get-tuple-element.31), channel_id=1, source_target_pairs={{0,128},{1,129},{2,130},{3,131},{4,132},{5,133},{6,134},{7,135},{8... | collective-permute-start | bytes 1228808 | tf_op jit(solution)/shard_map/ppermute | solution.py:115
  181.1 18.9 %collective-permute-start.11 = (bf16[200,8,128]{2,1,0:T(8,128)(2,1)S(1)}, bf16[200,8,128]{2,1,0:T(8,128)(2,1)}, u32[]{:S(2)}, u32[]{:S(2)}) collective-permute-start(bf16[200,8,128]{2,1,0:T(8,128)(2,1)S(1)} %get-tuple-element.29), channel_id=1, source_target_pairs={{0,192},{1,193},{2,194},{3,195},{4,196},{5,197},{6,198},{7,199},{8... | collective-permute-start | bytes 1228808 | tf_op jit(solution)/shard_map/ppermute | solution.py:115
  182.0 18.0 %collective-permute-start.9 = (bf16[200,8,128]{2,1,0:T(8,128)(2,1)S(1)}, bf16[200,8,128]{2,1,0:T(8,128)(2,1)}, u32[]{:S(2)}, u32[]{:S(2)}) collective-permute-start(bf16[200,8,128]{2,1,0:T(8,128)(2,1)S(1)} %get-tuple-element.30), channel_id=1, source_target_pairs={{0,64},{1,65},{2,66},{3,67},{4,68},{5,69},{6,70},{7,71},{8,72},{9,... | collective-permute-start | bytes 1228808 | tf_op jit(solution)/shard_map/ppermute | solution.py:115
  182.3 69.7 %copy-start.14 = (s32[2,4,4,24]{3,2,1,0:T(4,128)S(1)}, s32[2,4,4,24]{3,2,1,0:T(4,128)}, u32[]{:S(2)}) copy-start(s32[2,4,4,24]{3,2,1,0:T(4,128)} %constant.160.clone) | copy-start | bytes 9220
  182.3 69.7 %copy-start.15 = (s32[2,4,4,24]{3,2,1,0:T(4,128)S(1)}, s32[2,4,4,24]{3,2,1,0:T(4,128)}, u32[]{:S(2)}) copy-start(s32[2,4,4,24]{3,2,1,0:T(4,128)} %constant.161.clone) | copy-start | bytes 9220
  182.3 69.7 %copy-start.16 = (s32[2,4,4,24]{3,2,1,0:T(4,128)S(1)}, s32[2,4,4,24]{3,2,1,0:T(4,128)}, u32[]{:S(2)}) copy-start(s32[2,4,4,24]{3,2,1,0:T(4,128)} %constant.162.clone) | copy-start | bytes 9220
  182.3 69.7 %copy-start.23 = (pred[2,4,4,24]{3,2,1,0:T(4,128)(4,1)S(1)}, pred[2,4,4,24]{3,2,1,0:T(4,128)(4,1)}, u32[]{:S(2)}) copy-start(pred[2,4,4,24]{3,2,1,0:T(4,128)(4,1)} %constant.164.clone) | copy-start | bytes 2308
  251.0 5.5 %collective-permute-start.12 = (bf16[496,8,128]{2,1,0:T(8,128)(2,1)}, bf16[496,8,128]{2,1,0:T(8,128)(2,1)}, u32[]{:S(2)}, u32[]{:S(2)}) collective-permute-start(bf16[496,8,128]{2,1,0:T(8,128)(2,1)} %get-tuple-element.22), channel_id=1, source_target_pairs={{0,8},{1,9},{2,10},{3,11},{4,12},{5,13},{6,14},{7,15},{8,0},{9,1},... | collective-permute-start | bytes 3047432 | tf_op jit(solution)/shard_map/ppermute | solution.py:115
  255.1 1.1 copy-start.6
  258.1 1.2 copy-start.26
  258.1 1.2 copy-start.27
  258.2 2.7 copy-start.5
  260.8 2.3 copy-start.1
  260.8 0.7 copy-start.22
  261.5 1.5 copy-start.8
  266.4 1.4 copy-start.7
  266.4 1.4 copy-start.13
  267.9 0.9 copy-start.11
  268.3 0.9 copy-start.25
  268.3 0.9 copy-start.29
  269.2 0.9 copy-start.2
  270.1 1.5 copy-start.3

commit v7 on v6

--- a/solution.py
+++ b/solution.py
@@ -127,16 +127,20 @@
     return permuted(value, lambda g, d: (g, d ^ (k << 1)))
 
 
-HBM = pl.BlockSpec(memory_space=pl.ANY)
-
-
-def copied(plan, scalars, arrays, shapes):
+def copied(plan, scalars, arrays, shapes, far=False):
+    near = pl.BlockSpec(memory_space=pltpu.VMEM)
+
     def body(*refs):
         some, rest = refs[: len(scalars)], refs[len(scalars) :]
-        ins, outs, sem = rest[: len(arrays)], rest[len(arrays) : -1], rest[-1]
+        ins, rest = rest[: len(arrays)], rest[len(arrays) :]
+        outs, sems = rest[: len(shapes)], rest[len(shapes) :]
         pairs = plan([ref[0] for ref in some], ins, outs)
+        if not far:
+            for source, target in pairs:
+                target[...] = source[...]
+            return
         copies = [
-            pltpu.make_async_copy(source, target, sem.at[i])
+            pltpu.make_async_copy(source, target, sems[0].at[i])
             for i, (source, target) in enumerate(pairs)
         ]
         for copy in copies:
@@ -144,14 +148,16 @@
         for copy in copies:
             copy.wait()
 
-    return pl.pallas_call(
-        body,
-        out_shape=[jax.ShapeDtypeStruct(shape, arrays[0].dtype) for shape in shapes],
-        in_specs=[pl.BlockSpec(memory_space=pltpu.SMEM)] * len(scalars)
-        + [HBM] * len(arrays),
-        out_specs=[HBM] * len(shapes),
-        scratch_shapes=[pltpu.SemaphoreType.DMA((32,))],
-    )(*[jnp.reshape(v, (1,)) for v in scalars], *arrays)
+    return list(
+        pl.pallas_call(
+            body,
+            out_shape=[pltpu.VMEM(shape, arrays[0].dtype) for shape in shapes],
+            in_specs=[pl.BlockSpec(memory_space=pltpu.SMEM)] * len(scalars)
+            + [pl.BlockSpec(memory_space=pl.ANY) if far else near] * len(arrays),
+            out_specs=[near] * len(shapes),
+            scratch_shapes=[pltpu.SemaphoreType.DMA((32,))] if far else [],
+        )(*[jnp.reshape(v, (1,)) for v in scalars], *arrays)
+    )
 
 
 def on_device(stack, network, bands):
@@ -178,8 +184,7 @@
             for j in range(2)
         ]
 
-    planes = copied(plane_plan, [z], [strips], [(4, 2, held, *tile)] * 4)
-    planes = list(planes)
+    planes = copied(plane_plan, [z], [strips], [(4, 2, held, *tile)] * 4, True)
     planes[1:] = [over_z(planes[k], k) for k in (1, 2, 3)]
 
     rows = basis(jnp.arange(rows_all, dtype=jnp.int32), rows_all)
@@ -200,7 +205,11 @@
         ]
 
     (packed,) = copied(
-        bulk_plan, [], [stack.reshape(held, groups, row_dev, col_dev)], [(groups, held, *tile)]
+        bulk_plan,
+        [],
+        [stack.reshape(held, groups, row_dev, col_dev)],
+        [(groups, held, *tile)],
+        True,
     )
     block = lax.all_to_all(packed, "grp", 0, 0, tiled=True)
 
@@ -248,10 +257,9 @@
             for kz in range(4)
             for j in range(2)
         ]
-        return pairs
-
-    lines = copied(line_plan, [y], planes, [(2 * quad, *tile)] * 4)
-    lines = [jnp.concatenate([line, sums]) for line in lines]
+        return pairs + [(ins[4], outs[k].at[pl.ds(2 * quad, count)]) for k in range(4)]
+
+    lines = copied(line_plan, [y], [*planes, sums], [(2 * quad + count, *tile)] * 4)
     lines[1:] = [over_y(lines[k], k) for k in (1, 2, 3)]
 
     def core_plan(scalars, ins, outs):

time: 273 us -> 128 us (0.47)
  Pallas kernels: 180 us -> 18.5 us
  starting transfers between devices: 36.2 us -> 44.7 us
  local copies, waits for them, and re-layouts: 9.65 us -> 14.3 us
    pallas_call x4, Pallas kernels: 168 us -> 7.08 us  [copied(): pl.pallas_call(body, out_shape=[pltpu.VMEM(shape, arrays[0].dtype) for sh...]
    ppermute x13, starting transfers between devices: 26.6 us -> 35.2 us  [permuted(): return lax.ppermute(value, ('grp', 'dev'), pairs)]
    unnamed x68 -> x76, local copies, waits for them, and re-layouts: 3.09 us -> 8.1 us
  transfers between devices with their start and end apart: 14 -> 14, of which waited for: 6 -> 5; matrix products, arithmetic and copies ran while one was open for 9% -> 19% of each run, Pallas kernels for 52% -> 15%
where the time goes in v7:
time: 128 us; the launch traced here: 127 us
  starting transfers between devices  44.7 us (35%)
  waiting for transfers between devices  26.4 us (21%)
  Pallas kernels  18.5 us (14%)
  matrix products  15.6 us (12%)
  local copies, waits for them, and re-layouts  14.3 us (11%)
  other arithmetic  6 us (5%)
  between operations  1.36 us (1%)
    ppermute x13, starting transfers between devices, permuted(): return lax.ppermute(value, ('grp', 'dev'), pairs)  35.2 us
    ppermute x13, waiting for transfers between devices, permuted(): return lax.ppermute(value, ('grp', 'dev'), pairs)  26.4 us
    pallas_call x1, Pallas kernels, inverse_of(): pl.pallas_call(sweep_kernel, out_shape=jax.ShapeDtypeStruct((size, width)...  11.4 us
    all_to_all x1, starting transfers between devices, on_device(): block = lax.all_to_all(packed, 'grp', 0, 0, tiled=True)  9.54 us
    unnamed x76, local copies, waits for them, and re-layouts  8.1 us
    pallas_call x4, Pallas kernels, copied(): pl.pallas_call(body, out_shape=[pltpu.VMEM(shape, arrays[0].dtype) for sh...  7.08 us
    dot_general x2, matrix products, on_device(): lax.dot_general(inverse, some.astype(jnp.float32), (((1,), (1,)), ((), ()...  3.43 us
    dot_general x1, matrix products, on_device(): half = jnp.einsum('ihw,ha->iaw', wide, rows, precision=HIGH)  2.9 us
  transfers between devices with their start and end apart: 14, of which 5 were waited for; matrix products, arithmetic and copies ran while one was open for 19% of the time, Pallas kernels for 15%

profile of v7, /device:TPU:1, one launch (start us, length us, event | category | flops | bytes accessed | tf_op | source)
XLA Modules:
  0.0 126.8 jit_solution(4448935401513253377)
XLA Ops:
  0.7 2.9 %convolution_bitcast_fusion = f32[19,15,256]{2,1,0:T(8,128)S(1)} fusion(bf16[19,256,256]{2,1,0:T(8,128)(2,1)} %param.16, s32[15]{0:T(128)S(1)} %add_select_fusion.4, pred[15]{0:T(512)(128)(4,1)S(1)} %iota_compare_fusion.7), kind=kOutput, calls=%fused_computation.16 | convolution fusion | flops 224190720 | bytes 2782283 | tf_op jit(solution)/shard_map/ihw,ha->iaw/dot_general | solution.py:193
  4.2 2.1 %collective-permute-start.3 = (f32[24,256]{1,0:T(8,128)S(1)}, f32[24,256]{1,0:T(8,128)S(1)}, u32[]{:S(2)}, u32[]{:S(2)}) collective-permute-start(f32[24,256]{1,0:T(8,128)S(1)} %pad.9), channel_id=1, source_target_pairs={{0,2},{1,3},{2,0},{3,1},{4,6},{5,7},{6,4},{7,5},{8,10},{9,11},{10,... | collective-permute-start | bytes 73736 | tf_op jit(solution)/shard_map/ppermute | solution.py:115
  6.4 1.6 %shard_map.175 = (bf16[4,2,19,8,128]{4,3,2,1,0:T(8,128)(2,1)S(1)}, bf16[4,2,19,8,128]{4,3,2,1,0:T(8,128)(2,1)S(1)}, bf16[4,2,19,8,128]{4,3,2,1,0:T(8,128)(2,1)S(1)}, bf16[4,2,19,8,128]{4,3,2,1,0:T(8,128)(2,1)S(1)}) custom-call(s32[1]{0:T(128)} %bitcast.2.refs_0_, bf16[19,4,4,2,8,256]{5,4,3,2,1,0:T(8,128)(2,1)} %bitcast.98), custom_call_target="tpu_custom_call" | custom-call | tf_op jit(solution)/shard_map/pallas_call | solution.py:152
  8.0 0.7 copy-done.1
  8.7 1.6 %collective-permute-start = (bf16[4,2,19,8,128]{4,3,2,1,0:T(8,128)(2,1)S(1)}, bf16[4,2,19,8,128]{4,3,2,1,0:T(8,128)(2,1)S(1)}, u32[]{:S(2)}, u32[]{:S(2)}) collective-permute-start(bf16[4,2,19,8,128]{4,3,2,1,0:T(8,128)(2,1)S(1)} %get-tuple-element.14), channel_id=1, source_target_pairs={{0,16},{1,17},{2,18},{3,19},{4,20},{5,21},{6,22},{7,23},{8,24},{9,... | collective-permute-start | bytes 933896 | tf_op jit(solution)/shard_map/ppermute | solution.py:115
  10.3 3.0 %collective-permute-start.1 = (bf16[4,2,19,8,128]{4,3,2,1,0:T(8,128)(2,1)S(1)}, bf16[4,2,19,8,128]{4,3,2,1,0:T(8,128)(2,1)S(1)}, u32[]{:S(2)}, u32[]{:S(2)}) collective-permute-start(bf16[4,2,19,8,128]{4,3,2,1,0:T(8,128)(2,1)S(1)} %get-tuple-element.15), channel_id=1, source_target_pairs={{0,32},{1,33},{2,34},{3,35},{4,36},{5,37},{6,38},{7,39},{8,40},{9,... | collective-permute-start | bytes 933896 | tf_op jit(solution)/shard_map/ppermute | solution.py:115
  13.3 2.6 %shard_map.178 = bf16[32,19,8,128]{3,2,1,0:T(8,128)(2,1)} custom-call(bf16[19,32,8,256]{3,2,1,0:T(8,128)(2,1)} %bitcast.99), custom_call_target="tpu_custom_call" | custom-call | tf_op jit(solution)/shard_map/pallas_call | solution.py:152
  16.0 9.5 %all-to-all-start = ((bf16[32,19,8,128]{3,2,1,0:T(8,128)(2,1)}), bf16[32,19,8,128]{3,2,1,0:T(8,128)(2,1)S(1)}, u32[]{:S(2)}, u32[]{:S(2)}) async-start(bf16[32,19,8,128]{3,2,1,0:T(8,128)(2,1)} %shard_map.178), calls=%async_computation | async-start | bytes 2490368 | tf_op jit(solution)/shard_map/all_to_all | solution.py:214
  25.8 0.6 fusion.19
  26.5 0.8 fusion.8
  27.3 0.8 select_add_fusion.normal_ref
  28.1 11.4 %sweep.1 = f32[152,256]{1,0:T(8,128)} custom-call(f32[152,256]{1,0:T(8,128)} %select_add_fusion.normal_ref), custom_call_target="tpu_custom_call" | custom-call | flops 30000000 | bytes 300000 | tf_op jit(solution)/shard_map/sweep/pallas_call | solution.py:67
  39.5 1.2 convolution_convert_fusion.1
  40.8 2.5 %collective-permute-start.4 = (f32[24,256]{1,0:T(8,128)S(1)}, f32[24,256]{1,0:T(8,128)S(1)}, u32[]{:S(2)}, u32[]{:S(2)}) collective-permute-start(f32[24,256]{1,0:T(8,128)S(1)} %pad_add_fusion), channel_id=1, source_target_pairs={{0,4},{1,5},{2,6},{3,7},{4,0},{5,1},{6,2},{7,3},{8,12},{9,13},{10,... | collective-permute-start | bytes 73736 | tf_op jit(solution)/shard_map/ppermute | solution.py:115
  43.3 2.2 %convolution_convert_fusion = bf16[149,608]{1,0:T(8,128)(2,1)} fusion(s32[149]{0:T(256)S(1)} %iota_add_fusion.1, s32[608]{0:T(1024)S(1)} %get-tuple-element.24, s32[608]{0:T(1024)S(1)} %get-tuple-element.23, f32[152,256]{1,0:T(8,128)} %sweep.1), kind=kOutput, calls=%fused_computation.17 | convolution fusion | flops 162612640 | bytes 342292 | tf_op jit(solution)/shard_map/dot_general | solution.py:233
  45.5 0.7 collective-permute-start.5
  46.2 4.3 %collective-permute-start.6 = (f32[24,256]{1,0:T(8,128)S(1)}, f32[24,256]{1,0:T(8,128)S(1)}, u32[]{:S(2)}, u32[]{:S(2)}) collective-permute-start(f32[24,256]{1,0:T(8,128)S(1)} %add.145), channel_id=1, source_target_pairs={{0,1},{1,0},{2,19},{3,18},{4,37},{5,36},{6,55},{7,54},{8,9},{9,8},... | collective-permute-start | bytes 73736 | tf_op jit(solution)/shard_map/ppermute | solution.py:115
  50.7 6.2 %collective-permute-done.6 = f32[24,256]{1,0:T(8,128)S(1)} collective-permute-done((f32[24,256]{1,0:T(8,128)S(1)}, f32[24,256]{1,0:T(8,128)S(1)}, u32[]{:S(2)}, u32[]{:S(2)}) %collective-permute-start.6) | collective-permute-done | bytes 24608 | tf_op jit(solution)/shard_map/ppermute | solution.py:115
  56.8 14.3 %collective-permute-start.7 = (f32[24,256]{1,0:T(8,128)S(1)}, f32[24,256]{1,0:T(8,128)S(1)}, u32[]{:S(2)}, u32[]{:S(2)}) collective-permute-start(f32[24,256]{1,0:T(8,128)S(1)} %add.146), channel_id=1, source_target_pairs={{0,2},{1,3},{2,0},{3,1},{4,6},{5,7},{6,4},{7,5},{8,10},{9,11},{10,... | collective-permute-start | bytes 73736 | tf_op jit(solution)/shard_map/ppermute | solution.py:115
  71.1 1.2 collective-permute-done.7
  72.6 4.2 %collective-permute-done.8 = f32[2,24,256]{2,1,0:T(8,128)S(1)} collective-permute-done((f32[2,24,256]{2,1,0:T(8,128)S(1)}, f32[2,24,256]{2,1,0:T(8,128)S(1)}, u32[]{:S(2)}, u32[]{:S(2)}) %collective-permute-start.8) | collective-permute-done | bytes 49184 | tf_op jit(solution)/shard_map/ppermute | solution.py:115
  77.1 0.6 copy.20
  77.8 0.7 copy-done.10
  78.6 1.4 %shard_map.176 = (bf16[200,8,128]{2,1,0:T(8,128)(2,1)S(1)}, bf16[200,8,128]{2,1,0:T(8,128)(2,1)S(1)}, bf16[200,8,128]{2,1,0:T(8,128)(2,1)S(1)}, bf16[200,8,128]{2,1,0:T(8,128)(2,1)S(1)}) custom-call(s32[1]{0:T(128)} %bitcast.1.refs_0_, bf16[4,2,19,8,128]{4,3,2,1,0:T(8,128)(2,1)} %copy-done.1, bf16[4,2,19,8,128]{4,3,2,1,0:T(8,128)(2,1)} %copy-done.9, ...), custom_call_target="tpu_custom_call" | custom-call | tf_op jit(solution)/shard_map/pallas_call | solution.py:152
  80.0 3.0 %collective-permute-start.10 = (bf16[200,8,128]{2,1,0:T(8,128)(2,1)S(1)}, bf16[200,8,128]{2,1,0:T(8,128)(2,1)S(1)}, u32[]{:S(2)}, u32[]{:S(2)}) collective-permute-start(bf16[200,8,128]{2,1,0:T(8,128)(2,1)S(1)} %get-tuple-element.19), channel_id=1, source_target_pairs={{0,128},{1,129},{2,130},{3,131},{4,132},{5,133},{6,134},{7,135},{8... | collective-permute-start | bytes 1228808 | tf_op jit(solution)/shard_map/ppermute | solution.py:115
  83.0 0.8 collective-permute-start.11
  83.9 1.4 %broadcast_multiply_fusion.1 = (f32[15,15,8,128]{3,2,1,0:T(8,128)}, f32[15,15,8,128]{3,2,1,0:T(8,128)}) fusion(f32[15,128]{1,0:T(8,128)S(1)} %get-tuple-element.31, f32[15,8]{1,0:T(8,128)S(1)} %sine_select_fusion.1, f32[15,128]{1,0:T(8,128)S(1)} %get-tuple-element.32), kind=kLoop, calls=%fused_computation.35 | loop fusion | flops 460800 | bytes 1859040 | tf_op jit(solution)/shard_map/mul | solution.py:303
  85.3 3.1 %collective-permute-done.10.refs_3_ = bf16[200,8,128]{2,1,0:T(8,128)(2,1)S(1)} collective-permute-done((bf16[200,8,128]{2,1,0:T(8,128)(2,1)S(1)}, bf16[200,8,128]{2,1,0:T(8,128)(2,1)S(1)}, u32[]{:S(2)}, u32[]{:S(2)}) %collective-permute-start.10) | collective-permute-done | bytes 409632 | tf_op jit(solution)/shard_map/ppermute | solution.py:115
  88.5 11.7 %collective-permute-done.11.refs_4_ = bf16[200,8,128]{2,1,0:T(8,128)(2,1)S(1)} collective-permute-done((bf16[200,8,128]{2,1,0:T(8,128)(2,1)S(1)}, bf16[200,8,128]{2,1,0:T(8,128)(2,1)S(1)}, u32[]{:S(2)}, u32[]{:S(2)}) %collective-permute-start.11) | collective-permute-done | bytes 409632 | tf_op jit(solution)/shard_map/ppermute | solution.py:115
  100.2 0.7 copy-done.7
  101.1 1.5 %shard_map.177 = (bf16[304,8,128]{2,1,0:T(8,128)(2,1)S(1)}, bf16[496,8,128]{2,1,0:T(8,128)(2,1)S(1)}) custom-call(s32[1]{0:T(128)} %bitcast.refs_0_, bf16[200,8,128]{2,1,0:T(8,128)(2,1)} %copy-done, bf16[200,8,128]{2,1,0:T(8,128)(2,1)} %copy-done.8, bf16[200,8,128]{2,1,0:T(8,128)(2,1)} %copy-done.6, bf16[200,8,128]{2,1,0:T(8,128)(2,1)} %copy-done.7), custom_call_target="tpu_custom_call" | custom-call | tf_op jit(solution)/shard_map/pallas_call | solution.py:152
  102.5 2.6 %collective-permute-start.12 = (bf16[496,8,128]{2,1,0:T(8,128)(2,1)S(1)}, bf16[496,8,128]{2,1,0:T(8,128)(2,1)}, u32[]{:S(2)}, u32[]{:S(2)}) collective-permute-start(bf16[496,8,128]{2,1,0:T(8,128)(2,1)S(1)} %get-tuple-element.22), channel_id=1, source_target_pairs={{0,8},{1,9},{2,10},{3,11},{4,12},{5,13},{6,14},{7,15},{8,0},{9,1},... | collective-permute-start | bytes 3047432 | tf_op jit(solution)/shard_map/ppermute | solution.py:115
  105.1 0.7 add_select_fusion.2
  105.9 1.2 pad.25
  107.4 1.0 copy-done.3
  108.5 1.1 copy.38
  111.1 1.0 slice.75
  112.8 1.1 slice.72
  113.9 1.4 %fusion.9 = f32[225,149]{0,1:T(8,128)S(1)} fusion(f32[768,149]{1,0:T(8,128)S(1)} %fusion, f32[384,256]{1,0:T(8,128)S(1)} %bitcast.113, f32[384,256]{1,0:T(8,128)S(1)} %bitcast.112, s32[225]{0:T(256)S(1)} %copy-done.31, s32[149]{0:T(256)S(1)} %copy-done.30), kind=kOutput, calls=%fused_computation.21 | convolution fusion | flops 309239776 | bytes 1379756 | tf_op jit(solution)/shard_map/dot_general | solution.py:286
  116.0 0.8 fusion.6
  116.9 0.8 slice.82
  117.6 1.3 %fusion.89 = f32[450,149]{1,0:T(8,128)} fusion(f32[450,225]{1,0:T(8,128)S(1)} %copy-done.5, f32[225,149]{0,1:T(8,128)S(1)} %fusion.9), kind=kOutput, calls=%fused_computation.143 | convolution fusion | flops 181035008 | bytes 807300 | tf_op jit(solution)/shard_map/dot_general | solution.py:293
  118.9 2.1 %reshape.197 = f32[15,15,2,149]{3,2,1,0:T(2,128)} reshape(f32[450,149]{1,0:T(8,128)} %fusion.89) | data formatting | bytes 536400 | tf_op jit(solution)/shard_map/reshape | solution.py:294
  123.3 0.6 multiply_reduce_fusion
  123.9 0.6 copy-done.2
  124.5 0.7 fusion.7
  125.3 0.6 pad_maximum_fusion.6
  126.0 0.9 pad_maximum_fusion.2
  (118 shorter events, 7.4 us)
Async XLA Ops:
  4.2 36.5 %collective-permute-start.3 = (f32[24,256]{1,0:T(8,128)S(1)}, f32[24,256]{1,0:T(8,128)S(1)}, u32[]{:S(2)}, u32[]{:S(2)}) collective-permute-start(f32[24,256]{1,0:T(8,128)S(1)} %pad.9), channel_id=1, source_target_pairs={{0,2},{1,3},{2,0},{3,1},{4,6},{5,7},{6,4},{7,5},{8,10},{9,11},{10,... | collective-permute-start | bytes 73736 | tf_op jit(solution)/shard_map/ppermute | solution.py:115
  7.9 0.7 copy-start.1
  8.7 69.1 %collective-permute-start = (bf16[4,2,19,8,128]{4,3,2,1,0:T(8,128)(2,1)S(1)}, bf16[4,2,19,8,128]{4,3,2,1,0:T(8,128)(2,1)S(1)}, u32[]{:S(2)}, u32[]{:S(2)}) collective-permute-start(bf16[4,2,19,8,128]{4,3,2,1,0:T(8,128)(2,1)S(1)} %get-tuple-element.14), channel_id=1, source_target_pairs={{0,16},{1,17},{2,18},{3,19},{4,20},{5,21},{6,22},{7,23},{8,24},{9,... | collective-permute-start | bytes 933896 | tf_op jit(solution)/shard_map/ppermute | solution.py:115
  10.3 67.4 %collective-permute-start.1 = (bf16[4,2,19,8,128]{4,3,2,1,0:T(8,128)(2,1)S(1)}, bf16[4,2,19,8,128]{4,3,2,1,0:T(8,128)(2,1)S(1)}, u32[]{:S(2)}, u32[]{:S(2)}) collective-permute-start(bf16[4,2,19,8,128]{4,3,2,1,0:T(8,128)(2,1)S(1)} %get-tuple-element.15), channel_id=1, source_target_pairs={{0,32},{1,33},{2,34},{3,35},{4,36},{5,37},{6,38},{7,39},{8,40},{9,... | collective-permute-start | bytes 933896 | tf_op jit(solution)/shard_map/ppermute | solution.py:115
  13.3 64.5 %collective-permute-start.2 = (bf16[4,2,19,8,128]{4,3,2,1,0:T(8,128)(2,1)S(1)}, bf16[4,2,19,8,128]{4,3,2,1,0:T(8,128)(2,1)}, u32[]{:S(2)}, u32[]{:S(2)}) collective-permute-start(bf16[4,2,19,8,128]{4,3,2,1,0:T(8,128)(2,1)S(1)} %get-tuple-element.16), channel_id=1, source_target_pairs={{0,48},{1,49},{2,50},{3,51},{4,52},{5,53},{6,54},{7,55},{8,56},{9,... | collective-permute-start | bytes 933896 | tf_op jit(solution)/shard_map/ppermute | solution.py:115
  15.9 9.7 %copy-start.20 = (s32[2,4,4,19]{3,2,1,0:T(4,128)S(1)}, s32[2,4,4,19]{3,2,1,0:T(4,128)}, u32[]{:S(2)}) copy-start(s32[2,4,4,19]{3,2,1,0:T(4,128)} %constant.155.clone) | copy-start | bytes 7300
  16.0 9.7 %copy-start.21 = (s32[2,4,4,19]{3,2,1,0:T(4,128)S(1)}, s32[2,4,4,19]{3,2,1,0:T(4,128)}, u32[]{:S(2)}) copy-start(s32[2,4,4,19]{3,2,1,0:T(4,128)} %constant.156.clone) | copy-start | bytes 7300
  16.0 9.7 %copy-start.22 = (s32[2,4,4,19]{3,2,1,0:T(4,128)S(1)}, s32[2,4,4,19]{3,2,1,0:T(4,128)}, u32[]{:S(2)}) copy-start(s32[2,4,4,19]{3,2,1,0:T(4,128)} %constant.157.clone) | copy-start | bytes 7300
  16.0 9.7 %copy-start.23 = (s32[2,4,4,19]{3,2,1,0:T(4,128)S(1)}, s32[2,4,4,19]{3,2,1,0:T(4,128)}, u32[]{:S(2)}) copy-start(s32[2,4,4,19]{3,2,1,0:T(4,128)} %constant.158.clone) | copy-start | bytes 7300
  16.0 9.8 %copy-start.24 = (s32[608,2]{0,1:T(2,128)S(1)}, s32[608,2]{0,1:T(2,128)}, u32[]{:S(2)}) copy-start(s32[608,2]{0,1:T(2,128)} %param.17) | copy-start | bytes 14596
  16.0 106.4 %all-to-all-start = ((bf16[32,19,8,128]{3,2,1,0:T(8,128)(2,1)}), bf16[32,19,8,128]{3,2,1,0:T(8,128)(2,1)S(1)}, u32[]{:S(2)}, u32[]{:S(2)}) async-start(bf16[32,19,8,128]{3,2,1,0:T(8,128)(2,1)} %shard_map.178), calls=%async_computation | async-start | bytes 2490368 | tf_op jit(solution)/shard_map/all_to_all | solution.py:214
  25.6 17.8 %copy-start.32 = (s32[149]{0:T(256)}, s32[149]{0:T(256)S(1)}, u32[]{:S(2)}) copy-start(s32[149]{0:T(256)S(1)} %iota_add_fusion.1) | copy-start | bytes 1792
  25.8 17.5 %copy-start.26 = (s32[608]{0:T(1024)}, s32[608]{0:T(1024)S(1)}, u32[]{:S(2)}) copy-start(s32[608]{0:T(1024)S(1)} %get-tuple-element.23) | copy-start | bytes 7300
  25.8 17.5 %copy-start.28 = (s32[608]{0:T(1024)}, s32[608]{0:T(1024)S(1)}, u32[]{:S(2)}) copy-start(s32[608]{0:T(1024)S(1)} %get-tuple-element.24) | copy-start | bytes 7300
  27.3 49.6 %copy-start.13 = (bf16[608,149]{0,1:T(8,128)(2,1)}, bf16[608,149]{0,1:T(8,128)(2,1)S(1)}, u32[]{:S(2)}) copy-start(bf16[608,149]{0,1:T(8,128)(2,1)S(1)} %fusion.8) | copy-start | bytes 543556
  40.8 4.7 %collective-permute-start.4 = (f32[24,256]{1,0:T(8,128)S(1)}, f32[24,256]{1,0:T(8,128)S(1)}, u32[]{:S(2)}, u32[]{:S(2)}) collective-permute-start(f32[24,256]{1,0:T(8,128)S(1)} %pad_add_fusion), channel_id=1, source_target_pairs={{0,4},{1,5},{2,6},{3,7},{4,0},{5,1},{6,2},{7,3},{8,12},{9,13},{10,... | collective-permute-start | bytes 73736 | tf_op jit(solution)/shard_map/ppermute | solution.py:115
  45.5 5.1 %collective-permute-start.5 = (f32[24,256]{1,0:T(8,128)S(1)}, f32[24,256]{1,0:T(8,128)S(1)}, u32[]{:S(2)}, u32[]{:S(2)}) collective-permute-start(f32[24,256]{1,0:T(8,128)S(1)} %add.145), channel_id=1, source_target_pairs={{0,0},{1,1},{2,18},{3,19},{4,36},{5,37},{6,54},{7,55},{8,8},{9,9},... | collective-permute-start | bytes 73736 | tf_op jit(solution)/shard_map/ppermute | solution.py:115
  46.2 10.6 %collective-permute-start.6 = (f32[24,256]{1,0:T(8,128)S(1)}, f32[24,256]{1,0:T(8,128)S(1)}, u32[]{:S(2)}, u32[]{:S(2)}) collective-permute-start(f32[24,256]{1,0:T(8,128)S(1)} %add.145), channel_id=1, source_target_pairs={{0,1},{1,0},{2,19},{3,18},{4,37},{5,36},{6,55},{7,54},{8,9},{9,8},... | collective-permute-start | bytes 73736 | tf_op jit(solution)/shard_map/ppermute | solution.py:115
  56.8 15.5 %collective-permute-start.7 = (f32[24,256]{1,0:T(8,128)S(1)}, f32[24,256]{1,0:T(8,128)S(1)}, u32[]{:S(2)}, u32[]{:S(2)}) collective-permute-start(f32[24,256]{1,0:T(8,128)S(1)} %add.146), channel_id=1, source_target_pairs={{0,2},{1,3},{2,0},{3,1},{4,6},{5,7},{6,4},{7,5},{8,10},{9,11},{10,... | collective-permute-start | bytes 73736 | tf_op jit(solution)/shard_map/ppermute | solution.py:115
  72.3 4.4 %collective-permute-start.8 = (f32[2,24,256]{2,1,0:T(8,128)S(1)}, f32[2,24,256]{2,1,0:T(8,128)S(1)}, u32[]{:S(2)}, u32[]{:S(2)}) collective-permute-start(f32[2,24,256]{2,1,0:T(8,128)S(1)} %pad_maximum_fusion.5), channel_id=1, source_target_pairs={{0,4},{1,5},{2,6},{3,7},{4,0},{5,1},{6,2},{7,3},{8,12},{9,13},{10,... | collective-permute-start | bytes 147464 | tf_op jit(solution)/shard_map/ppermute | solution.py:115
  77.7 0.8 copy-start.9
  77.8 0.8 copy-start.10
  80.0 20.2 %copy-start = (bf16[200,8,128]{2,1,0:T(8,128)(2,1)}, bf16[200,8,128]{2,1,0:T(8,128)(2,1)S(1)}, u32[]{:S(2)}) copy-start(bf16[200,8,128]{2,1,0:T(8,128)(2,1)S(1)} %get-tuple-element.17.refs_1_) | copy-start | bytes 1228804
  80.0 8.5 %collective-permute-start.10 = (bf16[200,8,128]{2,1,0:T(8,128)(2,1)S(1)}, bf16[200,8,128]{2,1,0:T(8,128)(2,1)S(1)}, u32[]{:S(2)}, u32[]{:S(2)}) collective-permute-start(bf16[200,8,128]{2,1,0:T(8,128)(2,1)S(1)} %get-tuple-element.19), channel_id=1, source_target_pairs={{0,128},{1,129},{2,130},{3,131},{4,132},{5,133},{6,134},{7,135},{8... | collective-permute-start | bytes 1228808 | tf_op jit(solution)/shard_map/ppermute | solution.py:115
  83.0 17.2 %collective-permute-start.11 = (bf16[200,8,128]{2,1,0:T(8,128)(2,1)S(1)}, bf16[200,8,128]{2,1,0:T(8,128)(2,1)S(1)}, u32[]{:S(2)}, u32[]{:S(2)}) collective-permute-start(bf16[200,8,128]{2,1,0:T(8,128)(2,1)S(1)} %get-tuple-element.20), channel_id=1, source_target_pairs={{0,192},{1,193},{2,194},{3,195},{4,196},{5,197},{6,198},{7,199},{8... | collective-permute-start | bytes 1228808 | tf_op jit(solution)/shard_map/ppermute | solution.py:115
  83.8 16.4 %collective-permute-start.9 = (bf16[200,8,128]{2,1,0:T(8,128)(2,1)S(1)}, bf16[200,8,128]{2,1,0:T(8,128)(2,1)S(1)}, u32[]{:S(2)}, u32[]{:S(2)}) collective-permute-start(bf16[200,8,128]{2,1,0:T(8,128)(2,1)S(1)} %get-tuple-element.18), channel_id=1, source_target_pairs={{0,64},{1,65},{2,66},{3,67},{4,68},{5,69},{6,70},{7,71},{8,72},{9,... | collective-permute-start | bytes 1228808 | tf_op jit(solution)/shard_map/ppermute | solution.py:115
  85.3 19.8 %copy-start.16 = (s32[2,4,4,24]{3,2,1,0:T(4,128)S(1)}, s32[2,4,4,24]{3,2,1,0:T(4,128)}, u32[]{:S(2)}) copy-start(s32[2,4,4,24]{3,2,1,0:T(4,128)} %constant.160.clone) | copy-start | bytes 9220
  85.3 19.8 %copy-start.17 = (s32[2,4,4,24]{3,2,1,0:T(4,128)S(1)}, s32[2,4,4,24]{3,2,1,0:T(4,128)}, u32[]{:S(2)}) copy-start(s32[2,4,4,24]{3,2,1,0:T(4,128)} %constant.161.clone) | copy-start | bytes 9220
  85.3 19.8 %copy-start.18 = (s32[2,4,4,24]{3,2,1,0:T(4,128)S(1)}, s32[2,4,4,24]{3,2,1,0:T(4,128)}, u32[]{:S(2)}) copy-start(s32[2,4,4,24]{3,2,1,0:T(4,128)} %constant.162.clone) | copy-start | bytes 9220
  85.3 19.8 %copy-start.19 = (s32[2,4,4,24]{3,2,1,0:T(4,128)S(1)}, s32[2,4,4,24]{3,2,1,0:T(4,128)}, u32[]{:S(2)}) copy-start(s32[2,4,4,24]{3,2,1,0:T(4,128)} %constant.163.clone) | copy-start | bytes 9220
  88.5 12.6 %copy-start.6 = (bf16[200,8,128]{2,1,0:T(8,128)(2,1)}, bf16[200,8,128]{2,1,0:T(8,128)(2,1)S(1)}, u32[]{:S(2)}) copy-start(bf16[200,8,128]{2,1,0:T(8,128)(2,1)S(1)} %collective-permute-done.10.refs_3_) | copy-start | bytes 1228804
  100.2 0.8 copy-start.7
  100.2 0.9 copy-start.8
  102.5 8.6 %collective-permute-start.12 = (bf16[496,8,128]{2,1,0:T(8,128)(2,1)S(1)}, bf16[496,8,128]{2,1,0:T(8,128)(2,1)}, u32[]{:S(2)}, u32[]{:S(2)}) collective-permute-start(bf16[496,8,128]{2,1,0:T(8,128)(2,1)S(1)} %get-tuple-element.22), channel_id=1, source_target_pairs={{0,8},{1,9},{2,10},{3,11},{4,12},{5,13},{6,14},{7,15},{8,0},{9,1},... | collective-permute-start | bytes 3047432 | tf_op jit(solution)/shard_map/ppermute | solution.py:115
  107.2 1.2 copy-start.3
  108.4 1.1 copy-start.11
  112.7 1.2 copy-start.30
  112.8 1.2 copy-start.31
  115.4 0.7 copy-start.25
  116.0 1.6 %copy-start.5 = (f32[450,225]{1,0:T(8,128)S(1)}, f32[450,225]{1,0:T(8,128)}, u32[]{:S(2)}) copy-start(f32[450,225]{1,0:T(8,128)} %constant.166.clone) | copy-start | bytes 1215004
  116.9 4.1 %copy-start.14 = (bf16[608,149]{0,1:T(8,128)(2,1)S(1)}, bf16[608,149]{0,1:T(8,128)(2,1)}, u32[]{:S(2)}) copy-start(bf16[608,149]{0,1:T(8,128)(2,1)} %copy-done.13) | copy-start | bytes 543556
  121.0 0.9 copy-start.15
  121.9 0.9 copy-start.12
  122.3 0.9 copy-start.27
  122.3 0.9 copy-start.29
  122.4 0.9 copy-start.33
  123.3 1.2 copy-start.2
  124.5 1.5 %copy-start.4 = (bf16[149,8,128]{2,1,0:T(8,128)(2,1)S(1)}, bf16[149,8,128]{2,1,0:T(8,128)(2,1)}, u32[]{:S(2)}) copy-start(bf16[149,8,128]{2,1,0:T(8,128)(2,1)} %slice.82) | copy-start | bytes 915460

commit v8 on v7

--- a/solution.py
+++ b/solution.py
@@ -242,46 +242,32 @@
         preferred_element_type=jnp.float32,
     )
 
-    total = near + far
-    total = jnp.stack([total, over_x(total, 1)])
-    total = jnp.concatenate([total, over_x(total, 2)]).reshape(4 * deep, 2, span)
-    total = total.transpose(1, 0, 2)
-    top = lax.reduce_precision(total, 8, 7)
-    sums = jnp.stack([top, total - top]).astype(jnp.bfloat16).reshape(-1, *tile)
-    count = sums.shape[0]
-
     def line_plan(scalars, ins, outs):
-        pairs = [
+        return [
             (ins[kz].at[scalars[0] ^ k, j], outs[k].at[pl.ds(j * quad + kz * held, held)])
             for k in range(4)
             for kz in range(4)
             for j in range(2)
         ]
-        return pairs + [(ins[4], outs[k].at[pl.ds(2 * quad, count)]) for k in range(4)]
-
-    lines = copied(line_plan, [y], [*planes, sums], [(2 * quad + count, *tile)] * 4)
+
+    lines = copied(line_plan, [y], planes, [(2 * quad, *tile)] * 4)
     lines[1:] = [over_y(lines[k], k) for k in (1, 2, 3)]
 
     def core_plan(scalars, ins, outs):
-        keep, give = outs
-        pairs = []
-        for k in range(4):
-            at = pl.ds(k * quad, quad)
-            pairs.append((ins[k].at[pl.ds(scalars[0] * quad, quad)], keep.at[at]))
-            pairs.append((ins[k].at[pl.ds((1 - scalars[0]) * quad, quad)], give.at[at]))
-            pairs.append(
-                (ins[k].at[pl.ds(2 * quad, count)], give.at[pl.ds(4 * quad + k * count, count)])
-            )
-        return pairs
-
-    keep, give = copied(core_plan, [c], lines, [(4 * quad, *tile), (4 * quad + 4 * count, *tile)])
+        return [
+            (ins[k].at[pl.ds((side ^ scalars[0]) * quad, quad)], outs[side].at[pl.ds(k * quad, quad)])
+            for k in range(4)
+            for side in range(2)
+        ]
+
+    keep, give = copied(core_plan, [c], lines, [(4 * quad, *tile)] * 2)
     got = permuted(give, lambda g, d: (g ^ 1, d))
 
-    def combined(value):
-        pieces = value[4 * quad :].reshape(4, 2, 2, 4 * deep, span).astype(jnp.float32)
-        return (pieces[:, 0] + pieces[:, 1]).transpose(0, 2, 1, 3).reshape(-1, col_dev)
-
-    total = jnp.concatenate([combined(give), combined(got)])
+    total = near + far
+    total = jnp.stack([total, over_x(total, 1)])
+    total = jnp.concatenate([total, over_x(total, 2)]).reshape(-1, col_dev)
+    total = jnp.concatenate([total, *(over_y(total, k) for k in (1, 2, 3))])
+    total = jnp.concatenate([total, permuted(total, lambda g, d: (g ^ 1, d))])
     scale = 1.0 / (rows_all * cols_all)
     coef = scale * lax.dot_general(total, pinv_f, (((0,), (0,)), ((), ())), precision=HIGH)[:modes]
     index = np.arange(FREQS)
@@ -296,7 +282,7 @@
     row_here = basis(grp * row_dev + jnp.arange(row_dev, dtype=jnp.int32), rows_all)
 
     cut = 4 * quad
-    first = [(keep, pinv_a[:, :cut], design_a[:cut]), (got[:cut], pinv_a[:, cut:], design_a[cut:])]
+    first = [(keep, pinv_a[:, :cut], design_a[:cut]), (got, pinv_a[:, cut:], design_a[cut:])]
     images, misfits = [], []
     for part, pieces in enumerate((first, [(block, pinv, design)])):
         here = cols[part * span : (part + 1) * span]

time: 128 us -> 134 us (1.047)
  starting transfers between devices: 44.7 us -> 54.8 us
  local copies, waits for them, and re-layouts: 14.3 us -> 9.35 us
  matrix products: 15.6 us -> 19.7 us
  other arithmetic: 6 us -> 3.59 us
    ppermute x13 -> x17, starting transfers between devices: 35.2 us -> 45.5 us  [permuted(): return lax.ppermute(value, ('grp', 'dev'), pairs)]
    dot_general x3, matrix products: 1.09 us -> 5.45 us  [on_device(): jnp.dot(some_pinv, flat, preferred_element_type=jnp.float32)]
    dot_general x3, matrix products: 1.43 us -> 3.79 us  [on_device(): jnp.dot(some_design, series.astype(jnp.bfloat16), preferred_element_type=...]
    slice x5 -> x0, local copies, waits for them, and re-layouts: 2.31 us -> none  [the longest x1 1.12 us: on_device(): got[:cut]]
    unnamed x76 -> x64, local copies, waits for them, and re-layouts: 8.1 us -> 5.82 us
    dot_general x2, matrix products: 3.43 us -> 1.6 us  [on_device(): lax.dot_general(inverse, some.astype(jnp.float32), (((1,), (1,)), ((), ()...]
    dot_general x1, matrix products: 2.9 us -> 1.2 us  [on_device(): half = jnp.einsum('ihw,ha->iaw', wide, rows, precision=HIGH)]
    ppermute x13 -> x17, waiting for transfers between devices: 26.4 us -> 25.9 us  [permuted(): return lax.ppermute(value, ('grp', 'dev'), pairs)]
  transfers between devices with their start and end apart: 14 -> 18, of which waited for: 5 -> 9; matrix products, arithmetic and copies ran while one was open for 19% -> 18% of each run, Pallas kernels for 15% -> 13%
where the time goes in v8:
time: 134 us; the launch traced here: 133 us
  starting transfers between devices  54.8 us (41%)
  waiting for transfers between devices  25.9 us (19%)
  matrix products  19.7 us (15%)
  Pallas kernels  18.3 us (14%)
  local copies, waits for them, and re-layouts  9.35 us (7%)
  other arithmetic  3.59 us (3%)
    ppermute x17, starting transfers between devices, permuted(): return lax.ppermute(value, ('grp', 'dev'), pairs)  45.5 us
    ppermute x17, waiting for transfers between devices, permuted(): return lax.ppermute(value, ('grp', 'dev'), pairs)  25.9 us
    pallas_call x1, Pallas kernels, inverse_of(): pl.pallas_call(sweep_kernel, out_shape=jax.ShapeDtypeStruct((size, width)...  11.4 us
    all_to_all x1, starting transfers between devices, on_device(): block = lax.all_to_all(packed, 'grp', 0, 0, tiled=True)  9.31 us
    pallas_call x4, Pallas kernels, copied(): pl.pallas_call(body, out_shape=[pltpu.VMEM(shape, arrays[0].dtype) for sh...  6.87 us
    unnamed x64, local copies, waits for them, and re-layouts  5.82 us
    dot_general x3, matrix products, on_device(): jnp.dot(some_pinv, flat, preferred_element_type=jnp.float32)  5.45 us
    dot_general x3, matrix products, on_device(): jnp.dot(some_design, series.astype(jnp.bfloat16), preferred_element_type=...  3.79 us
  transfers between devices with their start and end apart: 18, of which 9 were waited for; matrix products, arithmetic and copies ran while one was open for 18% of the time, Pallas kernels for 13%

profile of v8, /device:TPU:1, one launch (start us, length us, event | category | flops | bytes accessed | tf_op | source)
XLA Modules:
  0.0 132.9 jit_solution(5215646409504813671)
XLA Ops:
  0.7 1.6 %shard_map.175 = (bf16[4,2,19,8,128]{4,3,2,1,0:T(8,128)(2,1)S(1)}, bf16[4,2,19,8,128]{4,3,2,1,0:T(8,128)(2,1)S(1)}, bf16[4,2,19,8,128]{4,3,2,1,0:T(8,128)(2,1)S(1)}, bf16[4,2,19,8,128]{4,3,2,1,0:T(8,128)(2,1)S(1)}) custom-call(s32[1]{0:T(128)} %bitcast.2.refs_0_, bf16[19,4,4,2,8,256]{5,4,3,2,1,0:T(8,128)(2,1)} %bitcast.67), custom_call_target="tpu_custom_call" | custom-call | tf_op jit(solution)/shard_map/pallas_call | solution.py:152
  2.3 0.7 copy-done
  3.0 2.5 %collective-permute-start = (bf16[4,2,19,8,128]{4,3,2,1,0:T(8,128)(2,1)S(1)}, bf16[4,2,19,8,128]{4,3,2,1,0:T(8,128)(2,1)}, u32[]{:S(2)}, u32[]{:S(2)}) collective-permute-start(bf16[4,2,19,8,128]{4,3,2,1,0:T(8,128)(2,1)S(1)} %get-tuple-element.14), channel_id=1, source_target_pairs={{0,16},{1,17},{2,18},{3,19},{4,20},{5,21},{6,22},{7,23},{8,24},{9,... | collective-permute-start | bytes 933896 | tf_op jit(solution)/shard_map/ppermute | solution.py:115
  5.4 3.0 %collective-permute-start.1 = (bf16[4,2,19,8,128]{4,3,2,1,0:T(8,128)(2,1)S(1)}, bf16[4,2,19,8,128]{4,3,2,1,0:T(8,128)(2,1)}, u32[]{:S(2)}, u32[]{:S(2)}) collective-permute-start(bf16[4,2,19,8,128]{4,3,2,1,0:T(8,128)(2,1)S(1)} %get-tuple-element.15), channel_id=1, source_target_pairs={{0,32},{1,33},{2,34},{3,35},{4,36},{5,37},{6,38},{7,39},{8,40},{9,... | collective-permute-start | bytes 933896 | tf_op jit(solution)/shard_map/ppermute | solution.py:115
  8.4 2.6 %shard_map.178 = bf16[32,19,8,128]{3,2,1,0:T(8,128)(2,1)} custom-call(bf16[19,32,8,256]{3,2,1,0:T(8,128)(2,1)} %bitcast.68), custom_call_target="tpu_custom_call" | custom-call | tf_op jit(solution)/shard_map/pallas_call | solution.py:152
  11.1 9.3 %all-to-all-start = ((bf16[32,19,8,128]{3,2,1,0:T(8,128)(2,1)}), bf16[32,19,8,128]{3,2,1,0:T(8,128)(2,1)}, u32[]{:S(2)}, u32[]{:S(2)}) async-start(bf16[32,19,8,128]{3,2,1,0:T(8,128)(2,1)} %shard_map.178), calls=%async_computation | async-start | bytes 2490368 | tf_op jit(solution)/shard_map/all_to_all | solution.py:214
  20.4 1.2 convolution_bitcast_fusion
  22.3 1.3 collective-permute-start.7
  24.4 0.8 select_add_fusion.normal_ref
  25.2 11.4 %sweep.1 = f32[152,256]{1,0:T(8,128)} custom-call(f32[152,256]{1,0:T(8,128)} %select_add_fusion.normal_ref), custom_call_target="tpu_custom_call" | custom-call | flops 30000000 | bytes 300000 | tf_op jit(solution)/shard_map/sweep/pallas_call | solution.py:67
  38.2 2.5 %collective-permute-start.8 = (f32[24,256]{1,0:T(8,128)S(1)}, f32[24,256]{1,0:T(8,128)S(1)}, u32[]{:S(2)}, u32[]{:S(2)}) collective-permute-start(f32[24,256]{1,0:T(8,128)S(1)} %pad_add_fusion), channel_id=1, source_target_pairs={{0,4},{1,5},{2,6},{3,7},{4,0},{5,1},{6,2},{7,3},{8,12},{9,13},{10,... | collective-permute-start | bytes 73736 | tf_op jit(solution)/shard_map/ppermute | solution.py:115
  40.9 1.6 %collective-permute-done.8 = f32[24,256]{1,0:T(8,128)S(1)} collective-permute-done((f32[24,256]{1,0:T(8,128)S(1)}, f32[24,256]{1,0:T(8,128)S(1)}, u32[]{:S(2)}, u32[]{:S(2)}) %collective-permute-start.8) | collective-permute-done | bytes 24608 | tf_op jit(solution)/shard_map/ppermute | solution.py:115
  42.5 4.2 %collective-permute-start.10 = (f32[24,256]{1,0:T(8,128)S(1)}, f32[24,256]{1,0:T(8,128)S(1)}, u32[]{:S(2)}, u32[]{:S(2)}) collective-permute-start(f32[24,256]{1,0:T(8,128)S(1)} %add.134), channel_id=1, source_target_pairs={{0,1},{1,0},{2,19},{3,18},{4,37},{5,36},{6,55},{7,54},{8,9},{9,8},... | collective-permute-start | bytes 73736 | tf_op jit(solution)/shard_map/ppermute | solution.py:115
  47.4 1.4 %fusion = f32[768,149]{1,0:T(8,128)} fusion(bf16[149,608]{1,0:T(8,128)(2,1)S(1)} %convolution_convert_fusion, s32[768]{0:T(1024)S(1)} %eq.95), kind=kOutput, calls=%fused_computation.2 | convolution fusion | flops 139616256 | bytes 641984 | tf_op jit(solution)/shard_map/dot_general | solution.py:238
  48.8 3.6 %collective-permute-done.10 = f32[24,256]{1,0:T(8,128)S(1)} collective-permute-done((f32[24,256]{1,0:T(8,128)S(1)}, f32[24,256]{1,0:T(8,128)S(1)}, u32[]{:S(2)}, u32[]{:S(2)}) %collective-permute-start.10) | collective-permute-done | bytes 24608 | tf_op jit(solution)/shard_map/ppermute | solution.py:115
  52.3 15.2 %collective-permute-start.11 = (f32[24,256]{1,0:T(8,128)S(1)}, f32[24,256]{1,0:T(8,128)S(1)}, u32[]{:S(2)}, u32[]{:S(2)}) collective-permute-start(f32[24,256]{1,0:T(8,128)S(1)} %add.135), channel_id=1, source_target_pairs={{0,2},{1,3},{2,0},{3,1},{4,6},{5,7},{6,4},{7,5},{8,10},{9,11},{10,... | collective-permute-start | bytes 73736 | tf_op jit(solution)/shard_map/ppermute | solution.py:115
  67.7 1.1 collective-permute-done.11
  68.8 0.8 fusion.8
  69.7 3.6 %collective-permute-done.12 = f32[2,24,256]{2,1,0:T(8,128)S(1)} collective-permute-done((f32[2,24,256]{2,1,0:T(8,128)S(1)}, f32[2,24,256]{2,1,0:T(8,128)S(1)}, u32[]{:S(2)}, u32[]{:S(2)}) %collective-permute-start.12) | collective-permute-done | bytes 49184 | tf_op jit(solution)/shard_map/ppermute | solution.py:115
  73.3 1.4 %collective-permute-start.13 = (f32[96,256]{1,0:T(8,128)S(1)}, f32[96,256]{1,0:T(8,128)S(1)}, u32[]{:S(2)}, u32[]{:S(2)}) collective-permute-start(f32[96,256]{1,0:T(8,128)S(1)} %bitcast.79), channel_id=1, source_target_pairs={{0,64},{1,65},{2,66},{3,67},{4,68},{5,69},{6,70},{7,71},{8,72},{9,... | collective-permute-start | bytes 294920 | tf_op jit(solution)/shard_map/ppermute | solution.py:115
  74.6 1.0 convolution_convert_fusion.1
  76.2 2.7 %collective-permute-start.14 = (f32[96,256]{1,0:T(8,128)S(1)}, f32[96,256]{1,0:T(8,128)S(1)}, u32[]{:S(2)}, u32[]{:S(2)}) collective-permute-start(f32[96,256]{1,0:T(8,128)S(1)} %bitcast.80), channel_id=1, source_target_pairs={{0,128},{1,129},{2,130},{3,131},{4,132},{5,133},{6,134},{7,135},{8... | collective-permute-start | bytes 294920 | tf_op jit(solution)/shard_map/ppermute | solution.py:115
  78.9 0.8 collective-permute-start.15
  80.3 0.9 collective-permute-done.14
  81.2 2.3 %collective-permute-done.15 = f32[96,256]{1,0:T(8,128)S(1)} collective-permute-done((f32[96,256]{1,0:T(8,128)S(1)}, f32[96,256]{1,0:T(8,128)S(1)}, u32[]{:S(2)}, u32[]{:S(2)}) %collective-permute-start.15) | collective-permute-done | bytes 98336 | tf_op jit(solution)/shard_map/ppermute | solution.py:115
  83.6 0.8 pad_maximum_fusion.1
  84.3 5.8 %collective-permute-start.16 = (f32[384,256]{1,0:T(8,128)}, f32[384,256]{1,0:T(8,128)}, u32[]{:S(2)}, u32[]{:S(2)}) collective-permute-start(f32[384,256]{1,0:T(8,128)} %pad_maximum_fusion.1), channel_id=1, source_target_pairs={{0,8},{1,9},{2,10},{3,11},{4,12},{5,13},{6,14},{7,15},{8,0},{9,1},... | collective-permute-start | bytes 1179656 | tf_op jit(solution)/shard_map/ppermute | solution.py:115
  90.1 1.3 %shard_map.176 = (bf16[152,8,128]{2,1,0:T(8,128)(2,1)S(1)}, bf16[152,8,128]{2,1,0:T(8,128)(2,1)S(1)}, bf16[152,8,128]{2,1,0:T(8,128)(2,1)S(1)}, bf16[152,8,128]{2,1,0:T(8,128)(2,1)S(1)}) custom-call(s32[1]{0:T(128)} %bitcast.1.refs_0_, bf16[4,2,19,8,128]{4,3,2,1,0:T(8,128)(2,1)} %copy-done, bf16[4,2,19,8,128]{4,3,2,1,0:T(8,128)(2,1)} %collective-permute-done.refs_2_, ...), custom_call_target="tpu_custom_call" | custom-call | tf_op jit(solution)/shard_map/pallas_call | solution.py:152
  91.6 2.4 %collective-permute-start.4 = (bf16[152,8,128]{2,1,0:T(8,128)(2,1)S(1)}, bf16[152,8,128]{2,1,0:T(8,128)(2,1)S(1)}, u32[]{:S(2)}, u32[]{:S(2)}) collective-permute-start(bf16[152,8,128]{2,1,0:T(8,128)(2,1)S(1)} %get-tuple-element.19), channel_id=1, source_target_pairs={{0,128},{1,129},{2,130},{3,131},{4,132},{5,133},{6,134},{7,135},{8... | collective-permute-start | bytes 933896 | tf_op jit(solution)/shard_map/ppermute | solution.py:115
  94.0 1.4 %collective-permute-start.5 = (bf16[152,8,128]{2,1,0:T(8,128)(2,1)S(1)}, bf16[152,8,128]{2,1,0:T(8,128)(2,1)S(1)}, u32[]{:S(2)}, u32[]{:S(2)}) collective-permute-start(bf16[152,8,128]{2,1,0:T(8,128)(2,1)S(1)} %get-tuple-element.20), channel_id=1, source_target_pairs={{0,192},{1,193},{2,194},{3,195},{4,196},{5,197},{6,198},{7,199},{8... | collective-permute-start | bytes 933896 | tf_op jit(solution)/shard_map/ppermute | solution.py:115
  97.4 3.1 %collective-permute-done.3.refs_2_ = bf16[152,8,128]{2,1,0:T(8,128)(2,1)S(1)} collective-permute-done((bf16[152,8,128]{2,1,0:T(8,128)(2,1)S(1)}, bf16[152,8,128]{2,1,0:T(8,128)(2,1)S(1)}, u32[]{:S(2)}, u32[]{:S(2)}) %collective-permute-start.3) | collective-permute-done | bytes 311328 | tf_op jit(solution)/shard_map/ppermute | solution.py:115
  100.5 7.7 %collective-permute-done.4.refs_3_ = bf16[152,8,128]{2,1,0:T(8,128)(2,1)S(1)} collective-permute-done((bf16[152,8,128]{2,1,0:T(8,128)(2,1)S(1)}, bf16[152,8,128]{2,1,0:T(8,128)(2,1)S(1)}, u32[]{:S(2)}, u32[]{:S(2)}) %collective-permute-start.4) | collective-permute-done | bytes 311328 | tf_op jit(solution)/shard_map/ppermute | solution.py:115
  108.2 2.1 %collective-permute-done.5.refs_4_ = bf16[152,8,128]{2,1,0:T(8,128)(2,1)S(1)} collective-permute-done((bf16[152,8,128]{2,1,0:T(8,128)(2,1)S(1)}, bf16[152,8,128]{2,1,0:T(8,128)(2,1)S(1)}, u32[]{:S(2)}, u32[]{:S(2)}) %collective-permute-start.5) | collective-permute-done | bytes 311328 | tf_op jit(solution)/shard_map/ppermute | solution.py:115
  110.2 0.7 copy-done.9
  111.0 1.3 %shard_map.177 = (bf16[304,8,128]{2,1,0:T(8,128)(2,1)S(1)}, bf16[304,8,128]{2,1,0:T(8,128)(2,1)S(1)}) custom-call(s32[1]{0:T(128)} %bitcast.refs_0_, bf16[152,8,128]{2,1,0:T(8,128)(2,1)} %copy-done.1, bf16[152,8,128]{2,1,0:T(8,128)(2,1)} %copy-done.7, bf16[152,8,128]{2,1,0:T(8,128)(2,1)} %copy-done.8, bf16[152,8,128]{2,1,0:T(8,128)(2,1)} %copy-done.9), custom_call_target="tpu_custom_call" | custom-call | tf_op jit(solution)/shard_map/pallas_call | solution.py:152
  112.3 1.5 %collective-permute-start.6 = (bf16[304,8,128]{2,1,0:T(8,128)(2,1)S(1)}, bf16[304,8,128]{2,1,0:T(8,128)(2,1)}, u32[]{:S(2)}, u32[]{:S(2)}) collective-permute-start(bf16[304,8,128]{2,1,0:T(8,128)(2,1)S(1)} %get-tuple-element.22), channel_id=1, source_target_pairs={{0,8},{1,9},{2,10},{3,11},{4,12},{5,13},{6,14},{7,15},{8,0},{9,1},... | collective-permute-start | bytes 1867784 | tf_op jit(solution)/shard_map/ppermute | solution.py:115
  113.8 2.1 %fusion.15 = f32[149,1024]{1,0:T(8,128)} fusion(bf16[38,8,8,128]{3,2,1,0:T(8,128)(2,1)S(1)} %bitcast.65, bf16[149,608]{1,0:T(8,128)(2,1)} %convolution_convert_fusion.1), kind=kOutput, calls=%fused_computation.27 | convolution fusion | flops 92766208 | bytes 1349632 | tf_op jit(solution)/shard_map/dot_general | solution.py:296
  116.0 1.1 constant_dynamic-update-slice_fusion
  117.1 1.4 %fusion.9 = f32[225,149]{0,1:T(8,128)S(1)} fusion(f32[768,149]{1,0:T(8,128)S(1)} %copy-done.4, f32[768,256]{1,0:T(8,128)S(1)} %constant_dynamic-update-slice_fusion, s32[225]{0:T(256)S(1)} %copy-done.26, s32[149]{0:T(256)S(1)} %copy-done.25), kind=kOutput, calls=%fused_computation.21 | convolution fusion | flops 309066976 | bytes 1379756 | tf_op jit(solution)/shard_map/dot_general | solution.py:272
  118.5 1.3 fusion.83
  119.8 2.1 %reshape.178 = f32[15,15,2,149]{3,2,1,0:T(2,128)} reshape(f32[450,149]{1,0:T(8,128)} %fusion.83) | data formatting | bytes 536400 | tf_op jit(solution)/shard_map/reshape | solution.py:280
  121.9 1.7 %convolution_add_fusion = f32[149,1024]{1,0:T(8,128)S(1)} fusion(f32[149,1024]{1,0:T(8,128)} %fusion.15, bf16[38,8,8,128]{3,2,1,0:T(8,128)(2,1)} %bitcast.18, bf16[149,608]{1,0:T(8,128)(2,1)} %convolution_convert_fusion.1), kind=kOutput, calls=%fused_computation.10 | convolution fusion | flops 92918784 | bytes 1972224 | tf_op jit(solution)/shard_map/dot_general | solution.py:296
  123.6 0.7 fusion.6
  124.5 1.5 %multiply_reduce_fusion.1 = f32[1024]{0:T(1024)S(1)} fusion(bf16[38,8,8,128]{3,2,1,0:T(8,128)(2,1)} %bitcast.18, f32[149,1024]{1,0:T(8,128)S(1)} %convolution_add_fusion, bf16[608,149]{0,1:T(8,128)(2,1)S(1)} %copy-done.13), kind=kOutput, calls=%fused_computation.13 | convolution fusion | flops 94162944 | bytes 1366016 | tf_op jit(solution)/shard_map/dot_general | solution.py:302
  127.0 1.7 %fusion.4 = f32[149,1024]{1,0:T(8,128)S(1)} fusion(bf16[149,608]{1,0:T(8,128)(2,1)S(1)} %copy-done.11, bf16[76,8,8,128]{3,2,1,0:T(8,128)(2,1)} %bitcast.28), kind=kOutput, calls=%fused_computation.11 | convolution fusion | flops 185532416 | bytes 2036672 | tf_op jit(solution)/shard_map/dot_general | solution.py:296
  128.7 1.9 %multiply_reduce_fusion = f32[1024]{0:T(1024)S(1)} fusion(bf16[76,8,8,128]{3,2,1,0:T(8,128)(2,1)} %bitcast.28, f32[149,1024]{1,0:T(8,128)S(1)} %fusion.4, s32[149]{0:T(256)S(1)} %iota_add_fusion.1, s32[608]{0:T(1024)S(1)} %get-tuple-element.24, s32[608]{0:T(1024)S(1)} %get-tuple-element.23), kind=kOutput, calls=%fused_computation | convolution fusion | flops 188717888 | bytes 1865044 | tf_op jit(solution)/shard_map/dot_general | solution.py:302
  130.6 0.7 fusion.7
  132.0 0.9 pad_maximum_fusion
  (105 shorter events, 8.8 us)
Async XLA Ops:
  2.2 0.7 copy-start
  3.0 87.2 %collective-permute-start = (bf16[4,2,19,8,128]{4,3,2,1,0:T(8,128)(2,1)S(1)}, bf16[4,2,19,8,128]{4,3,2,1,0:T(8,128)(2,1)}, u32[]{:S(2)}, u32[]{:S(2)}) collective-permute-start(bf16[4,2,19,8,128]{4,3,2,1,0:T(8,128)(2,1)S(1)} %get-tuple-element.14), channel_id=1, source_target_pairs={{0,16},{1,17},{2,18},{3,19},{4,20},{5,21},{6,22},{7,23},{8,24},{9,... | collective-permute-start | bytes 933896 | tf_op jit(solution)/shard_map/ppermute | solution.py:115
  5.4 84.7 %collective-permute-start.1 = (bf16[4,2,19,8,128]{4,3,2,1,0:T(8,128)(2,1)S(1)}, bf16[4,2,19,8,128]{4,3,2,1,0:T(8,128)(2,1)}, u32[]{:S(2)}, u32[]{:S(2)}) collective-permute-start(bf16[4,2,19,8,128]{4,3,2,1,0:T(8,128)(2,1)S(1)} %get-tuple-element.15), channel_id=1, source_target_pairs={{0,32},{1,33},{2,34},{3,35},{4,36},{5,37},{6,38},{7,39},{8,40},{9,... | collective-permute-start | bytes 933896 | tf_op jit(solution)/shard_map/ppermute | solution.py:115
  8.4 81.7 %collective-permute-start.2 = (bf16[4,2,19,8,128]{4,3,2,1,0:T(8,128)(2,1)S(1)}, bf16[4,2,19,8,128]{4,3,2,1,0:T(8,128)(2,1)}, u32[]{:S(2)}, u32[]{:S(2)}) collective-permute-start(bf16[4,2,19,8,128]{4,3,2,1,0:T(8,128)(2,1)S(1)} %get-tuple-element.16), channel_id=1, source_target_pairs={{0,48},{1,49},{2,50},{3,51},{4,52},{5,53},{6,54},{7,55},{8,56},{9,... | collective-permute-start | bytes 933896 | tf_op jit(solution)/shard_map/ppermute | solution.py:115
  11.0 9.4 %copy-start.2 = (bf16[19,256,256]{2,1,0:T(8,128)(2,1)S(1)}, bf16[19,256,256]{2,1,0:T(8,128)(2,1)}, u32[]{:S(2)}) copy-start(bf16[19,256,256]{2,1,0:T(8,128)(2,1)} %param.16) | copy-start | bytes 7471108
  11.1 115.4 %all-to-all-start = ((bf16[32,19,8,128]{3,2,1,0:T(8,128)(2,1)}), bf16[32,19,8,128]{3,2,1,0:T(8,128)(2,1)}, u32[]{:S(2)}, u32[]{:S(2)}) async-start(bf16[32,19,8,128]{3,2,1,0:T(8,128)(2,1)} %shard_map.178), calls=%async_computation | async-start | bytes 2490368 | tf_op jit(solution)/shard_map/all_to_all | solution.py:214
  20.4 3.3 %copy-start.22 = (s32[608,2]{0,1:T(2,128)S(1)}, s32[608,2]{0,1:T(2,128)}, u32[]{:S(2)}) copy-start(s32[608,2]{0,1:T(2,128)} %param.17) | copy-start | bytes 14596
  22.3 15.9 %collective-permute-start.7 = (f32[24,256]{1,0:T(8,128)S(1)}, f32[24,256]{1,0:T(8,128)S(1)}, u32[]{:S(2)}, u32[]{:S(2)}) collective-permute-start(f32[24,256]{1,0:T(8,128)S(1)} %pad.9), channel_id=1, source_target_pairs={{0,2},{1,3},{2,0},{3,1},{4,6},{5,7},{6,4},{7,5},{8,10},{9,11},{10,... | collective-permute-start | bytes 73736 | tf_op jit(solution)/shard_map/ppermute | solution.py:115
  36.6 0.9 copy-start.5
  36.8 4.0 %copy-start.18 = (s32[2,4,4,24]{3,2,1,0:T(4,128)S(1)}, s32[2,4,4,24]{3,2,1,0:T(4,128)}, u32[]{:S(2)}) copy-start(s32[2,4,4,24]{3,2,1,0:T(4,128)} %constant.160.clone) | copy-start | bytes 9220
  36.8 4.0 %copy-start.19 = (s32[2,4,4,24]{3,2,1,0:T(4,128)S(1)}, s32[2,4,4,24]{3,2,1,0:T(4,128)}, u32[]{:S(2)}) copy-start(s32[2,4,4,24]{3,2,1,0:T(4,128)} %constant.161.clone) | copy-start | bytes 9220
  36.8 4.0 %copy-start.20 = (s32[2,4,4,24]{3,2,1,0:T(4,128)S(1)}, s32[2,4,4,24]{3,2,1,0:T(4,128)}, u32[]{:S(2)}) copy-start(s32[2,4,4,24]{3,2,1,0:T(4,128)} %constant.162.clone) | copy-start | bytes 9220
  36.8 3.9 %copy-start.21 = (s32[2,4,4,24]{3,2,1,0:T(4,128)S(1)}, s32[2,4,4,24]{3,2,1,0:T(4,128)}, u32[]{:S(2)}) copy-start(s32[2,4,4,24]{3,2,1,0:T(4,128)} %constant.163.clone) | copy-start | bytes 9220
  36.8 3.9 %copy-start.24 = (pred[2,4,4,24]{3,2,1,0:T(4,128)(4,1)S(1)}, pred[2,4,4,24]{3,2,1,0:T(4,128)(4,1)}, u32[]{:S(2)}) copy-start(pred[2,4,4,24]{3,2,1,0:T(4,128)(4,1)} %constant.164.clone) | copy-start | bytes 2308
  37.5 30.0 %copy-start.14 = (s32[2,4,4,19]{3,2,1,0:T(4,128)S(1)}, s32[2,4,4,19]{3,2,1,0:T(4,128)}, u32[]{:S(2)}) copy-start(s32[2,4,4,19]{3,2,1,0:T(4,128)} %constant.155.clone) | copy-start | bytes 7300
  37.5 30.0 %copy-start.15 = (s32[2,4,4,19]{3,2,1,0:T(4,128)S(1)}, s32[2,4,4,19]{3,2,1,0:T(4,128)}, u32[]{:S(2)}) copy-start(s32[2,4,4,19]{3,2,1,0:T(4,128)} %constant.156.clone) | copy-start | bytes 7300
  37.6 30.0 %copy-start.16 = (s32[2,4,4,19]{3,2,1,0:T(4,128)S(1)}, s32[2,4,4,19]{3,2,1,0:T(4,128)}, u32[]{:S(2)}) copy-start(s32[2,4,4,19]{3,2,1,0:T(4,128)} %constant.157.clone) | copy-start | bytes 7300
  37.6 30.0 %copy-start.17 = (s32[2,4,4,19]{3,2,1,0:T(4,128)S(1)}, s32[2,4,4,19]{3,2,1,0:T(4,128)}, u32[]{:S(2)}) copy-start(s32[2,4,4,19]{3,2,1,0:T(4,128)} %constant.158.clone) | copy-start | bytes 7300
  38.1 31.5 %copy-start.10 = (bf16[149,608]{1,0:T(8,128)(2,1)}, bf16[149,608]{1,0:T(8,128)(2,1)S(1)}, u32[]{:S(2)}) copy-start(bf16[149,608]{1,0:T(8,128)(2,1)S(1)} %convolution_convert_fusion) | copy-start | bytes 543556
  38.2 4.3 %collective-permute-start.8 = (f32[24,256]{1,0:T(8,128)S(1)}, f32[24,256]{1,0:T(8,128)S(1)}, u32[]{:S(2)}, u32[]{:S(2)}) collective-permute-start(f32[24,256]{1,0:T(8,128)S(1)} %pad_add_fusion), channel_id=1, source_target_pairs={{0,4},{1,5},{2,6},{3,7},{4,0},{5,1},{6,2},{7,3},{8,12},{9,13},{10,... | collective-permute-start | bytes 73736 | tf_op jit(solution)/shard_map/ppermute | solution.py:115
  42.5 9.9 %collective-permute-start.10 = (f32[24,256]{1,0:T(8,128)S(1)}, f32[24,256]{1,0:T(8,128)S(1)}, u32[]{:S(2)}, u32[]{:S(2)}) collective-permute-start(f32[24,256]{1,0:T(8,128)S(1)} %add.134), channel_id=1, source_target_pairs={{0,1},{1,0},{2,19},{3,18},{4,37},{5,36},{6,55},{7,54},{8,9},{9,8},... | collective-permute-start | bytes 73736 | tf_op jit(solution)/shard_map/ppermute | solution.py:115
  46.7 5.6 %collective-permute-start.9 = (f32[24,256]{1,0:T(8,128)S(1)}, f32[24,256]{1,0:T(8,128)S(1)}, u32[]{:S(2)}, u32[]{:S(2)}) collective-permute-start(f32[24,256]{1,0:T(8,128)S(1)} %add.134), channel_id=1, source_target_pairs={{0,0},{1,1},{2,18},{3,19},{4,36},{5,37},{6,54},{7,55},{8,8},{9,9},... | collective-permute-start | bytes 73736 | tf_op jit(solution)/shard_map/ppermute | solution.py:115
  52.3 16.4 %collective-permute-start.11 = (f32[24,256]{1,0:T(8,128)S(1)}, f32[24,256]{1,0:T(8,128)S(1)}, u32[]{:S(2)}, u32[]{:S(2)}) collective-permute-start(f32[24,256]{1,0:T(8,128)S(1)} %add.135), channel_id=1, source_target_pairs={{0,2},{1,3},{2,0},{3,1},{4,6},{5,7},{6,4},{7,5},{8,10},{9,11},{10,... | collective-permute-start | bytes 73736 | tf_op jit(solution)/shard_map/ppermute | solution.py:115
  68.8 4.4 %collective-permute-start.12 = (f32[2,24,256]{2,1,0:T(8,128)S(1)}, f32[2,24,256]{2,1,0:T(8,128)S(1)}, u32[]{:S(2)}, u32[]{:S(2)}) collective-permute-start(f32[2,24,256]{2,1,0:T(8,128)S(1)} %pad_maximum_fusion.3), channel_id=1, source_target_pairs={{0,4},{1,5},{2,6},{3,7},{4,0},{5,1},{6,2},{7,3},{8,12},{9,13},{10,... | collective-permute-start | bytes 147464 | tf_op jit(solution)/shard_map/ppermute | solution.py:115
  69.6 6.0 %copy-start.12 = (bf16[608,149]{0,1:T(8,128)(2,1)}, bf16[608,149]{0,1:T(8,128)(2,1)S(1)}, u32[]{:S(2)}) copy-start(bf16[608,149]{0,1:T(8,128)(2,1)S(1)} %fusion.8) | copy-start | bytes 543556
  73.3 5.6 %collective-permute-start.13 = (f32[96,256]{1,0:T(8,128)S(1)}, f32[96,256]{1,0:T(8,128)S(1)}, u32[]{:S(2)}, u32[]{:S(2)}) collective-permute-start(f32[96,256]{1,0:T(8,128)S(1)} %bitcast.79), channel_id=1, source_target_pairs={{0,64},{1,65},{2,66},{3,67},{4,68},{5,69},{6,70},{7,71},{8,72},{9,... | collective-permute-start | bytes 294920 | tf_op jit(solution)/shard_map/ppermute | solution.py:115
  76.2 5.1 %collective-permute-start.14 = (f32[96,256]{1,0:T(8,128)S(1)}, f32[96,256]{1,0:T(8,128)S(1)}, u32[]{:S(2)}, u32[]{:S(2)}) collective-permute-start(f32[96,256]{1,0:T(8,128)S(1)} %bitcast.80), channel_id=1, source_target_pairs={{0,128},{1,129},{2,130},{3,131},{4,132},{5,133},{6,134},{7,135},{8... | collective-permute-start | bytes 294920 | tf_op jit(solution)/shard_map/ppermute | solution.py:115
  78.9 4.7 %collective-permute-start.15 = (f32[96,256]{1,0:T(8,128)S(1)}, f32[96,256]{1,0:T(8,128)S(1)}, u32[]{:S(2)}, u32[]{:S(2)}) collective-permute-start(f32[96,256]{1,0:T(8,128)S(1)} %bitcast.81), channel_id=1, source_target_pairs={{0,192},{1,193},{2,194},{3,195},{4,196},{5,197},{6,198},{7,199},{8... | collective-permute-start | bytes 294920 | tf_op jit(solution)/shard_map/ppermute | solution.py:115
  84.3 31.6 %collective-permute-start.16 = (f32[384,256]{1,0:T(8,128)}, f32[384,256]{1,0:T(8,128)}, u32[]{:S(2)}, u32[]{:S(2)}) collective-permute-start(f32[384,256]{1,0:T(8,128)} %pad_maximum_fusion.1), channel_id=1, source_target_pairs={{0,8},{1,9},{2,10},{3,11},{4,12},{5,13},{6,14},{7,15},{8,0},{9,1},... | collective-permute-start | bytes 1179656 | tf_op jit(solution)/shard_map/ppermute | solution.py:115
  91.5 18.8 %copy-start.1 = (bf16[152,8,128]{2,1,0:T(8,128)(2,1)}, bf16[152,8,128]{2,1,0:T(8,128)(2,1)S(1)}, u32[]{:S(2)}) copy-start(bf16[152,8,128]{2,1,0:T(8,128)(2,1)S(1)} %get-tuple-element.17.refs_1_) | copy-start | bytes 933892
  91.5 9.0 %collective-permute-start.3 = (bf16[152,8,128]{2,1,0:T(8,128)(2,1)S(1)}, bf16[152,8,128]{2,1,0:T(8,128)(2,1)S(1)}, u32[]{:S(2)}, u32[]{:S(2)}) collective-permute-start(bf16[152,8,128]{2,1,0:T(8,128)(2,1)S(1)} %get-tuple-element.18), channel_id=1, source_target_pairs={{0,64},{1,65},{2,66},{3,67},{4,68},{5,69},{6,70},{7,71},{8,72},{9,... | collective-permute-start | bytes 933896 | tf_op jit(solution)/shard_map/ppermute | solution.py:115
  91.6 16.6 %collective-permute-start.4 = (bf16[152,8,128]{2,1,0:T(8,128)(2,1)S(1)}, bf16[152,8,128]{2,1,0:T(8,128)(2,1)S(1)}, u32[]{:S(2)}, u32[]{:S(2)}) collective-permute-start(bf16[152,8,128]{2,1,0:T(8,128)(2,1)S(1)} %get-tuple-element.19), channel_id=1, source_target_pairs={{0,128},{1,129},{2,130},{3,131},{4,132},{5,133},{6,134},{7,135},{8... | collective-permute-start | bytes 933896 | tf_op jit(solution)/shard_map/ppermute | solution.py:115
  94.0 16.2 %collective-permute-start.5 = (bf16[152,8,128]{2,1,0:T(8,128)(2,1)S(1)}, bf16[152,8,128]{2,1,0:T(8,128)(2,1)S(1)}, u32[]{:S(2)}, u32[]{:S(2)}) collective-permute-start(bf16[152,8,128]{2,1,0:T(8,128)(2,1)S(1)} %get-tuple-element.20), channel_id=1, source_target_pairs={{0,192},{1,193},{2,194},{3,195},{4,196},{5,197},{6,198},{7,199},{8... | collective-permute-start | bytes 933896 | tf_op jit(solution)/shard_map/ppermute | solution.py:115
  100.5 9.8 %copy-start.7 = (bf16[152,8,128]{2,1,0:T(8,128)(2,1)}, bf16[152,8,128]{2,1,0:T(8,128)(2,1)S(1)}, u32[]{:S(2)}) copy-start(bf16[152,8,128]{2,1,0:T(8,128)(2,1)S(1)} %collective-permute-done.3.refs_2_) | copy-start | bytes 933892
  108.2 2.1 %copy-start.8 = (bf16[152,8,128]{2,1,0:T(8,128)(2,1)}, bf16[152,8,128]{2,1,0:T(8,128)(2,1)S(1)}, u32[]{:S(2)}) copy-start(bf16[152,8,128]{2,1,0:T(8,128)(2,1)S(1)} %collective-permute-done.4.refs_3_) | copy-start | bytes 933892
  110.2 0.7 copy-start.9
  112.3 3.7 %copy-start.3 = (f32[768,256]{1,0:T(8,128)S(1)}, f32[768,256]{1,0:T(8,128)}, u32[]{:S(2)}) copy-start(f32[768,256]{1,0:T(8,128)} %constant_dynamic-update-slice_fusion.1) | copy-start | bytes 2359300
  112.3 4.7 %copy-start.4 = (f32[768,149]{1,0:T(8,128)S(1)}, f32[768,149]{1,0:T(8,128)}, u32[]{:S(2)}) copy-start(f32[768,149]{1,0:T(8,128)} %fusion) | copy-start | bytes 1373188
  112.3 4.7 %copy-start.25 = (s32[149]{0:T(256)S(1)}, s32[149]{0:T(256)}, u32[]{:S(2)}) copy-start(s32[149]{0:T(256)} %param.18) | copy-start | bytes 1792
  112.3 4.7 %copy-start.26 = (s32[225]{0:T(256)S(1)}, s32[225]{0:T(256)}, u32[]{:S(2)}) copy-start(s32[225]{0:T(256)} %constant.165.clone) | copy-start | bytes 2704
  112.3 9.6 %collective-permute-start.6 = (bf16[304,8,128]{2,1,0:T(8,128)(2,1)S(1)}, bf16[304,8,128]{2,1,0:T(8,128)(2,1)}, u32[]{:S(2)}, u32[]{:S(2)}) collective-permute-start(bf16[304,8,128]{2,1,0:T(8,128)(2,1)S(1)} %get-tuple-element.22), channel_id=1, source_target_pairs={{0,8},{1,9},{2,10},{3,11},{4,12},{5,13},{6,14},{7,15},{8,0},{9,1},... | collective-permute-start | bytes 1867784 | tf_op jit(solution)/shard_map/ppermute | solution.py:115
  115.9 2.5 %copy-start.6 = (f32[450,225]{1,0:T(8,128)S(1)}, f32[450,225]{1,0:T(8,128)}, u32[]{:S(2)}) copy-start(f32[450,225]{1,0:T(8,128)} %constant.166.clone) | copy-start | bytes 1215004
  119.8 3.8 %copy-start.23 = (f32[225]{0:T(256)S(1)}, f32[225]{0:T(256)}, u32[]{:S(2)}) copy-start(f32[225]{0:T(256)} %constant.167.clone) | copy-start | bytes 2704
  123.6 0.9 copy-start.13
  126.0 0.9 copy-start.11

commit v9 on v5

--- a/solution.py
+++ b/solution.py
@@ -73,6 +73,7 @@
         cost_estimate=pl.CostEstimate(
             flops=int(3e7), bytes_accessed=300000, transcendentals=0
         ),
+        compiler_params=pltpu.CompilerParams(vmem_limit_bytes=2 << 20),
         name="sweep",
     )(padded)
     return inverse[:solved, :solved]
@@ -101,7 +102,7 @@
                 out[k, l, 1, sk, cl] -= gk
             if gl:
                 out[k, l, 1, ck, sl] -= gl
-    return out.transpose(2, 0, 1, 3, 4).reshape(2, FREQS * FREQS, FREQS * FREQS)
+    return out.reshape(FREQS * FREQS * 2, FREQS * FREQS)
 
 
 DEVS = 8
@@ -210,8 +211,8 @@
     kmax = np.maximum(step[:, None], step[None, :]).reshape(-1)
     both = (weight[:, None] * weight[None, :]).reshape(-1).astype(np.float32)
     masked = jnp.where(jnp.asarray(kmax)[:, None] < bands[None, :], coef, 0.0)
-    signed = [jnp.dot(jnp.asarray(part), masked, precision=HIGH) for part in mirror()]
-    spectrum = jnp.stack(signed).reshape(2, FREQS, FREQS, solved).transpose(0, 3, 1, 2)
+    signed = jnp.dot(jnp.asarray(mirror()), masked, precision=HIGH)
+    spectrum = signed.reshape(FREQS, FREQS, 2, solved).transpose(2, 3, 0, 1)
     weighed = masked * jnp.asarray(both)[:, None]
     row_here = basis(grp * row_dev + jnp.arange(row_dev, dtype=jnp.int32), rows_all)
 

time: 103 us -> 95.7 us (0.929)
  waiting for transfers between devices: 21.4 us -> 19.1 us
  matrix products: 14.3 us -> 12.3 us
  other arithmetic: 4.68 us -> 3.09 us
  Pallas kernels: 16.4 us -> 14.9 us
    all_to_all x2, waiting for transfers between devices: 7.52 us -> 3.69 us  [on_device(): blocks.append(lax.all_to_all(packed, 'grp', 0, 0, tiled=True))]
    reshape x0 -> x1, local copies, waits for them, and re-layouts: none -> 2.06 us  [on_device(): spectrum = signed.reshape(FREQS, FREQS, 2, solved).transpose(2, 3, 0, 1)]
    dot_general x1, matrix products: 2.9 us -> 1.2 us  [on_device(): half = jnp.einsum('ihw,ha->iaw', wide, rows, precision=HIGH)]
    unnamed x39 -> x38, local copies, waits for them, and re-layouts: 4.61 us -> 2.95 us
    ppermute x10, waiting for transfers between devices: 13.9 us -> 15.5 us  [permuted(): return lax.ppermute(value, ('grp', 'dev'), pairs)]
    dot_general x1, matrix products: 2.16 us -> 0.57 us  [on_device(): lax.dot_general(inverse, design.astype(jnp.float32), (((1,), (1,)), ((),...]
    pallas_call x1, Pallas kernels: 11.4 us -> 9.87 us  [inverse_of(): pl.pallas_call(sweep_kernel, out_shape=jax.ShapeDtypeStruct((size, width)...]
    dot_general x2, matrix products: 0.8 us -> 2.09 us  [on_device(): series = jnp.dot(pinv, flat, preferred_element_type=jnp.float32)]
  transfers between devices with their start and end apart: 12 -> 12, of which waited for: 5 -> 6; matrix products, arithmetic and copies ran while one was open for 15% -> 15% of each run, Pallas kernels for 16% -> 13%
where the time goes in v9:
time: 95.7 us; the launch traced here: 95.1 us
  starting transfers between devices  39.1 us (41%)
  waiting for transfers between devices  19.1 us (20%)
  Pallas kernels  14.9 us (16%)
  matrix products  12.3 us (13%)
  local copies, waits for them, and re-layouts  5.32 us (6%)
  other arithmetic  3.09 us (3%)
  between operations  1.26 us (1%)
    ppermute x10, starting transfers between devices, permuted(): return lax.ppermute(value, ('grp', 'dev'), pairs)  21.6 us
    all_to_all x2, starting transfers between devices, on_device(): blocks.append(lax.all_to_all(packed, 'grp', 0, 0, tiled=True))  17.5 us
    ppermute x10, waiting for transfers between devices, permuted(): return lax.ppermute(value, ('grp', 'dev'), pairs)  15.5 us
    pallas_call x1, Pallas kernels, inverse_of(): pl.pallas_call(sweep_kernel, out_shape=jax.ShapeDtypeStruct((size, width)...  9.87 us
    pallas_call x2, Pallas kernels, pack(): pl.pallas_call(functools.partial(pack_kernel, part), out_shape=jax.ShapeD...  5.02 us
    all_to_all x2, waiting for transfers between devices, on_device(): blocks.append(lax.all_to_all(packed, 'grp', 0, 0, tiled=True))  3.69 us
    unnamed x38, local copies, waits for them, and re-layouts  2.95 us
    dot_general x2, matrix products, on_device(): jnp.dot(design, series.astype(jnp.bfloat16), preferred_element_type=jnp.f...  2.48 us
  transfers between devices with their start and end apart: 12, of which 6 were waited for; matrix products, arithmetic and copies ran while one was open for 15% of the time, Pallas kernels for 13%

profile of v9, /device:TPU:1, one launch (start us, length us, event | category | flops | bytes accessed | tf_op | source)
XLA Modules:
  0.0 95.1 jit_solution(368820380381337998)
XLA Ops:
  0.6 2.5 %shard_map.131 = bf16[32,19,8,128]{3,2,1,0:T(8,128)(2,1)} custom-call(bf16[19,32,8,256]{3,2,1,0:T(8,128)(2,1)} %bitcast.57), custom_call_target="tpu_custom_call" | custom-call | tf_op jit(solution)/shard_map/pallas_call | solution.py:144
  3.2 10.4 %all-to-all-start.1 = ((bf16[32,19,8,128]{3,2,1,0:T(8,128)(2,1)}), bf16[32,19,8,128]{3,2,1,0:T(8,128)(2,1)}, u32[]{:S(2)}, u32[]{:S(2)}) async-start(bf16[32,19,8,128]{3,2,1,0:T(8,128)(2,1)} %shard_map.131), calls=%async_computation.1 | async-start | bytes 2490368 | tf_op jit(solution)/shard_map/all_to_all | solution.py:169
  13.6 1.2 %convolution_bitcast_fusion = f32[19,15,256]{2,1,0:T(8,128)S(1)} fusion(bf16[19,256,256]{2,1,0:T(8,128)(2,1)S(1)} %copy-done, s32[15]{0:T(128)S(1)} %add_select_fusion.4, pred[15]{0:T(512)(128)(4,1)S(1)} %iota_compare_fusion.3), kind=kOutput, calls=%fused_computation.12 | convolution fusion | flops 224190720 | bytes 2782283 | tf_op jit(solution)/shard_map/ihw,ha->iaw/dot_general | solution.py:174
  14.8 0.5 fusion.38
  15.4 0.1 reshape.147
  15.5 1.3 %collective-permute-start = (f32[24,256]{1,0:T(8,128)S(1)}, f32[24,256]{1,0:T(8,128)S(1)}, u32[]{:S(2)}, u32[]{:S(2)}) collective-permute-start(f32[24,256]{1,0:T(8,128)S(1)} %pad.9), channel_id=1, source_target_pairs={{0,2},{1,3},{2,0},{3,1},{4,6},{5,7},{6,4},{7,5},{8,10},{9,11},{10,... | collective-permute-start | bytes 73736 | tf_op jit(solution)/shard_map/ppermute | solution.py:117
  16.8 0.1 sine_select_fusion.1
  16.9 0.2 sine_select_fusion
  17.1 1.1 %broadcast_multiply_fusion.1 = (f32[15,15,8,128]{3,2,1,0:T(8,128)}, f32[15,15,8,128]{3,2,1,0:T(8,128)S(1)}) fusion(f32[15,128]{1,0:T(8,128)S(1)} %get-tuple-element.5, f32[15,8]{1,0:T(8,128)S(1)} %sine_select_fusion.1, f32[15,128]{1,0:T(8,128)S(1)} %get-tuple-element.6), kind=kLoop, calls=%fused_computation.23 | loop fusion | flops 460800 | bytes 1859040 | tf_op jit(solution)/shard_map/mul | solution.py:222
  18.2 0.6 fusion.12
  18.9 2.6 %collective-permute-start.1 = (f32[24,256]{1,0:T(8,128)S(1)}, f32[24,256]{1,0:T(8,128)S(1)}, u32[]{:S(2)}, u32[]{:S(2)}) collective-permute-start(f32[24,256]{1,0:T(8,128)S(1)} %pad_add_fusion), channel_id=1, source_target_pairs={{0,4},{1,5},{2,6},{3,7},{4,0},{5,1},{6,2},{7,3},{8,12},{9,13},{10,... | collective-permute-start | bytes 73736 | tf_op jit(solution)/shard_map/ppermute | solution.py:117
  21.5 2.1 %collective-permute-done.1 = f32[24,256]{1,0:T(8,128)S(1)} collective-permute-done((f32[24,256]{1,0:T(8,128)S(1)}, f32[24,256]{1,0:T(8,128)S(1)}, u32[]{:S(2)}, u32[]{:S(2)}) %collective-permute-start.1) | collective-permute-done | bytes 24608 | tf_op jit(solution)/shard_map/ppermute | solution.py:117
  23.6 4.2 %collective-permute-start.3 = (f32[24,256]{1,0:T(8,128)S(1)}, f32[24,256]{1,0:T(8,128)S(1)}, u32[]{:S(2)}, u32[]{:S(2)}) collective-permute-start(f32[24,256]{1,0:T(8,128)S(1)} %add.111), channel_id=1, source_target_pairs={{0,1},{1,0},{2,19},{3,18},{4,37},{5,36},{6,55},{7,54},{8,9},{9,8},... | collective-permute-start | bytes 73736 | tf_op jit(solution)/shard_map/ppermute | solution.py:117
  27.8 0.7 collective-permute-start.2
  28.4 0.1 select_add_fusion.normal_ref
  28.5 9.9 %sweep.1 = f32[152,256]{1,0:T(8,128)S(1)} custom-call(f32[152,256]{1,0:T(8,128)S(1)} %select_add_fusion.normal_ref), custom_call_target="tpu_custom_call" | custom-call | flops 30000000 | bytes 300000 | tf_op jit(solution)/shard_map/sweep/pallas_call | solution.py:68
  38.4 1.1 %collective-permute-done.3 = f32[24,256]{1,0:T(8,128)S(1)} collective-permute-done((f32[24,256]{1,0:T(8,128)S(1)}, f32[24,256]{1,0:T(8,128)S(1)}, u32[]{:S(2)}, u32[]{:S(2)}) %collective-permute-start.3) | collective-permute-done | bytes 24608 | tf_op jit(solution)/shard_map/ppermute | solution.py:117
  39.5 8.5 %collective-permute-start.4 = (f32[24,256]{1,0:T(8,128)S(1)}, f32[24,256]{1,0:T(8,128)S(1)}, u32[]{:S(2)}, u32[]{:S(2)}) collective-permute-start(f32[24,256]{1,0:T(8,128)S(1)} %add.112), channel_id=1, source_target_pairs={{0,2},{1,3},{2,0},{3,1},{4,6},{5,7},{6,4},{7,5},{8,10},{9,11},{10,... | collective-permute-start | bytes 73736 | tf_op jit(solution)/shard_map/ppermute | solution.py:117
  48.0 0.6 convolution_convert_fusion
  48.6 2.5 %shard_map.130 = bf16[32,19,8,128]{3,2,1,0:T(8,128)(2,1)} custom-call(bf16[19,32,8,256]{3,2,1,0:T(8,128)(2,1)} %bitcast.58), custom_call_target="tpu_custom_call" | custom-call | tf_op jit(solution)/shard_map/pallas_call | solution.py:144
  51.3 7.1 %all-to-all-start = ((bf16[32,19,8,128]{3,2,1,0:T(8,128)(2,1)}), bf16[32,19,8,128]{3,2,1,0:T(8,128)(2,1)S(1)}, u32[]{:S(2)}, u32[]{:S(2)}) async-start(bf16[32,19,8,128]{3,2,1,0:T(8,128)(2,1)} %shard_map.130), calls=%async_computation | async-start | bytes 2490368 | tf_op jit(solution)/shard_map/all_to_all | solution.py:169
  58.4 0.1 collective-permute-start.5
  58.6 0.1 eq.76
  58.7 4.5 %collective-permute-done.5 = f32[2,24,256]{2,1,0:T(8,128)S(1)} collective-permute-done((f32[2,24,256]{2,1,0:T(8,128)S(1)}, f32[2,24,256]{2,1,0:T(8,128)S(1)}, u32[]{:S(2)}, u32[]{:S(2)}) %collective-permute-start.5) | collective-permute-done | bytes 49184 | tf_op jit(solution)/shard_map/ppermute | solution.py:117
  63.3 2.7 %collective-permute-start.8 = (f32[96,256]{1,0:T(8,128)S(1)}, f32[96,256]{1,0:T(8,128)S(1)}, u32[]{:S(2)}, u32[]{:S(2)}) collective-permute-start(f32[96,256]{1,0:T(8,128)S(1)} %bitcast.71), channel_id=1, source_target_pairs={{0,192},{1,193},{2,194},{3,195},{4,196},{5,197},{6,198},{7,199},{8... | collective-permute-start | bytes 294920 | tf_op jit(solution)/shard_map/ppermute | solution.py:117
  66.0 0.2 collective-permute-start.7
  66.2 0.4 collective-permute-start.6
  66.7 0.5 fusion
  67.3 0.2 copy.21
  67.5 1.0 %copy-done.1 = f32[15,15,8,128]{3,2,1,0:T(8,128)S(1)} copy-done((f32[15,15,8,128]{3,2,1,0:T(8,128)S(1)}, f32[15,15,8,128]{3,2,1,0:T(8,128)}, u32[]{:S(2)}) %copy-start.1) | copy-done | bytes 921624
  68.5 0.2 copy.18
  68.7 6.4 %collective-permute-done.8 = f32[96,256]{1,0:T(8,128)S(1)} collective-permute-done((f32[96,256]{1,0:T(8,128)S(1)}, f32[96,256]{1,0:T(8,128)S(1)}, u32[]{:S(2)}, u32[]{:S(2)}) %collective-permute-start.8) | collective-permute-done | bytes 98336 | tf_op jit(solution)/shard_map/ppermute | solution.py:117
  75.2 0.9 collective-permute-start.9
  76.1 1.3 %collective-permute-done.9 = f32[384,256]{1,0:T(8,128)S(1)} collective-permute-done((f32[384,256]{1,0:T(8,128)S(1)}, f32[384,256]{1,0:T(8,128)S(1)}, u32[]{:S(2)}, u32[]{:S(2)}) %collective-permute-start.9) | collective-permute-done | bytes 393248 | tf_op jit(solution)/shard_map/ppermute | solution.py:117
  77.4 1.4 %fusion.7 = f32[225,149]{0,1:T(8,128)S(1)} fusion(f32[768,149]{1,0:T(8,128)S(1)} %fusion, f32[768,256]{1,0:T(8,128)S(1)} %constant_dynamic-update-slice_fusion, s32[225]{0:T(256)S(1)} %copy-done.13, s32[149]{0:T(256)S(1)} %copy-done.12), kind=kOutput, calls=%fused_computation.15 | convolution fusion | flops 309066976 | bytes 1379756 | tf_op jit(solution)/shard_map/dot_general | solution.py:207
  78.9 1.3 %fusion.67 = f32[450,149]{1,0:T(8,128)} fusion(f32[450,225]{1,0:T(8,128)S(1)} %copy-done.4, f32[225,149]{0,1:T(8,128)S(1)} %fusion.7), kind=kOutput, calls=%fused_computation.116 | convolution fusion | flops 181035008 | bytes 807300 | tf_op jit(solution)/shard_map/dot_general | solution.py:214
  80.2 2.1 %reshape.152 = f32[15,15,2,149]{3,2,1,0:T(2,128)} reshape(f32[450,149]{1,0:T(8,128)} %fusion.67) | data formatting | bytes 536400 | tf_op jit(solution)/shard_map/reshape | solution.py:215
  82.3 1.7 %fusion.1 = f32[149,1024]{1,0:T(8,128)S(1)} fusion(bf16[149,608]{1,0:T(8,128)(2,1)S(1)} %convolution_convert_fusion, bf16[76,8,8,128]{3,2,1,0:T(8,128)(2,1)} %bitcast.23), kind=kOutput, calls=%fused_computation.6 | convolution fusion | flops 185532416 | bytes 2036672 | tf_op jit(solution)/shard_map/dot_general | solution.py:227
  84.0 0.8 copy-done.2
  84.8 1.9 %multiply_reduce_fusion = f32[1024]{0:T(1024)S(1)} fusion(bf16[76,8,8,128]{3,2,1,0:T(8,128)(2,1)} %bitcast.23, f32[149,1024]{1,0:T(8,128)S(1)} %fusion.1, s32[149]{0:T(256)S(1)} %iota_add_fusion.1, s32[608]{0:T(1024)S(1)} %get-tuple-element.4, s32[608]{0:T(1024)S(1)} %get-tuple-element.3), kind=kOutput, calls=%fused_computation | convolution fusion | flops 188717888 | bytes 1865044 | tf_op jit(solution)/shard_map/dot_general | solution.py:230
  86.7 3.7 %all-to-all-done = bf16[32,19,8,128]{3,2,1,0:T(8,128)(2,1)S(1)} async-done(((bf16[32,19,8,128]{3,2,1,0:T(8,128)(2,1)}), bf16[32,19,8,128]{3,2,1,0:T(8,128)(2,1)S(1)}, u32[]{:S(2)}, u32[]{:S(2)}) %all-to-all-start) | async-done | bytes 1245216 | tf_op jit(solution)/shard_map/all_to_all | solution.py:169
  90.4 0.4 fusion.3
  90.8 0.6 multiply_reduce_fusion.1
  91.4 0.5 copy-done.3
  91.9 0.7 fusion.6
  92.7 0.7 fusion.5
  93.6 0.6 pad_maximum_fusion.4
  94.2 0.9 pad_maximum_fusion
  (59 shorter events, 0.6 us)
Async XLA Ops:
  3.1 10.4 %copy-start = (bf16[19,256,256]{2,1,0:T(8,128)(2,1)S(1)}, bf16[19,256,256]{2,1,0:T(8,128)(2,1)}, u32[]{:S(2)}) copy-start(bf16[19,256,256]{2,1,0:T(8,128)(2,1)} %param.11) | copy-start | bytes 7471108
  3.2 48.1 %all-to-all-start.1 = ((bf16[32,19,8,128]{3,2,1,0:T(8,128)(2,1)}), bf16[32,19,8,128]{3,2,1,0:T(8,128)(2,1)}, u32[]{:S(2)}, u32[]{:S(2)}) async-start(bf16[32,19,8,128]{3,2,1,0:T(8,128)(2,1)} %shard_map.131), calls=%async_computation.1 | async-start | bytes 2490368 | tf_op jit(solution)/shard_map/all_to_all | solution.py:169
  13.6 3.2 %copy-start.9 = (s32[608,2]{0,1:T(2,128)S(1)}, s32[608,2]{0,1:T(2,128)}, u32[]{:S(2)}) copy-start(s32[608,2]{0,1:T(2,128)} %param.12) | copy-start | bytes 14596
  15.5 3.4 %collective-permute-start = (f32[24,256]{1,0:T(8,128)S(1)}, f32[24,256]{1,0:T(8,128)S(1)}, u32[]{:S(2)}, u32[]{:S(2)}) collective-permute-start(f32[24,256]{1,0:T(8,128)S(1)} %pad.9), channel_id=1, source_target_pairs={{0,2},{1,3},{2,0},{3,1},{4,6},{5,7},{6,4},{7,5},{8,10},{9,11},{10,... | collective-permute-start | bytes 73736 | tf_op jit(solution)/shard_map/ppermute | solution.py:117
  18.9 4.7 %collective-permute-start.1 = (f32[24,256]{1,0:T(8,128)S(1)}, f32[24,256]{1,0:T(8,128)S(1)}, u32[]{:S(2)}, u32[]{:S(2)}) collective-permute-start(f32[24,256]{1,0:T(8,128)S(1)} %pad_add_fusion), channel_id=1, source_target_pairs={{0,4},{1,5},{2,6},{3,7},{4,0},{5,1},{6,2},{7,3},{8,12},{9,13},{10,... | collective-permute-start | bytes 73736 | tf_op jit(solution)/shard_map/ppermute | solution.py:117
  23.6 16.0 %collective-permute-start.3 = (f32[24,256]{1,0:T(8,128)S(1)}, f32[24,256]{1,0:T(8,128)S(1)}, u32[]{:S(2)}, u32[]{:S(2)}) collective-permute-start(f32[24,256]{1,0:T(8,128)S(1)} %add.111), channel_id=1, source_target_pairs={{0,1},{1,0},{2,19},{3,18},{4,37},{5,36},{6,55},{7,54},{8,9},{9,8},... | collective-permute-start | bytes 73736 | tf_op jit(solution)/shard_map/ppermute | solution.py:117
  27.8 11.7 %collective-permute-start.2 = (f32[24,256]{1,0:T(8,128)S(1)}, f32[24,256]{1,0:T(8,128)S(1)}, u32[]{:S(2)}, u32[]{:S(2)}) collective-permute-start(f32[24,256]{1,0:T(8,128)S(1)} %add.111), channel_id=1, source_target_pairs={{0,0},{1,1},{2,18},{3,19},{4,36},{5,37},{6,54},{7,55},{8,8},{9,9},... | collective-permute-start | bytes 73736 | tf_op jit(solution)/shard_map/ppermute | solution.py:117
  39.5 18.9 %collective-permute-start.4 = (f32[24,256]{1,0:T(8,128)S(1)}, f32[24,256]{1,0:T(8,128)S(1)}, u32[]{:S(2)}, u32[]{:S(2)}) collective-permute-start(f32[24,256]{1,0:T(8,128)S(1)} %add.112), channel_id=1, source_target_pairs={{0,2},{1,3},{2,0},{3,1},{4,6},{5,7},{6,4},{7,5},{8,10},{9,11},{10,... | collective-permute-start | bytes 73736 | tf_op jit(solution)/shard_map/ppermute | solution.py:117
  51.2 7.3 %copy-start.5 = (s32[2,4,4,24]{3,2,1,0:T(4,128)S(1)}, s32[2,4,4,24]{3,2,1,0:T(4,128)}, u32[]{:S(2)}) copy-start(s32[2,4,4,24]{3,2,1,0:T(4,128)} %constant.145.clone) | copy-start | bytes 9220
  51.2 7.3 %copy-start.6 = (s32[2,4,4,24]{3,2,1,0:T(4,128)S(1)}, s32[2,4,4,24]{3,2,1,0:T(4,128)}, u32[]{:S(2)}) copy-start(s32[2,4,4,24]{3,2,1,0:T(4,128)} %constant.144.clone) | copy-start | bytes 9220
  51.2 7.3 %copy-start.7 = (s32[2,4,4,24]{3,2,1,0:T(4,128)S(1)}, s32[2,4,4,24]{3,2,1,0:T(4,128)}, u32[]{:S(2)}) copy-start(s32[2,4,4,24]{3,2,1,0:T(4,128)} %constant.143.clone) | copy-start | bytes 9220
  51.2 7.3 %copy-start.8 = (s32[2,4,4,24]{3,2,1,0:T(4,128)S(1)}, s32[2,4,4,24]{3,2,1,0:T(4,128)}, u32[]{:S(2)}) copy-start(s32[2,4,4,24]{3,2,1,0:T(4,128)} %constant.142.clone) | copy-start | bytes 9220
  51.3 7.3 %copy-start.11 = (pred[2,4,4,24]{3,2,1,0:T(4,128)(4,1)S(1)}, pred[2,4,4,24]{3,2,1,0:T(4,128)(4,1)}, u32[]{:S(2)}) copy-start(pred[2,4,4,24]{3,2,1,0:T(4,128)(4,1)} %constant.146.clone) | copy-start | bytes 2308
  51.3 39.1 %all-to-all-start = ((bf16[32,19,8,128]{3,2,1,0:T(8,128)(2,1)}), bf16[32,19,8,128]{3,2,1,0:T(8,128)(2,1)S(1)}, u32[]{:S(2)}, u32[]{:S(2)}) async-start(bf16[32,19,8,128]{3,2,1,0:T(8,128)(2,1)} %shard_map.130), calls=%async_computation | async-start | bytes 2490368 | tf_op jit(solution)/shard_map/all_to_all | solution.py:169
  58.4 4.8 %collective-permute-start.5 = (f32[2,24,256]{2,1,0:T(8,128)S(1)}, f32[2,24,256]{2,1,0:T(8,128)S(1)}, u32[]{:S(2)}, u32[]{:S(2)}) collective-permute-start(f32[2,24,256]{2,1,0:T(8,128)S(1)} %pad_maximum_fusion.3), channel_id=1, source_target_pairs={{0,4},{1,5},{2,6},{3,7},{4,0},{5,1},{6,2},{7,3},{8,12},{9,13},{10,... | collective-permute-start | bytes 147464 | tf_op jit(solution)/shard_map/ppermute | solution.py:117
  63.3 11.9 %collective-permute-start.8 = (f32[96,256]{1,0:T(8,128)S(1)}, f32[96,256]{1,0:T(8,128)S(1)}, u32[]{:S(2)}, u32[]{:S(2)}) collective-permute-start(f32[96,256]{1,0:T(8,128)S(1)} %bitcast.71), channel_id=1, source_target_pairs={{0,192},{1,193},{2,194},{3,195},{4,196},{5,197},{6,198},{7,199},{8... | collective-permute-start | bytes 294920 | tf_op jit(solution)/shard_map/ppermute | solution.py:117
  66.0 9.2 %collective-permute-start.7 = (f32[96,256]{1,0:T(8,128)S(1)}, f32[96,256]{1,0:T(8,128)S(1)}, u32[]{:S(2)}, u32[]{:S(2)}) collective-permute-start(f32[96,256]{1,0:T(8,128)S(1)} %bitcast.72), channel_id=1, source_target_pairs={{0,128},{1,129},{2,130},{3,131},{4,132},{5,133},{6,134},{7,135},{8... | collective-permute-start | bytes 294920 | tf_op jit(solution)/shard_map/ppermute | solution.py:117
  66.2 8.9 %collective-permute-start.6 = (f32[96,256]{1,0:T(8,128)S(1)}, f32[96,256]{1,0:T(8,128)S(1)}, u32[]{:S(2)}, u32[]{:S(2)}) collective-permute-start(f32[96,256]{1,0:T(8,128)S(1)} %bitcast.73), channel_id=1, source_target_pairs={{0,64},{1,65},{2,66},{3,67},{4,68},{5,69},{6,70},{7,71},{8,72},{9,... | collective-permute-start | bytes 294920 | tf_op jit(solution)/shard_map/ppermute | solution.py:117
  67.3 1.2 %copy-start.1 = (f32[15,15,8,128]{3,2,1,0:T(8,128)S(1)}, f32[15,15,8,128]{3,2,1,0:T(8,128)}, u32[]{:S(2)}) copy-start(f32[15,15,8,128]{3,2,1,0:T(8,128)} %get-tuple-element.7) | copy-start | bytes 2764804
  68.7 8.7 %copy-start.12 = (s32[149]{0:T(256)S(1)}, s32[149]{0:T(256)}, u32[]{:S(2)}) copy-start(s32[149]{0:T(256)} %param.13) | copy-start | bytes 1792
  68.7 8.7 %copy-start.13 = (s32[225]{0:T(256)S(1)}, s32[225]{0:T(256)}, u32[]{:S(2)}) copy-start(s32[225]{0:T(256)} %constant.147.clone) | copy-start | bytes 2704
  75.2 2.2 %collective-permute-start.9 = (f32[384,256]{1,0:T(8,128)S(1)}, f32[384,256]{1,0:T(8,128)S(1)}, u32[]{:S(2)}, u32[]{:S(2)}) collective-permute-start(f32[384,256]{1,0:T(8,128)S(1)} %pad_maximum_fusion.1), channel_id=1, source_target_pairs={{0,8},{1,9},{2,10},{3,11},{4,12},{5,13},{6,14},{7,15},{8,0},{9,1},... | collective-permute-start | bytes 1179656 | tf_op jit(solution)/shard_map/ppermute | solution.py:117
  76.1 2.8 %copy-start.4 = (f32[450,225]{1,0:T(8,128)S(1)}, f32[450,225]{1,0:T(8,128)}, u32[]{:S(2)}) copy-start(f32[450,225]{1,0:T(8,128)} %constant.148.clone) | copy-start | bytes 1215004
  84.0 0.8 copy-start.2
  90.8 1.1 %copy-start.3 = (f32[149,1024]{1,0:T(8,128)S(1)}, f32[149,1024]{1,0:T(8,128)}, u32[]{:S(2)}) copy-start(f32[149,1024]{1,0:T(8,128)} %copy-done.2) | copy-start | bytes 1830916
  90.8 1.1 %copy-start.10 = (f32[225]{0:T(256)S(1)}, f32[225]{0:T(256)}, u32[]{:S(2)}) copy-start(f32[225]{0:T(256)} %constant.149.clone) | copy-start | bytes 2704

commit v10 on v9

--- a/solution.py
+++ b/solution.py
@@ -125,28 +125,40 @@
     return permuted(value, lambda g, d: (g, d ^ (k << 1)))
 
 
-def pack_kernel(part, strips_ref, out_ref, sems):
-    held, span = out_ref.shape[1], out_ref.shape[3]
-    copies = [
+def pack_kernel(part, strips_ref, out_ref, buffer, in_sems, out_sems):
+    groups, _, _, span = out_ref.shape
+    reads = [
         pltpu.make_async_copy(
-            strips_ref.at[i, :, :, pl.ds(part * span, span)], out_ref.at[:, i], sems.at[i]
+            strips_ref.at[:, j, :, pl.ds(part * span, span)], buffer.at[j], in_sems.at[j]
         )
-        for i in range(held)
+        for j in range(groups)
     ]
-    for copy in copies:
-        copy.start()
-    for copy in copies:
-        copy.wait()
+    writes = [
+        pltpu.make_async_copy(buffer.at[j], out_ref.at[j], out_sems.at[j])
+        for j in range(groups)
+    ]
+    for read in reads:
+        read.start()
+    for read, write in zip(reads, writes):
+        read.wait()
+        write.start()
+    for write in writes:
+        write.wait()
 
 
 def pack(strips, part, span):
     held, groups, row_dev, _ = strips.shape
+    shape = (groups, held, row_dev, span)
     return pl.pallas_call(
         functools.partial(pack_kernel, part),
-        out_shape=jax.ShapeDtypeStruct((groups, held, row_dev, span), strips.dtype),
+        out_shape=jax.ShapeDtypeStruct(shape, strips.dtype),
         in_specs=[pl.BlockSpec(memory_space=pl.ANY)],
-        out_specs=pl.BlockSpec(memory_space=pltpu.VMEM),
-        scratch_shapes=[pltpu.SemaphoreType.DMA((held,))],
+        out_specs=pl.BlockSpec(memory_space=pl.ANY),
+        scratch_shapes=[
+            pltpu.VMEM(shape, strips.dtype),
+            pltpu.SemaphoreType.DMA((groups,)),
+            pltpu.SemaphoreType.DMA((groups,)),
+        ],
     )(strips)
 
 
@@ -224,6 +236,8 @@
             weighed, waves.reshape(modes, -1), (((0,), (0,)), ((), ())), precision=HIGH
         )
         flat = block.reshape(ifgs, row_dev * span)
+        if part:
+            ramp = lax.optimization_barrier(ramp)
         series = jnp.dot(pinv, flat, preferred_element_type=jnp.float32)
         image = (series - ramp).astype(jnp.bfloat16)
         images.append(image.reshape(solved, row_dev, span))

time: 95.7 us -> 101 us (1.055)
  matrix products: 12.3 us -> 16.7 us
  local copies, waits for them, and re-layouts: 5.32 us -> 3.47 us
  other arithmetic: 3.09 us -> 4.73 us
    unnamed x38 -> x36, local copies, waits for them, and re-layouts: 2.95 us -> 1.11 us
    dot_general x1, matrix products: 1.2 us -> 2.9 us  [on_device(): half = jnp.einsum('ihw,ha->iaw', wide, rows, precision=HIGH)]
    dot_general x2, matrix products: 2.09 us -> 3.65 us  [on_device(): series = jnp.dot(pinv, flat, preferred_element_type=jnp.float32)]
    dot_general x2, matrix products: 2.48 us -> 1.19 us  [on_device(): jnp.dot(design, series.astype(jnp.bfloat16), preferred_element_type=jnp.f...]
    ppermute x10, waiting for transfers between devices: 15.5 us -> 16.6 us  [permuted(): return lax.ppermute(value, ('grp', 'dev'), pairs)]
  transfers between devices with their start and end apart: 12 -> 12, of which waited for: 6 -> 6; matrix products, arithmetic and copies ran while one was open for 15% -> 17% of each run, Pallas kernels for 13% -> 15%
where the time goes in v10:
time: 101 us; the launch traced here: 99.9 us
  starting transfers between devices  39 us (39%)
  waiting for transfers between devices  20 us (20%)
  matrix products  16.7 us (17%)
  Pallas kernels  14.9 us (15%)
  other arithmetic  4.73 us (5%)
  local copies, waits for them, and re-layouts  3.47 us (3%)
  between operations  1.19 us (1%)
    ppermute x10, starting transfers between devices, permuted(): return lax.ppermute(value, ('grp', 'dev'), pairs)  22.2 us
    all_to_all x2, starting transfers between devices, on_device(): blocks.append(lax.all_to_all(packed, 'grp', 0, 0, tiled=True))  16.8 us
    ppermute x10, waiting for transfers between devices, permuted(): return lax.ppermute(value, ('grp', 'dev'), pairs)  16.6 us
    pallas_call x1, Pallas kernels, inverse_of(): pl.pallas_call(sweep_kernel, out_shape=jax.ShapeDtypeStruct((size, width)...  9.87 us
    pallas_call x2, Pallas kernels, pack(): pl.pallas_call(functools.partial(pack_kernel, part), out_shape=jax.ShapeD...  5.01 us
    dot_general x2, matrix products, on_device(): series = jnp.dot(pinv, flat, preferred_element_type=jnp.float32)  3.65 us
    all_to_all x2, waiting for transfers between devices, on_device(): blocks.append(lax.all_to_all(packed, 'grp', 0, 0, tiled=True))  3.35 us
    dot_general x1, matrix products, on_device(): half = jnp.einsum('ihw,ha->iaw', wide, rows, precision=HIGH)  2.9 us
  transfers between devices with their start and end apart: 12, of which 6 were waited for; matrix products, arithmetic and copies ran while one was open for 17% of the time, Pallas kernels for 15%

profile of v10, /device:TPU:1, one launch (start us, length us, event | category | flops | bytes accessed | tf_op | source)
XLA Modules:
  0.0 99.9 jit_solution(7380713867893301335)
XLA Ops:
  0.7 2.9 %convolution_bitcast_fusion = f32[19,15,256]{2,1,0:T(8,128)S(1)} fusion(bf16[19,256,256]{2,1,0:T(8,128)(2,1)} %param.11, s32[15]{0:T(128)S(1)} %add_select_fusion.4, pred[15]{0:T(512)(128)(4,1)S(1)} %iota_compare_fusion.3), kind=kOutput, calls=%fused_computation.10 | convolution fusion | flops 224190720 | bytes 2782283 | tf_op jit(solution)/shard_map/ihw,ha->iaw/dot_general | solution.py:186
  3.6 0.5 fusion.38
  4.1 0.1 reshape.147
  4.2 2.1 %collective-permute-start = (f32[24,256]{1,0:T(8,128)S(1)}, f32[24,256]{1,0:T(8,128)S(1)}, u32[]{:S(2)}, u32[]{:S(2)}) collective-permute-start(f32[24,256]{1,0:T(8,128)S(1)} %pad.9), channel_id=1, source_target_pairs={{0,2},{1,3},{2,0},{3,1},{4,6},{5,7},{6,4},{7,5},{8,10},{9,11},{10,... | collective-permute-start | bytes 73736 | tf_op jit(solution)/shard_map/ppermute | solution.py:117
  6.4 2.5 %shard_map.131 = bf16[32,19,8,128]{3,2,1,0:T(8,128)(2,1)} custom-call(bf16[19,32,8,256]{3,2,1,0:T(8,128)(2,1)} %bitcast.60), custom_call_target="tpu_custom_call" | custom-call | tf_op jit(solution)/shard_map/pallas_call | solution.py:152
  8.9 9.7 %all-to-all-start.1 = ((bf16[32,19,8,128]{3,2,1,0:T(8,128)(2,1)}), bf16[32,19,8,128]{3,2,1,0:T(8,128)(2,1)S(1)}, u32[]{:S(2)}, u32[]{:S(2)}) async-start(bf16[32,19,8,128]{3,2,1,0:T(8,128)(2,1)} %shard_map.131), calls=%async_computation.1 | async-start | bytes 2490368 | tf_op jit(solution)/shard_map/all_to_all | solution.py:181
  18.6 0.1 sine_select_fusion.1
  18.8 0.2 sine_select_fusion
  18.9 1.1 %broadcast_multiply_fusion.1 = (f32[15,15,8,128]{3,2,1,0:T(8,128)S(1)}, f32[15,15,8,128]{3,2,1,0:T(8,128)}) fusion(f32[15,128]{1,0:T(8,128)S(1)} %get-tuple-element.5, f32[15,8]{1,0:T(8,128)S(1)} %sine_select_fusion.1, f32[15,128]{1,0:T(8,128)S(1)} %get-tuple-element.6), kind=kLoop, calls=%fused_computation.22 | loop fusion | flops 460800 | bytes 1859040 | tf_op jit(solution)/shard_map/mul | solution.py:234
  20.0 0.6 fusion.11
  20.7 2.5 %collective-permute-start.1 = (f32[24,256]{1,0:T(8,128)S(1)}, f32[24,256]{1,0:T(8,128)S(1)}, u32[]{:S(2)}, u32[]{:S(2)}) collective-permute-start(f32[24,256]{1,0:T(8,128)S(1)} %pad_add_fusion), channel_id=1, source_target_pairs={{0,4},{1,5},{2,6},{3,7},{4,0},{5,1},{6,2},{7,3},{8,12},{9,13},{10,... | collective-permute-start | bytes 73736 | tf_op jit(solution)/shard_map/ppermute | solution.py:117
  23.2 2.0 %collective-permute-done.1 = f32[24,256]{1,0:T(8,128)S(1)} collective-permute-done((f32[24,256]{1,0:T(8,128)S(1)}, f32[24,256]{1,0:T(8,128)S(1)}, u32[]{:S(2)}, u32[]{:S(2)}) %collective-permute-start.1) | collective-permute-done | bytes 24608 | tf_op jit(solution)/shard_map/ppermute | solution.py:117
  25.3 0.7 collective-permute-start.2
  25.9 4.3 %collective-permute-start.3 = (f32[24,256]{1,0:T(8,128)S(1)}, f32[24,256]{1,0:T(8,128)S(1)}, u32[]{:S(2)}, u32[]{:S(2)}) collective-permute-start(f32[24,256]{1,0:T(8,128)S(1)} %add.111), channel_id=1, source_target_pairs={{0,1},{1,0},{2,19},{3,18},{4,37},{5,36},{6,55},{7,54},{8,9},{9,8},... | collective-permute-start | bytes 73736 | tf_op jit(solution)/shard_map/ppermute | solution.py:117
  30.2 0.1 select_add_fusion.normal_ref
  30.3 9.9 %sweep.1 = f32[152,256]{1,0:T(8,128)S(1)} custom-call(f32[152,256]{1,0:T(8,128)S(1)} %select_add_fusion.normal_ref), custom_call_target="tpu_custom_call" | custom-call | flops 30000000 | bytes 300000 | tf_op jit(solution)/shard_map/sweep/pallas_call | solution.py:68
  40.2 4.4 %collective-permute-done.3 = f32[24,256]{1,0:T(8,128)S(1)} collective-permute-done((f32[24,256]{1,0:T(8,128)S(1)}, f32[24,256]{1,0:T(8,128)S(1)}, u32[]{:S(2)}, u32[]{:S(2)}) %collective-permute-start.3) | collective-permute-done | bytes 24608 | tf_op jit(solution)/shard_map/ppermute | solution.py:117
  44.6 7.5 %collective-permute-start.4 = (f32[24,256]{1,0:T(8,128)S(1)}, f32[24,256]{1,0:T(8,128)S(1)}, u32[]{:S(2)}, u32[]{:S(2)}) collective-permute-start(f32[24,256]{1,0:T(8,128)S(1)} %add.112), channel_id=1, source_target_pairs={{0,2},{1,3},{2,0},{3,1},{4,6},{5,7},{6,4},{7,5},{8,10},{9,11},{10,... | collective-permute-start | bytes 73736 | tf_op jit(solution)/shard_map/ppermute | solution.py:117
  52.0 1.2 %convolution_convert_fusion = bf16[149,608]{1,0:T(8,128)(2,1)} fusion(s32[149]{0:T(256)S(1)} %iota_add_fusion.1, s32[608]{0:T(1024)S(1)} %get-tuple-element.4, s32[608]{0:T(1024)S(1)} %get-tuple-element.3, f32[152,256]{1,0:T(8,128)S(1)} %sweep.1), kind=kOutput, calls=%fused_computation.11 | convolution fusion | flops 162612640 | bytes 342292 | tf_op jit(solution)/shard_map/dot_general | solution.py:202
  53.3 2.5 %shard_map.130 = bf16[32,19,8,128]{3,2,1,0:T(8,128)(2,1)} custom-call(bf16[19,32,8,256]{3,2,1,0:T(8,128)(2,1)} %bitcast.61), custom_call_target="tpu_custom_call" | custom-call | tf_op jit(solution)/shard_map/pallas_call | solution.py:152
  55.9 0.1 collective-permute-start.5
  56.0 7.1 %all-to-all-start = ((bf16[32,19,8,128]{3,2,1,0:T(8,128)(2,1)}), bf16[32,19,8,128]{3,2,1,0:T(8,128)(2,1)S(1)}, u32[]{:S(2)}, u32[]{:S(2)}) async-start(bf16[32,19,8,128]{3,2,1,0:T(8,128)(2,1)} %shard_map.130), calls=%async_computation | async-start | bytes 2490368 | tf_op jit(solution)/shard_map/all_to_all | solution.py:181
  63.2 0.8 add_select_fusion.2
  63.9 0.1 eq.76
  64.1 0.9 pad_maximum_fusion.2
  64.9 1.4 %collective-permute-start.6 = (f32[96,256]{1,0:T(8,128)S(1)}, f32[96,256]{1,0:T(8,128)S(1)}, u32[]{:S(2)}, u32[]{:S(2)}) collective-permute-start(f32[96,256]{1,0:T(8,128)S(1)} %bitcast.76), channel_id=1, source_target_pairs={{0,64},{1,65},{2,66},{3,67},{4,68},{5,69},{6,70},{7,71},{8,72},{9,... | collective-permute-start | bytes 294920 | tf_op jit(solution)/shard_map/ppermute | solution.py:117
  66.3 2.4 %collective-permute-start.7 = (f32[96,256]{1,0:T(8,128)S(1)}, f32[96,256]{1,0:T(8,128)S(1)}, u32[]{:S(2)}, u32[]{:S(2)}) collective-permute-start(f32[96,256]{1,0:T(8,128)S(1)} %bitcast.77), channel_id=1, source_target_pairs={{0,128},{1,129},{2,130},{3,131},{4,132},{5,133},{6,134},{7,135},{8... | collective-permute-start | bytes 294920 | tf_op jit(solution)/shard_map/ppermute | solution.py:117
  68.8 1.5 %fusion = f32[768,149]{1,0:T(8,128)S(1)} fusion(bf16[149,608]{1,0:T(8,128)(2,1)} %convolution_convert_fusion, s32[768]{0:T(1024)S(1)} %eq.76), kind=kOutput, calls=%fused_computation.3 | convolution fusion | flops 139616256 | bytes 641984 | tf_op jit(solution)/shard_map/dot_general | solution.py:206
  70.4 0.2 copy.21
  70.6 0.2 copy.18
  70.8 3.3 %collective-permute-done.6 = f32[96,256]{1,0:T(8,128)S(1)} collective-permute-done((f32[96,256]{1,0:T(8,128)S(1)}, f32[96,256]{1,0:T(8,128)S(1)}, u32[]{:S(2)}, u32[]{:S(2)}) %collective-permute-start.6) | collective-permute-done | bytes 98336 | tf_op jit(solution)/shard_map/ppermute | solution.py:117
  74.2 5.6 %collective-permute-done.7 = f32[96,256]{1,0:T(8,128)S(1)} collective-permute-done((f32[96,256]{1,0:T(8,128)S(1)}, f32[96,256]{1,0:T(8,128)S(1)}, u32[]{:S(2)}, u32[]{:S(2)}) %collective-permute-start.7) | collective-permute-done | bytes 98336 | tf_op jit(solution)/shard_map/ppermute | solution.py:117
  79.8 1.2 %collective-permute-start.9 = (f32[384,256]{1,0:T(8,128)S(1)}, f32[384,256]{1,0:T(8,128)S(1)}, u32[]{:S(2)}, u32[]{:S(2)}) collective-permute-start(f32[384,256]{1,0:T(8,128)S(1)} %pad_maximum_fusion.1), channel_id=1, source_target_pairs={{0,8},{1,9},{2,10},{3,11},{4,12},{5,13},{6,14},{7,15},{8,0},{9,1},... | collective-permute-start | bytes 1179656 | tf_op jit(solution)/shard_map/ppermute | solution.py:117
  81.1 1.3 %collective-permute-done.9 = f32[384,256]{1,0:T(8,128)S(1)} collective-permute-done((f32[384,256]{1,0:T(8,128)S(1)}, f32[384,256]{1,0:T(8,128)S(1)}, u32[]{:S(2)}, u32[]{:S(2)}) %collective-permute-start.9) | collective-permute-done | bytes 393248 | tf_op jit(solution)/shard_map/ppermute | solution.py:117
  82.4 1.4 %fusion.6 = f32[225,149]{0,1:T(8,128)S(1)} fusion(f32[768,149]{1,0:T(8,128)S(1)} %fusion, f32[768,256]{1,0:T(8,128)S(1)} %constant_dynamic-update-slice_fusion, s32[225]{0:T(256)S(1)} %copy-done.10, s32[149]{0:T(256)S(1)} %copy-done.9), kind=kOutput, calls=%fused_computation.13 | convolution fusion | flops 309066976 | bytes 1379756 | tf_op jit(solution)/shard_map/dot_general | solution.py:219
  83.9 1.6 %fusion.27 = f32[149,1024]{1,0:T(8,128)} fusion(f32[225,1024]{1,0:T(8,128)S(1)} %bitcast.67, f32[225,149]{0,1:T(8,128)S(1)} %fusion.6, f32[225]{0:T(256)S(1)} %copy-done.7), kind=kOutput, calls=%fused_computation.42 | convolution fusion | flops 411988736 | bytes 1666904 | tf_op jit(solution)/shard_map/dot_general | solution.py:235
  85.5 1.3 %fusion.67 = f32[450,149]{1,0:T(8,128)} fusion(f32[450,225]{1,0:T(8,128)S(1)} %copy-done.4, f32[225,149]{0,1:T(8,128)S(1)} %fusion.6), kind=kOutput, calls=%fused_computation.116 | convolution fusion | flops 181035008 | bytes 807300 | tf_op jit(solution)/shard_map/dot_general | solution.py:226
  86.8 2.1 %reshape.152 = f32[15,15,2,149]{3,2,1,0:T(2,128)} reshape(f32[450,149]{1,0:T(8,128)} %fusion.67) | data formatting | bytes 536400 | tf_op jit(solution)/shard_map/reshape | solution.py:227
  88.9 2.3 %subtract_convert_fusion = (bf16[149,1024]{1,0:T(8,128)(2,1)}, bf16[149,1024]{1,0:T(8,128)(2,1)S(1)}) fusion(f32[149,1024]{1,0:T(8,128)} %fusion.27, bf16[149,608]{1,0:T(8,128)(2,1)} %convolution_convert_fusion, bf16[76,8,8,128]{3,2,1,0:T(8,128)(2,1)S(1)} %bitcast.62), kind=kOutput, calls=%fused_computation.18 | convolution fusion | flops 185990144 | bytes 2646976 | tf_op jit(solution)/shard_map/dot_general | solution.py:241
  91.2 0.6 multiply_reduce_fusion
  91.8 3.4 %all-to-all-done = bf16[32,19,8,128]{3,2,1,0:T(8,128)(2,1)S(1)} async-done(((bf16[32,19,8,128]{3,2,1,0:T(8,128)(2,1)}), bf16[32,19,8,128]{3,2,1,0:T(8,128)(2,1)S(1)}, u32[]{:S(2)}, u32[]{:S(2)}) %all-to-all-start) | async-done | bytes 1245216 | tf_op jit(solution)/shard_map/all_to_all | solution.py:181
  95.1 1.3 %fusion.3 = f32[149,1024]{1,0:T(8,128)S(1)} fusion(bf16[149,608]{1,0:T(8,128)(2,1)} %convolution_convert_fusion, bf16[76,8,8,128]{3,2,1,0:T(8,128)(2,1)S(1)} %bitcast.64), kind=kOutput, calls=%fused_computation.7 | convolution fusion | flops 185532416 | bytes 2036672 | tf_op jit(solution)/shard_map/dot_general | solution.py:241
  96.5 0.6 multiply_reduce_fusion.1
  97.1 0.3 copy-done.2
  97.4 0.7 fusion.5
  98.2 0.1 copy-done.3
  98.5 0.6 pad_maximum_fusion.4
  99.1 0.9 pad_maximum_fusion
  (57 shorter events, 0.6 us)
Async XLA Ops:
  4.2 16.4 %collective-permute-start = (f32[24,256]{1,0:T(8,128)S(1)}, f32[24,256]{1,0:T(8,128)S(1)}, u32[]{:S(2)}, u32[]{:S(2)}) collective-permute-start(f32[24,256]{1,0:T(8,128)S(1)} %pad.9), channel_id=1, source_target_pairs={{0,2},{1,3},{2,0},{3,1},{4,6},{5,7},{6,4},{7,5},{8,10},{9,11},{10,... | collective-permute-start | bytes 73736 | tf_op jit(solution)/shard_map/ppermute | solution.py:117
  8.9 9.7 %copy-start.6 = (s32[608,2]{0,1:T(2,128)S(1)}, s32[608,2]{0,1:T(2,128)}, u32[]{:S(2)}) copy-start(s32[608,2]{0,1:T(2,128)} %param.12) | copy-start | bytes 14596
  8.9 47.1 %all-to-all-start.1 = ((bf16[32,19,8,128]{3,2,1,0:T(8,128)(2,1)}), bf16[32,19,8,128]{3,2,1,0:T(8,128)(2,1)S(1)}, u32[]{:S(2)}, u32[]{:S(2)}) async-start(bf16[32,19,8,128]{3,2,1,0:T(8,128)(2,1)} %shard_map.131), calls=%async_computation.1 | async-start | bytes 2490368 | tf_op jit(solution)/shard_map/all_to_all | solution.py:181
  18.6 33.5 %copy-start.11 = (s32[149]{0:T(256)}, s32[149]{0:T(256)S(1)}, u32[]{:S(2)}) copy-start(s32[149]{0:T(256)S(1)} %iota_add_fusion.1) | copy-start | bytes 1792
  20.7 4.6 %collective-permute-start.1 = (f32[24,256]{1,0:T(8,128)S(1)}, f32[24,256]{1,0:T(8,128)S(1)}, u32[]{:S(2)}, u32[]{:S(2)}) collective-permute-start(f32[24,256]{1,0:T(8,128)S(1)} %pad_add_fusion), channel_id=1, source_target_pairs={{0,4},{1,5},{2,6},{3,7},{4,0},{5,1},{6,2},{7,3},{8,12},{9,13},{10,... | collective-permute-start | bytes 73736 | tf_op jit(solution)/shard_map/ppermute | solution.py:117
  25.3 14.9 %collective-permute-start.2 = (f32[24,256]{1,0:T(8,128)S(1)}, f32[24,256]{1,0:T(8,128)S(1)}, u32[]{:S(2)}, u32[]{:S(2)}) collective-permute-start(f32[24,256]{1,0:T(8,128)S(1)} %add.111), channel_id=1, source_target_pairs={{0,0},{1,1},{2,18},{3,19},{4,36},{5,37},{6,54},{7,55},{8,8},{9,9},... | collective-permute-start | bytes 73736 | tf_op jit(solution)/shard_map/ppermute | solution.py:117
  25.9 18.7 %collective-permute-start.3 = (f32[24,256]{1,0:T(8,128)S(1)}, f32[24,256]{1,0:T(8,128)S(1)}, u32[]{:S(2)}, u32[]{:S(2)}) collective-permute-start(f32[24,256]{1,0:T(8,128)S(1)} %add.111), channel_id=1, source_target_pairs={{0,1},{1,0},{2,19},{3,18},{4,37},{5,36},{6,55},{7,54},{8,9},{9,8},... | collective-permute-start | bytes 73736 | tf_op jit(solution)/shard_map/ppermute | solution.py:117
  44.6 11.3 %collective-permute-start.4 = (f32[24,256]{1,0:T(8,128)S(1)}, f32[24,256]{1,0:T(8,128)S(1)}, u32[]{:S(2)}, u32[]{:S(2)}) collective-permute-start(f32[24,256]{1,0:T(8,128)S(1)} %add.112), channel_id=1, source_target_pairs={{0,2},{1,3},{2,0},{3,1},{4,6},{5,7},{6,4},{7,5},{8,10},{9,11},{10,... | collective-permute-start | bytes 73736 | tf_op jit(solution)/shard_map/ppermute | solution.py:117
  55.9 7.3 %copy-start.5 = (s32[2,4,4,24]{3,2,1,0:T(4,128)S(1)}, s32[2,4,4,24]{3,2,1,0:T(4,128)}, u32[]{:S(2)}) copy-start(s32[2,4,4,24]{3,2,1,0:T(4,128)} %constant.142.clone) | copy-start | bytes 9220
  55.9 7.3 %copy-start.8 = (pred[2,4,4,24]{3,2,1,0:T(4,128)(4,1)S(1)}, pred[2,4,4,24]{3,2,1,0:T(4,128)(4,1)}, u32[]{:S(2)}) copy-start(pred[2,4,4,24]{3,2,1,0:T(4,128)(4,1)} %constant.146.clone) | copy-start | bytes 2308
  55.9 8.2 %collective-permute-start.5 = (f32[2,24,256]{2,1,0:T(8,128)S(1)}, f32[2,24,256]{2,1,0:T(8,128)}, u32[]{:S(2)}, u32[]{:S(2)}) collective-permute-start(f32[2,24,256]{2,1,0:T(8,128)S(1)} %pad_maximum_fusion.3), channel_id=1, source_target_pairs={{0,4},{1,5},{2,6},{3,7},{4,0},{5,1},{6,2},{7,3},{8,12},{9,13},{10,... | collective-permute-start | bytes 147464 | tf_op jit(solution)/shard_map/ppermute | solution.py:117
  56.0 39.1 %all-to-all-start = ((bf16[32,19,8,128]{3,2,1,0:T(8,128)(2,1)}), bf16[32,19,8,128]{3,2,1,0:T(8,128)(2,1)S(1)}, u32[]{:S(2)}, u32[]{:S(2)}) async-start(bf16[32,19,8,128]{3,2,1,0:T(8,128)(2,1)} %shard_map.130), calls=%async_computation | async-start | bytes 2490368 | tf_op jit(solution)/shard_map/all_to_all | solution.py:181
  64.0 6.2 %copy-start = (f32[15,15,8,128]{3,2,1,0:T(8,128)S(1)}, f32[15,15,8,128]{3,2,1,0:T(8,128)}, u32[]{:S(2)}) copy-start(f32[15,15,8,128]{3,2,1,0:T(8,128)} %get-tuple-element.8) | copy-start | bytes 2764804
  64.9 9.2 %collective-permute-start.6 = (f32[96,256]{1,0:T(8,128)S(1)}, f32[96,256]{1,0:T(8,128)S(1)}, u32[]{:S(2)}, u32[]{:S(2)}) collective-permute-start(f32[96,256]{1,0:T(8,128)S(1)} %bitcast.76), channel_id=1, source_target_pairs={{0,64},{1,65},{2,66},{3,67},{4,68},{5,69},{6,70},{7,71},{8,72},{9,... | collective-permute-start | bytes 294920 | tf_op jit(solution)/shard_map/ppermute | solution.py:117
  66.3 13.4 %collective-permute-start.7 = (f32[96,256]{1,0:T(8,128)S(1)}, f32[96,256]{1,0:T(8,128)S(1)}, u32[]{:S(2)}, u32[]{:S(2)}) collective-permute-start(f32[96,256]{1,0:T(8,128)S(1)} %bitcast.77), channel_id=1, source_target_pairs={{0,128},{1,129},{2,130},{3,131},{4,132},{5,133},{6,134},{7,135},{8... | collective-permute-start | bytes 294920 | tf_op jit(solution)/shard_map/ppermute | solution.py:117
  68.7 11.0 %collective-permute-start.8 = (f32[96,256]{1,0:T(8,128)S(1)}, f32[96,256]{1,0:T(8,128)S(1)}, u32[]{:S(2)}, u32[]{:S(2)}) collective-permute-start(f32[96,256]{1,0:T(8,128)S(1)} %bitcast.78), channel_id=1, source_target_pairs={{0,192},{1,193},{2,194},{3,195},{4,196},{5,197},{6,198},{7,199},{8... | collective-permute-start | bytes 294920 | tf_op jit(solution)/shard_map/ppermute | solution.py:117
  70.8 11.6 %copy-start.9 = (s32[149]{0:T(256)S(1)}, s32[149]{0:T(256)}, u32[]{:S(2)}) copy-start(s32[149]{0:T(256)} %param.13) | copy-start | bytes 1792
  70.8 11.6 %copy-start.10 = (s32[225]{0:T(256)S(1)}, s32[225]{0:T(256)}, u32[]{:S(2)}) copy-start(s32[225]{0:T(256)} %constant.147.clone) | copy-start | bytes 2704
  79.8 2.6 %collective-permute-start.9 = (f32[384,256]{1,0:T(8,128)S(1)}, f32[384,256]{1,0:T(8,128)S(1)}, u32[]{:S(2)}, u32[]{:S(2)}) collective-permute-start(f32[384,256]{1,0:T(8,128)S(1)} %pad_maximum_fusion.1), channel_id=1, source_target_pairs={{0,8},{1,9},{2,10},{3,11},{4,12},{5,13},{6,14},{7,15},{8,0},{9,1},... | collective-permute-start | bytes 1179656 | tf_op jit(solution)/shard_map/ppermute | solution.py:117
  81.1 2.8 %copy-start.7 = (f32[225]{0:T(256)S(1)}, f32[225]{0:T(256)}, u32[]{:S(2)}) copy-start(f32[225]{0:T(256)} %constant.149.clone) | copy-start | bytes 2704
  83.8 1.6 %copy-start.1 = (f32[225,149]{0,1:T(8,128)}, f32[225,149]{0,1:T(8,128)S(1)}, u32[]{:S(2)}) copy-start(f32[225,149]{0,1:T(8,128)S(1)} %fusion.6) | copy-start | bytes 402304
  83.9 1.6 %copy-start.4 = (f32[450,225]{1,0:T(8,128)S(1)}, f32[450,225]{1,0:T(8,128)}, u32[]{:S(2)}) copy-start(f32[450,225]{1,0:T(8,128)} %constant.148.clone) | copy-start | bytes 1215004
  88.9 2.3 %copy-start.12 = (s32[149]{0:T(256)S(1)}, s32[149]{0:T(256)}, u32[]{:S(2)}) copy-start(s32[149]{0:T(256)} %copy-done.11) | copy-start | bytes 1792
  96.5 0.9 copy-start.2
  97.4 1.0 copy-start.3
